TPU v7x, 32 devices: a whole 2x2x4 slice. The times are simulated.
32 devices in a mesh: seq: 16 (over z, x, core), head: 2 (over y).
Axes of the slice: x: 2, y: 2, z: 4, core: 2. Of those that a mesh axis runs over, the one named last changes fastest.
Arguments:
- queries: bfloat16 [4096, 4096], P(('seq', 'head')), may hold values from -5 to 5
- key_rows: bfloat16 [4096, 4096], P(('seq', 'head')), may hold values from -5 to 5
- value_rows: bfloat16 [4096, 4096], P(('seq', 'head')), may hold values from -6 to 6
- step_rates: bfloat16 [4096, 8], P(('seq', 'head')), may hold values from 0.1 to 9
- w_gate: bfloat16 [512, 8, 512], P('seq', 'head'), may hold values from -0.25 to 0.25
- w_up: bfloat16 [512, 8, 512], P('seq', 'head'), may hold values from -0.25 to 0.25
- w_down: bfloat16 [512, 8, 512], P('seq', 'head'), may hold values from -0.25 to 0.25
Outputs:
- block_out: bfloat16 [4096, 4096], P(('seq', 'head'))
All inputs are finite; a program needn't handle non-finite values.
Results may differ from a plain program's by a relative error of at most 0.012.
Values may be sent and summed in bfloat16 or wider, within the bound.
No kernel may reach another device: no remote copies, remote signals or barrier semaphores. Data moves between devices by JAX's collectives and lax.ppermute only.
A program may use at most 128 MiB of HBM per device.

v0:
```python
import math

import jax
import jax.numpy as jnp
from jax import lax
from jax.sharding import PartitionSpec as P

ATT_HEADS = 32
HEAD_DIM = 128
HEADS = 8
HS = 512
WINDOW = 64


STEP_SIZE = 0.05
NORM_EPS = 1e-06


def from_behind(value, axis, by):
    count = lax.axis_size(axis)
    pairs = [(i, i + by) for i in range(count) if 0 <= i + by < count]
    return lax.ppermute(value, axis, pairs)


def local_attention(block_queries, key_span, value_span, start_pos):
    row_count = block_queries.shape[0]
    span_count = key_span.shape[0]
    query_heads = block_queries.reshape(row_count, ATT_HEADS, HEAD_DIM)
    key_heads = key_span.reshape(span_count, ATT_HEADS, HEAD_DIM)
    value_heads = value_span.reshape(span_count, ATT_HEADS, HEAD_DIM)
    scores = jnp.einsum(
        "qhd,khd->hqk", query_heads, key_heads, preferred_element_type=jnp.float32
    ) * (1.0 / math.sqrt(HEAD_DIM))
    query_pos = start_pos + lax.iota(jnp.int32, row_count)
    key_pos = start_pos - WINDOW + lax.iota(jnp.int32, span_count)
    allowed = (
        (key_pos[None, :] >= 0)
        & (key_pos[None, :] <= query_pos[:, None])
        & (key_pos[None, :] > query_pos[:, None] - WINDOW)
    )
    masked = jnp.where(allowed[None], scores, -1e30)
    maximum = jnp.max(masked, axis=2, keepdims=True)
    exp_scores = jnp.where(allowed[None], jnp.exp(masked - maximum), 0.0)
    totals = jnp.sum(exp_scores, axis=2)
    weights = exp_scores.astype(jnp.bfloat16)
    mixed = jnp.einsum("hqk,khd->qhd", weights, value_heads, preferred_element_type=jnp.float32)
    return (mixed / jnp.transpose(totals)[:, :, None]).reshape(row_count, ATT_HEADS * HEAD_DIM)


def rms_heads(tensor):
    blocks = tensor.astype(jnp.float32).reshape(tensor.shape[0], HEADS, HS)
    normed = blocks * lax.rsqrt(jnp.mean(blocks * blocks, axis=2, keepdims=True) + NORM_EPS)
    return normed.astype(jnp.bfloat16).reshape(tensor.shape[0], HEADS * HS)


def weight_columns(matrix, head, which):
    first = (3 * head + which) * HS
    return matrix[:, first : first + HS]


def head_columns(matrix, head):
    return matrix[:, head * HS : (head + 1) * HS]


def renorm(old_rows, grad_rows, norm_scale, local_heads):
    pieces = []
    for head in range(local_heads):
        for which in range(3):
            previous = weight_columns(old_rows, head, which).astype(jnp.float32)
            stepped = previous - STEP_SIZE * norm_scale[head] * weight_columns(
                grad_rows, head, which
            )
            factor = jnp.sqrt(jnp.mean(previous * previous, axis=-1, keepdims=True)) * lax.rsqrt(
                jnp.mean(stepped * stepped, axis=-1, keepdims=True) + NORM_EPS
            )
            pieces.append((stepped * factor).astype(jnp.bfloat16))
    return jnp.concatenate(pieces, 1)


def head_squares(grad_rows, local_heads):
    sums = []
    for head in range(local_heads):
        segment = grad_rows[:, 3 * head * HS : 3 * (head + 1) * HS]
        sums.append(jnp.sum(segment * segment))
    return jnp.stack(sums)


def shards(queries, key_rows, value_rows, step_rates, w_gate, w_up, w_down):
    row_count = queries.shape[0]
    local_heads = w_gate.shape[1]
    start_pos = lax.axis_index(("seq", "head")) * row_count
    tail_rows = jnp.stack([key_rows[row_count - WINDOW :], value_rows[row_count - WINDOW :]])
    before = from_behind(tail_rows, ("seq", "head"), 1)
    own_old = jnp.concatenate([w_gate, w_up, w_down], 2).reshape(
        w_gate.shape[0], local_heads * 3 * HS
    )
    stacked_old = lax.all_gather(own_old, "seq", axis=0, tiled=True)
    query_norm = rms_heads(queries)
    key_norm = rms_heads(key_rows)
    head_query, head_key, head_value, head_rate = (
        lax.all_to_all(query_norm, "head", split_axis=1, concat_axis=0, tiled=True),
        lax.all_to_all(key_norm, "head", split_axis=1, concat_axis=0, tiled=True),
        lax.all_to_all(value_rows, "head", split_axis=1, concat_axis=0, tiled=True),
        lax.all_to_all(step_rates, "head", split_axis=1, concat_axis=0, tiled=True),
    )
    attended = local_attention(
        queries,
        jnp.concatenate([before[0], key_rows], 0),
        jnp.concatenate([before[1], value_rows], 0),
        start_pos,
    )
    forward = []
    for head in range(local_heads):
        key_head = head_columns(head_key, head)
        gate_pre = jnp.dot(
            key_head, weight_columns(stacked_old, head, 0), preferred_element_type=jnp.float32
        )
        up_pre = jnp.dot(
            key_head, weight_columns(stacked_old, head, 1), preferred_element_type=jnp.float32
        )
        sigma_gate = jax.nn.sigmoid(gate_pre)
        silu_gate = gate_pre * sigma_gate
        hidden = (silu_gate * up_pre).astype(jnp.bfloat16)
        target = (
            -head_rate[:, head].astype(jnp.float32)[:, None]
            * head_columns(head_value, head).astype(jnp.float32)
        ).astype(jnp.bfloat16)
        hidden_grad = jnp.einsum(
            "to,mo->tm",
            target,
            weight_columns(stacked_old, head, 2),
            preferred_element_type=jnp.float32,
        )
        gate_grad = (
            hidden_grad * up_pre * sigma_gate * (1.0 + gate_pre * (1.0 - sigma_gate))
        ).astype(jnp.bfloat16)
        up_grad = (hidden_grad * silu_gate).astype(jnp.bfloat16)
        forward.append((key_head, hidden, target, gate_grad, up_grad))

    def grad_rows(start_row, count_rows):
        pieces = []
        for key_head, hidden, target, gate_grad, up_grad in forward:
            pieces.append(
                jnp.einsum("ti,tm->im", key_head, gate_grad, preferred_element_type=jnp.float32)
            )
            pieces.append(
                jnp.einsum("ti,tm->im", key_head, up_grad, preferred_element_type=jnp.float32)
            )
            pieces.append(
                jnp.einsum("tm,to->mo", hidden, target, preferred_element_type=jnp.float32)
            )
        return jnp.concatenate(pieces, 1)

    summed = lax.psum(grad_rows(0, HS), "seq")
    norm_scale = lax.rsqrt(head_squares(summed, local_heads) / (3 * HS * HS) + NORM_EPS)
    updated = renorm(stacked_old, summed, norm_scale, local_heads)
    outputs = []
    for head in range(local_heads):
        query_head = head_columns(head_query, head)
        query_gate = jnp.dot(
            query_head, weight_columns(updated, head, 0), preferred_element_type=jnp.float32
        )
        query_up = jnp.dot(
            query_head, weight_columns(updated, head, 1), preferred_element_type=jnp.float32
        )
        query_hidden = (query_gate * jax.nn.sigmoid(query_gate) * query_up).astype(jnp.bfloat16)
        outputs.append(
            jnp.dot(
                query_hidden, weight_columns(updated, head, 2), preferred_element_type=jnp.float32
            ).astype(jnp.bfloat16)
        )
    fast_out = jnp.concatenate(outputs, 1)
    returned = lax.all_to_all(fast_out, "head", split_axis=0, concat_axis=1, tiled=True)
    return (attended + returned.astype(jnp.float32)).astype(jnp.bfloat16)


def solution(mesh):
    placed = (
        P(("seq", "head"), None),
        P(("seq", "head"), None),
        P(("seq", "head"), None),
        P(("seq", "head"), None),
        P("seq", "head", None),
        P("seq", "head", None),
        P("seq", "head", None),
    )
    return jax.shard_map(
        shards, mesh=mesh, in_specs=placed, out_specs=P(("seq", "head"), None), check_vma=False
    )
```

profile of v0, /device:TPU:0, one launch (start us, length us, event | category | flops | bytes accessed | tf_op | source)
XLA Modules:
  0.0 401.6 jit_solution(13907573883006215831)
XLA Ops:
  8.7 4.3 %all-to-all-start.2 = ((bf16[128,2,4]{0,2,1:T(4,128)(2,1)}), bf16[128,2,4]{0,2,1:T(4,128)(2,1)S(1)}, u32[]{:S(2)}, u32[]{:S(2)}) async-start(bf16[128,2,4]{0,2,1:T(4,128)(2,1)} %bitcast.122), calls=%async_computation.2 | async-start | bytes 4096 | tf_op jit(solution)/shard_map/all_to_all | solution.py:104
  13.0 1.6 copy.41
  16.7 3.6 all-to-all-start.1
  21.7 12.0 %all-to-all-done.1 = bf16[128,2,2048]{0,2,1:T(8,128)(2,1)S(1)} async-done(((bf16[128,2,2048]{0,2,1:T(8,128)(2,1)}), bf16[128,2,2048]{0,2,1:T(8,128)(2,1)S(1)}, u32[]{:S(2)}, u32[]{:S(2)}) %all-to-all-start.1) | async-done | bytes 1048608 | tf_op jit(solution)/shard_map/all_to_all | solution.py:102
  33.7 4.4 %all-to-all-start.3 = ((bf16[128,2,2048]{0,2,1:T(8,128)(2,1)}), bf16[128,2,2048]{0,2,1:T(8,128)(2,1)}, u32[]{:S(2)}, u32[]{:S(2)}) async-start(bf16[128,2,2048]{0,2,1:T(8,128)(2,1)} %bitcast.22), calls=%async_computation.3 | async-start | bytes 2097152 | tf_op jit(solution)/shard_map/all_to_all | solution.py:103
  38.7 12.1 %all-to-all-done.3 = bf16[128,2,2048]{0,2,1:T(8,128)(2,1)} async-done(((bf16[128,2,2048]{0,2,1:T(8,128)(2,1)}), bf16[128,2,2048]{0,2,1:T(8,128)(2,1)}, u32[]{:S(2)}, u32[]{:S(2)}) %all-to-all-start.3) | async-done | bytes 1048608 | tf_op jit(solution)/shard_map/all_to_all | solution.py:103
  50.8 1.5 copy.51
  52.2 21.5 %all-gather.2.cloned.1.call-done = bf16[512,6144]{1,0:T(8,128)(2,1)} async-done(((bf16[32,6144]{1,0:T(8,128)(2,1)}), bf16[512,6144]{1,0:T(8,128)(2,1)}) %all-gather.2.cloned.1.call-update) | async-done | bytes 6291472 | tf_op jit(solution)/shard_map/all_gather | solution.py:97
  75.1 1.5 fusion.135
  76.6 1.4 fusion.145
  78.0 1.5 convolution_dynamic-update-slice_fusion.11
  80.9 1.5 convolution_dynamic-update-slice_fusion.9
  83.3 1.4 convolution_dynamic-update-slice_fusion.8
  84.7 1.4 convolution_dynamic-update-slice_fusion.7
  86.1 1.5 convolution_dynamic-update-slice_fusion.6
  88.6 1.4 convolution_dynamic-update-slice_fusion.5
  91.4 1.5 convolution_dynamic-update-slice_fusion.3
  93.8 1.5 convolution_dynamic-update-slice_fusion.2
  95.3 1.4 convolution_dynamic-update-slice_fusion.1
  96.7 1.5 convolution_dynamic-update-slice_fusion
  101.6 4.4 %collective-permute-start = (bf16[2,64,4096]{2,1,0:T(8,128)(2,1)}, bf16[2,64,4096]{2,1,0:T(8,128)(2,1)}, u32[]{:S(2)}, u32[]{:S(2)}) collective-permute-start(bf16[2,64,4096]{2,1,0:T(8,128)(2,1)} %pad_maximum_fusion), channel_id=1, source_target_pairs={{0,1},{1,2},{2,3},{3,4},{4,5},{5,6},{6,7},{7,8},{8,9},{9,10},{10,1... | collective-permute-start | bytes 3145736 | tf_op jit(solution)/shard_map/ppermute | solution.py:22
  108.1 4.6 %all-to-all-start = ((bf16[128,2,2048]{0,2,1:T(8,128)(2,1)}), bf16[128,2,2048]{0,2,1:T(8,128)(2,1)}, u32[]{:S(2)}, u32[]{:S(2)}) async-start(bf16[128,2,2048]{0,2,1:T(8,128)(2,1)} %bitcast.10), calls=%async_computation | async-start | bytes 2097152 | tf_op jit(solution)/shard_map/all_to_all | solution.py:101
  114.0 2.4 copy.40
  116.6 22.8 %all-to-all-done = bf16[128,2,2048]{0,2,1:T(8,128)(2,1)} async-done(((bf16[128,2,2048]{0,2,1:T(8,128)(2,1)}), bf16[128,2,2048]{0,2,1:T(8,128)(2,1)}, u32[]{:S(2)}, u32[]{:S(2)}) %all-to-all-start) | async-done | bytes 1048608 | tf_op jit(solution)/shard_map/all_to_all | solution.py:101
  139.3 1.5 copy.46
  140.8 2.2 slice_bitcast_fusion
  143.3 4.3 %fusion.11 = f32[32,192,128]{2,1,0:T(8,128)} fusion(bf16[128,32,128]{2,0,1:T(8,128)(2,1)} %copy.43, bf16[64,32,128]{2,0,1:T(8,128)(2,1)S(1)} %copy.42, bf16[128,4096]{1,0:T(8,128)(2,1)} %param.7), kind=kOutput, calls=%fused_computation.26 | convolution fusion | flops 204472320 | bytes 5767168 | tf_op jit(solution)/shard_map/qhd,khd->hqk/dot_general | solution.py:31
  147.6 2.7 fusion.187
  151.7 2.1 copy.66
  153.8 2.1 copy.71
  155.8 2.1 copy.72
  159.2 2.1 copy.74
  163.7 2.1 copy.67
  165.8 2.1 copy.68
  170.1 170.3 %all-reduce.2.cloned.1.call-done = f32[512,6144]{0,1:T(8,128)} async-done(((f32[512,6144]{0,1:T(8,128)}), f32[512,6144]{0,1:T(8,128)}) %all-reduce.2.cloned.1.call-update) | async-done | bytes 12582928 | tf_op jit(solution)/shard_map/psum | solution.py:154
  340.4 6.3 %fusion.4 = (f32[]{:T(128)}, f32[]{:T(128)}, f32[]{:T(128)}, f32[]{:T(128)}) fusion(f32[512,6144]{0,1:T(8,128)} %all-reduce.2.cloned.1.call-done), kind=kLoop, calls=%fused_computation.8 | loop fusion | flops 6291452 | bytes 12582928 | tf_op jit(solution)/shard_map/reduce_sum | solution.py:84
  346.7 3.4 fusion.154
  353.3 3.5 multiply_reduce_fusion.11
  362.8 2.6 convolution_convert_fusion.3
  365.4 3.4 convolution_convert_fusion.2
  368.8 3.1 convolution_convert_fusion.1
  371.9 2.4 convolution_convert_fusion
  374.2 2.1 pad_maximum_fusion.1
  376.4 3.9 all-to-all-start.4
  380.3 4.3 %fusion.189 = (f32[32,128]{1,0:T(8,128)S(1)}, bf16[32,128,192]{1,2,0:T(8,128)(2,1)S(1)}) fusion(f32[32,192,128]{2,1,0:T(8,128)} %fusion.11, pred[128,192]{0,1:T(8,128)(4,1)S(1)} %compare_and_fusion), kind=kOutput, calls=%fused_computation.315 | output fusion | flops 6291647 | bytes 4759552 | tf_op jit(solution)/shard_map/sub | solution.py:43
  384.9 2.1 bitcast_divide_fusion
  387.1 1.9 copy.64
  389.0 4.0 %all-to-all-done.4 = bf16[2,128,2048]{2,1,0:T(8,128)(2,1)S(1)} async-done(((bf16[2,128,2048]{2,1,0:T(8,128)(2,1)}), bf16[2,128,2048]{2,1,0:T(8,128)(2,1)S(1)}, u32[]{:S(2)}, u32[]{:S(2)}) %all-to-all-start.4) | async-done | bytes 1048608 | tf_op jit(solution)/shard_map/all_to_all | solution.py:173
  (106 shorter events, 36.1 us)
Async XLA Ops:
  6.5 13.8 %copy-start.2 = (bf16[128,4096]{1,0:T(8,128)(2,1)S(1)}, bf16[128,4096]{1,0:T(8,128)(2,1)}, u32[]{:S(2)}) copy-start(bf16[128,4096]{1,0:T(8,128)(2,1)} %param.9) | copy-start | bytes 3145732
  6.5 67.2 %all-gather.2.cloned.1.call-start = ((), (), s32[]{:S(2)}) async-start(), calls=%async_computation.5 | async-start | bytes 6684672 | tf_op jit(solution)/shard_map/all_gather | solution.py:97
  8.7 8.1 %all-to-all-start.2 = ((bf16[128,2,4]{0,2,1:T(4,128)(2,1)}), bf16[128,2,4]{0,2,1:T(4,128)(2,1)S(1)}, u32[]{:S(2)}, u32[]{:S(2)}) async-start(bf16[128,2,4]{0,2,1:T(4,128)(2,1)} %bitcast.122), calls=%async_computation.2 | async-start | bytes 4096 | tf_op jit(solution)/shard_map/all_to_all | solution.py:104
  16.7 16.9 %all-to-all-start.1 = ((bf16[128,2,2048]{0,2,1:T(8,128)(2,1)}), bf16[128,2,2048]{0,2,1:T(8,128)(2,1)S(1)}, u32[]{:S(2)}, u32[]{:S(2)}) async-start(bf16[128,2,2048]{0,2,1:T(8,128)(2,1)} %bitcast.15), calls=%async_computation.1 | async-start | bytes 2097152 | tf_op jit(solution)/shard_map/all_to_all | solution.py:102
  33.7 17.1 %all-to-all-start.3 = ((bf16[128,2,2048]{0,2,1:T(8,128)(2,1)}), bf16[128,2,2048]{0,2,1:T(8,128)(2,1)}, u32[]{:S(2)}, u32[]{:S(2)}) async-start(bf16[128,2,2048]{0,2,1:T(8,128)(2,1)} %bitcast.22), calls=%async_computation.3 | async-start | bytes 2097152 | tf_op jit(solution)/shard_map/all_to_all | solution.py:103
  38.1 302.3 %all-reduce.2.cloned.1.call-start = ((), (), s32[]{:S(2)}) async-start(), calls=%async_computation.6 | async-start | bytes 25165824 | tf_op jit(solution)/shard_map/psum | solution.py:154
  75.1 7.2 %slice-start = ((s8[6291456]{0:T(1024)(128)(4,1)}), s8[4194304]{0:T(1024)(128)(4,1)S(1)}, s32[]{:S(2)}) async-start(s8[6291456]{0:T(1024)(128)(4,1)} %bitcast.77), calls=%async_computation.7 | async-start | bytes 8388608
  78.0 4.3 %slice-start.1 = ((s8[6291456]{0:T(1024)(128)(4,1)}), s8[2097152]{0:T(1024)(128)(4,1)S(1)}, s32[]{:S(2)}) async-start(s8[6291456]{0:T(1024)(128)(4,1)} %bitcast.77), calls=%async_computation.8 | async-start | bytes 4194304
  98.1 1.2 copy-start.3
  98.1 7.8 %copy-start.1 = (bf16[128,4096]{1,0:T(8,128)(2,1)S(1)}, bf16[128,4096]{1,0:T(8,128)(2,1)}, u32[]{:S(2)}) copy-start(bf16[128,4096]{1,0:T(8,128)(2,1)} %param.7) | copy-start | bytes 3145732
  101.6 39.2 %collective-permute-start = (bf16[2,64,4096]{2,1,0:T(8,128)(2,1)}, bf16[2,64,4096]{2,1,0:T(8,128)(2,1)}, u32[]{:S(2)}, u32[]{:S(2)}) collective-permute-start(bf16[2,64,4096]{2,1,0:T(8,128)(2,1)} %pad_maximum_fusion), channel_id=1, source_target_pairs={{0,1},{1,2},{2,3},{3,4},{4,5},{5,6},{6,7},{7,8},{8,9},{9,10},{10,1... | collective-permute-start | bytes 3145736 | tf_op jit(solution)/shard_map/ppermute | solution.py:22
  108.1 31.3 %all-to-all-start = ((bf16[128,2,2048]{0,2,1:T(8,128)(2,1)}), bf16[128,2,2048]{0,2,1:T(8,128)(2,1)}, u32[]{:S(2)}, u32[]{:S(2)}) async-start(bf16[128,2,2048]{0,2,1:T(8,128)(2,1)} %bitcast.10), calls=%async_computation | async-start | bytes 2097152 | tf_op jit(solution)/shard_map/all_to_all | solution.py:101
  114.0 33.7 %slice-start.2 = ((s8[6291456]{0:T(1024)(128)(4,1)}), s8[2097152]{0:T(1024)(128)(4,1)S(1)}, s32[]{:S(2)}) async-start(s8[6291456]{0:T(1024)(128)(4,1)} %bitcast.79), calls=%async_computation.9 | async-start | bytes 4194304
  143.0 4.7 %slice-start.3 = ((s8[6291456]{0:T(1024)(128)(4,1)}), s8[4194304]{0:T(1024)(128)(4,1)S(1)}, s32[]{:S(2)}) async-start(s8[6291456]{0:T(1024)(128)(4,1)} %bitcast.79), calls=%async_computation.10 | async-start | bytes 8388608
  150.4 10.9 %copy-start.9 = (bf16[512,512]{1,0:T(8,128)(2,1)S(1)}, bf16[512,512]{1,0:T(8,128)(2,1)}, u32[]{:S(2)}) copy-start(bf16[512,512]{1,0:T(8,128)(2,1)} %get-tuple-element.34) | copy-start | bytes 1572868
  150.4 17.4 %copy-start.8 = (bf16[512,512]{1,0:T(8,128)(2,1)S(1)}, bf16[512,512]{1,0:T(8,128)(2,1)}, u32[]{:S(2)}) copy-start(bf16[512,512]{1,0:T(8,128)(2,1)} %get-tuple-element.39) | copy-start | bytes 1572868
  340.4 12.9 %copy-start = (f32[512,6144]{0,1:T(8,128)S(1)}, f32[512,6144]{0,1:T(8,128)}, u32[]{:S(2)}) copy-start(f32[512,6144]{0,1:T(8,128)} %all-reduce.2.cloned.1.call-done) | copy-start | bytes 37748740
  353.3 3.5 copy-start.11
  353.3 3.5 copy-start.12
  353.3 3.5 copy-start.13
  359.2 3.6 copy-start.15
  362.8 6.1 %copy-start.6 = (bf16[512,512]{0,1:T(8,128)(2,1)S(1)}, bf16[512,512]{0,1:T(8,128)(2,1)}, u32[]{:S(2)}) copy-start(bf16[512,512]{0,1:T(8,128)(2,1)} %copy.71) | copy-start | bytes 1572868
  362.8 6.1 %copy-start.7 = (bf16[512,512]{0,1:T(8,128)(2,1)S(1)}, bf16[512,512]{0,1:T(8,128)(2,1)}, u32[]{:S(2)}) copy-start(bf16[512,512]{0,1:T(8,128)(2,1)} %copy.72) | copy-start | bytes 1572868
  365.3 6.5 %copy-start.4 = (bf16[512,512]{0,1:T(8,128)(2,1)S(1)}, bf16[512,512]{0,1:T(8,128)(2,1)}, u32[]{:S(2)}) copy-start(bf16[512,512]{0,1:T(8,128)(2,1)} %copy.74) | copy-start | bytes 1572868
  365.4 6.5 %copy-start.5 = (bf16[512,512]{0,1:T(8,128)(2,1)S(1)}, bf16[512,512]{0,1:T(8,128)(2,1)}, u32[]{:S(2)}) copy-start(bf16[512,512]{0,1:T(8,128)(2,1)} %copy.75) | copy-start | bytes 1572868
  376.4 8.2 %copy-start.10 = (bf16[8,8,32,128]{3,1,2,0:T(8,128)(2,1)S(1)}, bf16[8,8,32,128]{3,1,2,0:T(8,128)(2,1)}, u32[]{:S(2)}) copy-start(bf16[8,8,32,128]{3,1,2,0:T(8,128)(2,1)} %get-tuple-element.46) | copy-start | bytes 1572868
  376.4 16.7 %all-to-all-start.4 = ((bf16[2,128,2048]{2,1,0:T(8,128)(2,1)}), bf16[2,128,2048]{2,1,0:T(8,128)(2,1)S(1)}, u32[]{:S(2)}, u32[]{:S(2)}) async-start(bf16[2,128,2048]{2,1,0:T(8,128)(2,1)} %bitcast.37), calls=%async_computation.4 | async-start | bytes 2097152 | tf_op jit(solution)/shard_map/all_to_all | solution.py:173
  380.3 4.6 %copy-start.14 = (bf16[128,32,128]{2,0,1:T(8,128)(2,1)S(1)}, bf16[128,32,128]{2,0,1:T(8,128)(2,1)}, u32[]{:S(2)}) copy-start(bf16[128,32,128]{2,0,1:T(8,128)(2,1)} %copy.40) | copy-start | bytes 3145732
Sparse Core Ops, SparseCore 0:
  9.6 64.1 all-gather.1
  98.3 242.0 all-reduce.1
where the time goes:
time: 403 us; the launch traced here: 402 us
  waiting for transfers between devices  243 us (60%)
  matrix products  46.9 us (12%)
  local copies, waits for them, and re-layouts  42 us (10%)
  other arithmetic  27.5 us (7%)
  starting transfers between devices  25.2 us (6%)
  between operations  16.5 us (4%)
    psum x1, waiting for transfers between devices, shards(): summed = lax.psum(grad_rows(0, HS), 'seq')  170 us
    unnamed x60, local copies, waits for them, and re-layouts  30.4 us
    all_to_all x1, waiting for transfers between devices, shards(): lax.all_to_all(query_norm, 'head', split_axis=1, concat_axis=0, tiled=True)  22.8 us
    all_gather x1, waiting for transfers between devices, shards(): stacked_old = lax.all_gather(own_old, 'seq', axis=0, tiled=True)  21.5 us
    all_to_all x1, waiting for transfers between devices, shards(): lax.all_to_all(value_rows, 'head', split_axis=1, concat_axis=0, tiled=True)  12.1 us
    all_to_all x1, waiting for transfers between devices, shards(): lax.all_to_all(key_norm, 'head', split_axis=1, concat_axis=0, tiled=True)  12 us
    dot_general x4, matrix products, shards(): jnp.dot(query_hidden, weight_columns(updated, head, 2), preferred_element...  11.4 us
  transfers between devices with their start and end apart: 8, of which 7 were waited for; matrix products, arithmetic and copies ran while one was open for 13% of the time, Pallas kernels for 0%

commit v1 on v0

v1 whole, which is shorter than its diff:
```python
import math

import jax
import jax.numpy as jnp
from jax import lax
from jax.experimental import pallas as pl
from jax.experimental.pallas import tpu as pltpu
from jax.sharding import Mesh, PartitionSpec as P


HEADS = 8
HEAD_DIM = 128
WINDOW = 64
STEP_SIZE = 0.05
NORM_EPS = 1e-06
VMEM_LIMIT = 28 * 1024 * 1024
ANY = pl.BlockSpec(memory_space=pl.ANY)
VMEM = pl.BlockSpec(memory_space=pltpu.VMEM)
SMEM = pl.BlockSpec(memory_space=pltpu.SMEM)


def in_vmem(x):
    return pltpu.with_memory_space_constraint(x, pltpu.VMEM)


def in_hbm(x):
    return pltpu.with_memory_space_constraint(x, pltpu.HBM)


def cost(microseconds):
    return pl.CostEstimate(
        flops=int(microseconds * 4e6), bytes_accessed=1 << 20, transcendentals=0
    )


def sds(shape, dtype):
    return jax.ShapeDtypeStruct(shape, dtype)


def params():
    return pltpu.CompilerParams(vmem_limit_bytes=VMEM_LIMIT)


def swap_pairs(count, stride):
    return [(i, i ^ stride) for i in range(count)]


def tiles_to_rows(ref, block, first, rows, tiles):
    return jnp.concatenate(
        [ref[block, first + t * rows : first + (t + 1) * rows, :] for t in range(tiles)], axis=1
    )


def rms_rows(rows):
    wide = rows.astype(jnp.float32)
    scale = lax.rsqrt(jnp.mean(wide * wide, axis=1, keepdims=True) + NORM_EPS)
    return (wide * scale).astype(jnp.bfloat16)


def move_by_head(sources, out_ref, stage_ref, sem_in, sem_out, order, rows, tiles):
    size = tiles * HEAD_DIM
    reads, writes = [], []
    for peer, head in enumerate(order):
        for which, ref in enumerate(sources):
            spot = peer * len(sources) + which
            reads.append(
                pltpu.make_async_copy(
                    ref.at[:, pl.ds(head * size, size)], stage_ref.at[spot], sem_in.at[spot]
                )
            )
            for t in range(tiles):
                writes.append(
                    pltpu.make_async_copy(
                        stage_ref.at[spot, :, pl.ds(t * HEAD_DIM, HEAD_DIM)],
                        out_ref.at[peer, pl.ds((which * tiles + t) * rows, rows), :],
                        sem_out.at[spot * tiles + t],
                    )
                )
    for read in reads:
        read.start()
    for i, read in enumerate(reads):
        read.wait()
        for write in writes[i * tiles : (i + 1) * tiles]:
            write.start()
    return writes


def pack_keys(key_rows, value_rows, rates_t, order, rate_rows):
    rows, width = key_rows.shape
    tiles = width // HEADS // HEAD_DIM

    def kernel(k_ref, v_ref, r_ref, out_ref, stage_ref, rate_ref, sem_in, sem_out, sem_rate):
        for peer, head in enumerate(order):
            rate_ref[peer] = jnp.broadcast_to(
                r_ref[head : head + 1, :].astype(jnp.float32), (rate_rows, rows)
            ).astype(jnp.bfloat16)
        last = pltpu.make_async_copy(
            rate_ref, out_ref.at[:, pl.ds(2 * tiles * rows, rate_rows), :], sem_rate
        )
        last.start()
        writes = move_by_head(
            (k_ref, v_ref), out_ref, stage_ref, sem_in, sem_out, order, rows, tiles
        )
        for write in writes:
            write.wait()
        last.wait()

    return pl.pallas_call(
        kernel,
        in_specs=[ANY, ANY, VMEM],
        out_specs=ANY,
        out_shape=pltpu.HBM((HEADS, 2 * tiles * rows + rate_rows, HEAD_DIM), jnp.bfloat16),
        scratch_shapes=[
            pltpu.VMEM((HEADS * 2, rows, tiles * HEAD_DIM), jnp.bfloat16),
            pltpu.VMEM((HEADS, rate_rows, rows), jnp.bfloat16),
            pltpu.SemaphoreType.DMA((HEADS * 2,)),
            pltpu.SemaphoreType.DMA((HEADS * 2 * tiles,)),
            pltpu.SemaphoreType.DMA,
        ],
        compiler_params=params(),
        name="pack_keys",
    )(in_hbm(key_rows), in_hbm(value_rows), rates_t)


def pack_queries(queries, order):
    rows, width = queries.shape
    tiles = width // HEADS // HEAD_DIM

    def kernel(q_ref, out_ref, stage_ref, sem_in, sem_out):
        writes = move_by_head((q_ref,), out_ref, stage_ref, sem_in, sem_out, order, rows, tiles)
        for write in writes:
            write.wait()

    return pl.pallas_call(
        kernel,
        in_specs=[ANY],
        out_specs=ANY,
        out_shape=pltpu.HBM((HEADS, tiles * rows, HEAD_DIM), jnp.bfloat16),
        scratch_shapes=[
            pltpu.VMEM((HEADS, rows, tiles * HEAD_DIM), jnp.bfloat16),
            pltpu.SemaphoreType.DMA((HEADS,)),
            pltpu.SemaphoreType.DMA((HEADS * tiles,)),
        ],
        compiler_params=params(),
        name="pack_queries",
    )(in_hbm(queries))


def pack_weights(w_gate, w_up, w_down):
    piece, heads, size = w_gate.shape

    def kernel(g_ref, u_ref, d_ref, out_ref):
        for which, ref in enumerate((g_ref, u_ref, d_ref)):
            for head in range(heads):
                out_ref[head, which] = ref[:, head, :]

    return pl.pallas_call(
        kernel,
        in_specs=[VMEM] * 3,
        out_specs=VMEM,
        out_shape=pltpu.HBM((heads, 3, piece, size), w_gate.dtype),
        compiler_params=params(),
        name="pack_weights",
    )(in_hbm(w_gate), in_hbm(w_up), in_hbm(w_down))


def unpack_columns(back, places):
    heads, rows, size = back.shape

    def kernel(back_ref, out_ref, sem):
        moves = [
            pltpu.make_async_copy(
                back_ref.at[place], out_ref.at[:, pl.ds(head * size, size)], sem.at[head]
            )
            for head, place in enumerate(places)
        ]
        for move in moves:
            move.start()
        for move in moves:
            move.wait()

    return pl.pallas_call(
        kernel,
        in_specs=[ANY],
        out_specs=ANY,
        out_shape=sds((rows, heads * size), back.dtype),
        scratch_shapes=[pltpu.SemaphoreType.DMA((heads,))],
        compiler_params=params(),
        name="unpack_columns",
    )(back)


def place_pieces(spot_ref, piece_refs, out_ref, outer, lane, inner):
    if len(piece_refs) == 1:
        out_ref[...] = piece_refs[0][...]
        return
    piece = piece_refs[0].shape[2]
    a, c = spot_ref[0], spot_ref[1]
    spots = [(a, c), (outer - 1 - a, c), (a, inner - 1 - c), (outer - 1 - a, inner - 1 - c)]
    for (at_a, at_c), ref in zip(spots, piece_refs):
        for l in range(lane):
            first = pl.multiple_of(((at_a * lane + l) * inner + at_c) * piece, piece)
            for which in range(3):
                out_ref[which, pl.ds(first, piece), :] = ref[l, which]


def gradients(spot, received, pieces, rows, tiles, outer, lane, inner):
    blocks = received.shape[0]
    size = tiles * HEAD_DIM
    half = size // inner
    count = blocks * rows
    group = 2 if blocks % 2 == 0 else 1
    span = group * rows

    def kernel(spot_ref, kv_ref, *refs):
        piece_refs = refs[: len(pieces)]
        keep_ref, send_ref, w_ref, kn_ref, hid_ref, tgt_ref, gg_ref, ug_ref = refs[len(pieces) :]
        place_pieces(spot_ref, piece_refs, w_ref, outer, lane, inner)
        for g in range(blocks // group):
            here = slice(g * span, (g + 1) * span)
            mine = range(g * group, (g + 1) * group)

            def stacked(first):
                return jnp.concatenate(
                    [tiles_to_rows(kv_ref, b, first, rows, tiles) for b in mine], axis=0
                )

            key_norm = rms_rows(stacked(0))
            values = stacked(tiles * rows).astype(jnp.float32)
            rates = []
            for b in mine:
                row = kv_ref[b, 2 * tiles * rows : 2 * tiles * rows + 1, :].astype(jnp.float32)
                rates.append(jnp.broadcast_to(row, (rows, rows)).T)
            rate_columns = jnp.concatenate([jnp.concatenate(rates, axis=0)] * tiles, axis=1)
            target = (-rate_columns * values).astype(jnp.bfloat16)
            tgt_ref[here, :] = target
            gate_pre = jnp.dot(key_norm, w_ref[0], preferred_element_type=jnp.float32)
            up_pre = jnp.dot(key_norm, w_ref[1], preferred_element_type=jnp.float32)
            hidden_grad = lax.dot_general(
                target, w_ref[2], (((1,), (1,)), ((), ())), preferred_element_type=jnp.float32
            )
            sigma_gate = jax.nn.sigmoid(gate_pre)
            silu_gate = gate_pre * sigma_gate
            hidden = (silu_gate * up_pre).astype(jnp.bfloat16)
            for part in range(inner):
                columns = slice(part * half, (part + 1) * half)
                kn_ref[part, here, :] = key_norm[:, columns]
                hid_ref[part, here, :] = hidden[:, columns]
            gg_ref[here, :] = (
                hidden_grad * up_pre * sigma_gate * (1.0 + gate_pre * (1.0 - sigma_gate))
            ).astype(jnp.bfloat16)
            ug_ref[here, :] = (hidden_grad * silu_gate).astype(jnp.bfloat16)

        def total(left_ref, right_ref, part):
            return lax.dot_general(
                left_ref[part],
                right_ref[...],
                (((0,), (0,)), ((), ())),
                preferred_element_type=jnp.float32,
            )

        own = spot_ref[1]
        pairs = ((kn_ref, gg_ref), (kn_ref, ug_ref), (hid_ref, tgt_ref))
        for which, (left_ref, right_ref) in enumerate(pairs):
            send_ref[which] = total(left_ref, right_ref, inner - 1 - own).astype(jnp.bfloat16)
            keep_ref[which] = total(left_ref, right_ref, own)

    return pl.pallas_call(
        kernel,
        in_specs=[SMEM, VMEM] + [VMEM] * len(pieces),
        out_specs=[VMEM, VMEM],
        out_shape=[
            pltpu.VMEM((3, half, size), jnp.float32),
            pltpu.VMEM((3, half, size), jnp.bfloat16),
        ],
        scratch_shapes=[
            pltpu.VMEM((3, size, size), jnp.bfloat16),
            pltpu.VMEM((inner, count, half), jnp.bfloat16),
            pltpu.VMEM((inner, count, half), jnp.bfloat16),
            pltpu.VMEM((count, size), jnp.bfloat16),
            pltpu.VMEM((count, size), jnp.bfloat16),
            pltpu.VMEM((count, size), jnp.bfloat16),
        ],
        compiler_params=params(),
        cost_estimate=cost(6),
        name="gradients",
    )(spot, in_vmem(received), *[in_vmem(p) for p in pieces])


def combine(keep, got):
    def kernel(keep_ref, got_ref, out_ref):
        out_ref[...] = (keep_ref[...] + got_ref[...].astype(jnp.float32)).astype(jnp.bfloat16)

    return pl.pallas_call(
        kernel,
        in_specs=[VMEM, VMEM],
        out_specs=VMEM,
        out_shape=pltpu.VMEM(keep.shape, jnp.bfloat16),
        compiler_params=params(),
        name="combine",
    )(in_vmem(keep), in_vmem(got))


def last_rows(received, rows, tiles, per_run):
    runs = received.shape[0] // per_run

    def kernel(kv_ref, out_ref):
        for run in range(runs):
            for t in range(2 * tiles):
                end = (t + 1) * rows
                out_ref[run, t * WINDOW : (t + 1) * WINDOW, :] = kv_ref[
                    (run + 1) * per_run - 1, end - WINDOW : end, :
                ]

    return pl.pallas_call(
        kernel,
        in_specs=[VMEM],
        out_specs=VMEM,
        out_shape=pltpu.VMEM((runs, 2 * tiles * WINDOW, HEAD_DIM), received.dtype),
        compiler_params=params(),
        name="last_rows",
    )(in_vmem(received))


def attention(spot, queries, received, around, from_outer, rows, tiles, per_run):
    blocks = queries.shape[0]
    width = tiles * HEAD_DIM
    span = WINDOW + rows

    def kernel(spot_ref, q_ref, kv_ref, around_ref, outer_ref, att_ref, qn_ref, bias_ref):
        on_first = jnp.where(spot_ref[1] == 0, 1, 0)
        begins = jnp.where(spot_ref[0] == 0, on_first, 0)
        row_id = lax.broadcasted_iota(jnp.int32, (rows, span), 0)
        key_id = lax.broadcasted_iota(jnp.int32, (rows, span), 1)
        allowed = (key_id <= row_id + WINDOW) & (key_id > row_id)
        bias_ref[0] = jnp.where(allowed, 0.0, -1e30)
        bias_ref[1] = jnp.where(allowed & (key_id >= WINDOW), 0.0, -1e30)
        for b in range(blocks):
            qn_ref[b] = rms_rows(tiles_to_rows(q_ref, b, 0, rows, tiles))
            bias = bias_ref[begins] if b == 0 else bias_ref[0]
            for t in range(tiles):
                query = q_ref[b, t * rows : (t + 1) * rows, :]

                def with_tail(which):
                    base = (which * tiles + t) * rows
                    own = kv_ref[b, base : base + rows, :]
                    if b % per_run:
                        tail = kv_ref[b - 1, base + rows - WINDOW : base + rows, :]
                    else:
                        first = (which * tiles + t) * WINDOW
                        place = slice(first, first + WINDOW)
                        if b:
                            tail = around_ref[b // per_run - on_first, place, :]
                        else:
                            tail = jnp.where(
                                on_first == 1, outer_ref[0, place, :], around_ref[0, place, :]
                            )
                    return jnp.concatenate([tail, own], axis=0)

                keys = with_tail(0)
                values = with_tail(1)
                scores = lax.dot_general(
                    query, keys, (((1,), (1,)), ((), ())), preferred_element_type=jnp.float32
                )
                masked = scores * (1.0 / math.sqrt(HEAD_DIM)) + bias
                maximum = jnp.max(masked, axis=1, keepdims=True)
                exp_scores = jnp.exp(masked - maximum)
                totals = jnp.sum(exp_scores, axis=1, keepdims=True)
                mixed = jnp.dot(
                    exp_scores.astype(jnp.bfloat16), values, preferred_element_type=jnp.float32
                )
                att_ref[b, :, t * HEAD_DIM : (t + 1) * HEAD_DIM] = mixed * (1.0 / totals)

    return pl.pallas_call(
        kernel,
        in_specs=[SMEM] + [VMEM] * 4,
        out_specs=[VMEM, VMEM],
        out_shape=[
            pltpu.VMEM((blocks, rows, width), jnp.float32),
            pltpu.VMEM((blocks, rows, width), jnp.bfloat16),
        ],
        scratch_shapes=[pltpu.VMEM((2, rows, span), jnp.float32)],
        compiler_params=params(),
        cost_estimate=cost(6),
        name="attention",
    )(spot, in_vmem(queries), in_vmem(received), in_vmem(around), in_vmem(from_outer))


def update_and_apply(spot, pieces, sums, query_norm, attended, outer, lane, inner):
    blocks, rows, size = query_norm.shape
    halves = len(sums) // 2
    half = size // halves
    group = 2 if blocks % 2 == 0 else 1

    def kernel(spot_ref, *refs):
        piece_refs, refs = refs[: len(pieces)], refs[len(pieces) :]
        sum_refs = refs[: 2 * halves]
        q_ref, a_ref, out_ref, w_ref, total_ref, new_ref = refs[2 * halves :]
        place_pieces(spot_ref, piece_refs, w_ref, outer, lane, inner)
        squares = jnp.zeros((8, size), jnp.float32)
        for part in range(halves):
            place = spot_ref[1] if part == 0 else halves - 1 - spot_ref[1]
            for which in range(3):
                total = sum_refs[2 * part][which].astype(jnp.float32) + sum_refs[2 * part + 1][
                    which
                ].astype(jnp.float32)
                total_ref[place, which] = total
                squares = squares + jnp.sum(
                    (total * total).reshape(half // 8, 8, size), axis=0
                )
        norm_scale = lax.rsqrt(
            jnp.sum(squares, axis=(0, 1), keepdims=True) / (3 * size * size) + NORM_EPS
        )
        scale = STEP_SIZE * norm_scale
        for part in range(halves):
            for which in range(3):
                here = slice(part * half, (part + 1) * half)
                previous = w_ref[which, here, :].astype(jnp.float32)
                stepped = previous - scale * total_ref[part, which]
                factor = jnp.sqrt(
                    jnp.mean(previous * previous, axis=1, keepdims=True)
                ) * lax.rsqrt(jnp.mean(stepped * stepped, axis=1, keepdims=True) + NORM_EPS)
                new_ref[which, here, :] = (stepped * factor).astype(jnp.bfloat16)
        for g in range(blocks // group):
            mine = range(g * group, (g + 1) * group)
            query = jnp.concatenate([q_ref[b] for b in mine], axis=0)
            query_gate = jnp.dot(query, new_ref[0], preferred_element_type=jnp.float32)
            query_up = jnp.dot(query, new_ref[1], preferred_element_type=jnp.float32)
            query_hidden = (query_gate * jax.nn.sigmoid(query_gate) * query_up).astype(
                jnp.bfloat16
            )
            fast = jnp.dot(query_hidden, new_ref[2], preferred_element_type=jnp.float32).astype(
                jnp.bfloat16
            )
            for i, b in enumerate(mine):
                out_ref[b] = (
                    a_ref[b] + fast[i * rows : (i + 1) * rows, :].astype(jnp.float32)
                ).astype(jnp.bfloat16)

    return pl.pallas_call(
        kernel,
        in_specs=[SMEM] + [VMEM] * (len(pieces) + len(sums) + 2),
        out_specs=VMEM,
        out_shape=pltpu.HBM((blocks, rows, size), jnp.bfloat16),
        scratch_shapes=[
            pltpu.VMEM((3, size, size), jnp.bfloat16),
            pltpu.VMEM((halves, 3, half, size), jnp.float32),
            pltpu.VMEM((3, size, size), jnp.bfloat16),
        ],
        compiler_params=params(),
        cost_estimate=cost(6),
        name="update_and_apply",
    )(
        spot,
        *[in_vmem(p) for p in pieces],
        *[in_vmem(s) for s in sums],
        in_vmem(query_norm),
        in_vmem(attended),
    )


def gather_rows(mine, axis, count, index, order_axis):
    if count & (count - 1):
        return lax.all_gather(mine, axis, axis=order_axis, tiled=True)
    stride = 1
    while stride < count:
        theirs = lax.ppermute(mine, axis, swap_pairs(count, stride))
        low = (index // stride) % 2 == 0
        mine = jnp.concatenate(
            [jnp.where(low, mine, theirs), jnp.where(low, theirs, mine)], order_axis
        )
        stride *= 2
    return mine


def make_shards(outer, lane, inner, head_axis):
    group = ("lane", "head")
    order = [(p % head_axis) * lane + p // head_axis for p in range(HEADS)]
    place_of_head = [order.index(h) for h in range(HEADS)]

    def shards(queries, key_rows, value_rows, step_rates, w_gate, w_up, w_down):
        rows, width = queries.shape
        size = width // HEADS
        tiles = size // HEAD_DIM
        rate_rows = 16
        a = lax.axis_index("outer")
        c = lax.axis_index("inner")
        spot = jnp.stack([a, c]).astype(jnp.int32)
        spot, key_rows = lax.optimization_barrier((spot, key_rows))

        own = pack_weights(w_gate, w_up, w_down)
        if lane > 1:
            own = lax.all_to_all(own, "lane", split_axis=0, concat_axis=0, tiled=True)
        kv = pack_keys(key_rows, value_rows, jnp.transpose(step_rates), order, rate_rows)
        kv = lax.all_to_all(kv, group, split_axis=0, concat_axis=0, tiled=True)
        qs = pack_queries(queries, order)
        qs = lax.all_to_all(qs, group, split_axis=0, concat_axis=0, tiled=True)

        if outer == 2 and inner == 2:
            other = lax.ppermute(own, "outer", swap_pairs(outer, 1))
            own_beside = lax.ppermute(own, "inner", swap_pairs(inner, 1))
            other_beside = lax.ppermute(other, "inner", swap_pairs(inner, 1))
            pieces = [own, other, own_beside, other_beside]
        else:
            old = gather_rows(own[None], "outer", outer, a, 0)[:, :, None]
            old = gather_rows(old, "inner", inner, c, 2)
            pieces = [jnp.transpose(old, (3, 0, 1, 2, 4, 5)).reshape(3, size, size)]

        keep, send = gradients(spot, kv, pieces, rows, tiles, outer, lane, inner)
        if inner > 1:
            got = lax.ppermute(send, "inner", swap_pairs(inner, 1))
            half = combine(keep, got)
        else:
            half = keep.astype(jnp.bfloat16)
        mine, theirs = half, jnp.zeros_like(half)
        if outer & (outer - 1):
            mine = lax.psum(half, "outer")
        else:
            stride = 1
            while stride < outer:
                if stride > 1:
                    mine = (mine.astype(jnp.float32) + theirs.astype(jnp.float32)).astype(
                        jnp.bfloat16
                    )
                theirs = lax.ppermute(mine, "outer", swap_pairs(outer, stride))
                stride *= 2
        tails = last_rows(kv, rows, tiles, head_axis)
        around = tails
        if inner > 1:
            around = lax.ppermute(tails, "inner", [(i, (i + 1) % inner) for i in range(inner)])
        last = tails[lane - 1 :]
        pairs = [
            (i * inner + inner - 1, (i + 1) * inner) for i in range(outer - 1)
        ]
        from_outer = lax.ppermute(last, ("outer", "inner"), pairs) if pairs else last
        attended, query_norm = attention(spot, qs, kv, around, from_outer, rows, tiles, head_axis)

        theirs, attended, query_norm = lax.optimization_barrier((theirs, attended, query_norm))
        sums = [mine, theirs]
        if inner > 1:
            sums.append(lax.ppermute(mine, "inner", swap_pairs(inner, 1)))
            sums.append(lax.ppermute(theirs, "inner", swap_pairs(inner, 1)))

        out = update_and_apply(spot, pieces, sums, query_norm, attended, outer, lane, inner)
        back = lax.all_to_all(out, group, split_axis=0, concat_axis=0, tiled=True)
        return unpack_columns(back, place_of_head)

    return shards


def solution(mesh):
    seq, head_axis = mesh.shape["seq"], mesh.shape["head"]
    lane = HEADS // head_axis
    inner = 2 if (seq // lane) % 2 == 0 else 1
    outer = seq // lane // inner
    names = ("outer", "lane", "inner", "head")
    split = Mesh(mesh.devices.reshape(outer, lane, inner, head_axis), names)
    rows = P(names, None)
    weights = P(names[:3], names[3], None)
    shards = make_shards(outer, lane, inner, head_axis)

    return jax.shard_map(
        shards,
        mesh=split,
        in_specs=(rows, rows, rows, rows, weights, weights, weights),
        out_specs=rows,
        check_vma=False,
    )
```

time: 403 us -> 151 us (0.37)
  waiting for transfers between devices: 243 us -> 49.9 us
  matrix products: 46.9 us -> 0 us
  local copies, waits for them, and re-layouts: 42 us -> 1.59 us
  Pallas kernels: 0 us -> 33.5 us
  blocking collectives: 0 us -> 30.4 us
  other arithmetic: 27.5 us -> 0.07 us
  between operations: 16.5 us -> 0.24 us
  starting transfers between devices: 25.2 us -> 35.2 us
    psum x1 -> x0, waiting for transfers between devices: 170 us -> none  [shards(): summed = lax.psum(grad_rows(0, HS), 'seq')]
    dot_general x34 -> x0, matrix products: 46.9 us -> none  [the longest x4 11.4 us: shards(): jnp.dot(query_hidden, weight_columns(updated, head, 2), preferred_element...]
    all_to_all x5 -> x3, waiting for transfers between devices: 51.6 us -> 6.59 us  [the longest x1 3.3 us: shards(): own = lax.all_to_all(own, 'lane', split_axis=0, concat_axis=0, tiled=True)]
    ppermute x1 -> x9, waiting for transfers between devices: 0.01 us -> 43.3 us  [the longest x1 31.6 us: shards(): other = lax.ppermute(own, 'outer', swap_pairs(outer, 1))]
    pallas_call x0 -> x9, Pallas kernels: none -> 33.5 us  [the longest x1 9.34 us: attention(): pl.pallas_call(kernel, in_specs=[SMEM] + [VMEM] * 4, out_specs=[VMEM, VME...]
    all_to_all x0 -> x1, blocking collectives: none -> 30.4 us  [shards(): back = lax.all_to_all(out, group, split_axis=0, concat_axis=0, tiled=True)]
    unnamed x60 -> x2, local copies, waits for them, and re-layouts: 30.4 us -> 0.68 us
    all_gather x1 -> x0, waiting for transfers between devices: 21.5 us -> none  [shards(): stacked_old = lax.all_gather(own_old, 'seq', axis=0, tiled=True)]
  transfers between devices with their start and end apart: 8 -> 12, of which waited for: 7 -> 6; matrix products, arithmetic and copies ran while one was open for 13% -> 1% of each run, Pallas kernels for 0% -> 15%
where the time goes in v1:
time: 151 us
  waiting for transfers between devices  49.9 us (33%)
  starting transfers between devices  35.2 us (23%)
  Pallas kernels  33.5 us (22%)
  blocking collectives  30.4 us (20%)
  local copies, waits for them, and re-layouts  1.59 us (1%)
    ppermute x1, waiting for transfers between devices, shards(): other = lax.ppermute(own, 'outer', swap_pairs(outer, 1))  31.6 us
    all_to_all x1, blocking collectives, shards(): back = lax.all_to_all(out, group, split_axis=0, concat_axis=0, tiled=True)  30.4 us
    ppermute x1, starting transfers between devices, shards(): sums.append(lax.ppermute(mine, 'inner', swap_pairs(inner, 1)))  15.1 us
    pallas_call x1, Pallas kernels, attention(): pl.pallas_call(kernel, in_specs=[SMEM] + [VMEM] * 4, out_specs=[VMEM, VME...  9.34 us
    ppermute x1, waiting for transfers between devices, shards(): theirs = lax.ppermute(mine, 'outer', swap_pairs(outer, stride))  7.16 us
    pallas_call x1, Pallas kernels, update_and_apply(): pl.pallas_call(kernel, in_specs=[SMEM] + [VMEM] * (len(pieces) + len(sums...  7.11 us
    all_to_all x1, starting transfers between devices, shards(): qs = lax.all_to_all(qs, group, split_axis=0, concat_axis=0, tiled=True)  6.94 us
    pallas_call x1, Pallas kernels, gradients(): pl.pallas_call(kernel, in_specs=[SMEM, VMEM] + [VMEM] * len(pieces), out_...  6.32 us
  transfers between devices with their start and end apart: 12, of which 6 were waited for; matrix products, arithmetic and copies ran while one was open for 1% of the time, Pallas kernels for 15%

profile of v1, /device:TPU:0, one launch (start us, length us, event | category | flops | bytes accessed | tf_op | source)
XLA Modules:
  0.0 150.8 jit_solution(5371965769807096845)
XLA Ops:
  0.0 2.4 %pack_weights.1 = bf16[4,3,32,512]{3,2,1,0:T(8,128)(2,1)} custom-call(bf16[32,4,512]{2,1,0:T(4,128)(2,1)} %g_ref.1, bf16[32,4,512]{2,1,0:T(4,128)(2,1)} %u_ref.1, bf16[32,4,512]{2,1,0:T(4,128)(2,1)} %d_ref.1), custom_call_target="tpu_custom_call" | custom-call | tf_op jit(solution)/shard_map/pack_weights/pallas_call | solution.py:157
  2.4 5.2 %all-to-all-start = ((bf16[4,3,32,512]{3,2,1,0:T(8,128)(2,1)}), bf16[4,3,32,512]{3,2,1,0:T(8,128)(2,1)}, u32[]{:S(2)}, u32[]{:S(2)}) async-start(bf16[4,3,32,512]{3,2,1,0:T(8,128)(2,1)} %pack_weights.1), calls=%async_computation | async-start | bytes 786432 | tf_op jit(solution)/shard_map/all_to_all | solution.py:493
  7.7 0.1 pad_add_fusion.spot_ref
  7.8 0.0 copy-start
  7.8 0.7 copy-done
  8.5 3.1 %pack_keys.1 = bf16[8,1040,128]{2,1,0:T(8,128)(2,1)} custom-call(bf16[128,4096]{1,0:T(8,128)(2,1)} %k_ref, bf16[128,4096]{1,0:T(8,128)(2,1)} %v_ref.1, bf16[8,128]{1,0:T(8,128)(2,1)S(1)} %bitcast.3), custom_call_target="tpu_custom_call" | custom-call | tf_op jit(solution)/shard_map/pack_keys/pallas_call | solution.py:108
  11.5 3.3 %all-to-all-done.refs_0_ = bf16[4,3,32,512]{3,2,1,0:T(8,128)(2,1)} async-done(((bf16[4,3,32,512]{3,2,1,0:T(8,128)(2,1)}), bf16[4,3,32,512]{3,2,1,0:T(8,128)(2,1)}, u32[]{:S(2)}, u32[]{:S(2)}) %all-to-all-start) | async-done | bytes 393248 | tf_op jit(solution)/shard_map/all_to_all | solution.py:493
  14.8 3.8 %all-to-all-start.1 = ((bf16[8,1040,128]{2,1,0:T(8,128)(2,1)}), bf16[8,1040,128]{2,1,0:T(8,128)(2,1)S(1)}, u32[]{:S(2)}, u32[]{:S(2)}) async-start(bf16[8,1040,128]{2,1,0:T(8,128)(2,1)} %pack_keys.1), calls=%async_computation.1 | async-start | bytes 4259840 | tf_op jit(solution)/shard_map/all_to_all | solution.py:495
  18.7 2.6 %collective-permute-start = (bf16[4,3,32,512]{3,2,1,0:T(8,128)(2,1)}, bf16[4,3,32,512]{3,2,1,0:T(8,128)(2,1)}, u32[]{:S(2)}, u32[]{:S(2)}) collective-permute-start(bf16[4,3,32,512]{3,2,1,0:T(8,128)(2,1)} %all-to-all-done.refs_0_), channel_id=1, source_target_pairs={{0,16},{16,0},{1,17},{17,1},{2,18},{18,2},{3,19},{19,3},{4,20},{20... | collective-permute-start | bytes 1179656 | tf_op jit(solution)/shard_map/ppermute | solution.py:500
  21.3 0.0 collective-permute-start.1
  21.3 31.6 %collective-permute-done.refs_1_ = bf16[4,3,32,512]{3,2,1,0:T(8,128)(2,1)} collective-permute-done((bf16[4,3,32,512]{3,2,1,0:T(8,128)(2,1)}, bf16[4,3,32,512]{3,2,1,0:T(8,128)(2,1)}, u32[]{:S(2)}, u32[]{:S(2)}) %collective-permute-start) | collective-permute-done | bytes 393248 | tf_op jit(solution)/shard_map/ppermute | solution.py:500
  52.9 0.0 collective-permute-start.2
  52.9 2.3 %pack_queries.1 = bf16[8,512,128]{2,1,0:T(8,128)(2,1)} custom-call(bf16[128,4096]{1,0:T(8,128)(2,1)} %q_ref.1), custom_call_target="tpu_custom_call" | custom-call | tf_op jit(solution)/shard_map/pack_queries/pallas_call | solution.py:134
  55.2 0.0 all-to-all-done.1.kv_ref
  55.2 6.9 %all-to-all-start.2 = ((bf16[8,512,128]{2,1,0:T(8,128)(2,1)}), bf16[8,512,128]{2,1,0:T(8,128)(2,1)S(1)}, u32[]{:S(2)}, u32[]{:S(2)}) async-start(bf16[8,512,128]{2,1,0:T(8,128)(2,1)} %pack_queries.1), calls=%async_computation.2 | async-start | bytes 2097152 | tf_op jit(solution)/shard_map/all_to_all | solution.py:497
  62.1 0.0 collective-permute-done.1.refs_2_
  62.1 0.0 collective-permute-done.2.refs_3_
  62.1 6.3 %gradients.1 = (f32[3,256,512]{2,1,0:T(8,128)S(1)}, bf16[3,256,512]{2,1,0:T(8,128)(2,1)S(1)}) custom-call(s32[2]{0:T(128)S(1)} %pad_add_fusion.spot_ref, bf16[8,1040,128]{2,1,0:T(8,128)(2,1)S(1)} %all-to-all-done.1.kv_ref, bf16[4,3,32,512]{3,2,1,0:T(8,128)(2,1)} %all-to-all-done.refs_0_, bf16[4,3,32,512]{3,2,1,0:T(8,128)(2,1)} %collective-permute-done.refs_1_, ...), custom_call_target="tpu_custom_call" | custom-call | flops 24000000 | bytes 1048576 | tf_op jit(solution)/shard_map/gradients/pallas_call | solution.py:268
  68.5 0.3 collective-permute-start.3
  68.8 2.1 %collective-permute-done.3.got_ref = bf16[3,256,512]{2,1,0:T(8,128)(2,1)S(1)} collective-permute-done((bf16[3,256,512]{2,1,0:T(8,128)(2,1)S(1)}, bf16[3,256,512]{2,1,0:T(8,128)(2,1)S(1)}, u32[]{:S(2)}, u32[]{:S(2)}) %collective-permute-start.3) | collective-permute-done | bytes 786464 | tf_op jit(solution)/shard_map/ppermute | solution.py:511
  70.8 1.0 combine.1.refs_4_
  71.9 0.2 collective-permute-start.4
  72.0 0.9 last_rows.1
  72.9 0.1 collective-permute-start.5
  73.0 0.9 slice.4
  73.9 0.8 collective-permute-start.6
  74.7 3.3 %all-to-all-done.2.q_ref = bf16[8,512,128]{2,1,0:T(8,128)(2,1)S(1)} async-done(((bf16[8,512,128]{2,1,0:T(8,128)(2,1)}), bf16[8,512,128]{2,1,0:T(8,128)(2,1)S(1)}, u32[]{:S(2)}, u32[]{:S(2)}) %all-to-all-start.2) | async-done | bytes 1048608 | tf_op jit(solution)/shard_map/all_to_all | solution.py:497
  78.0 0.0 collective-permute-done.6.outer_ref
  78.0 0.0 collective-permute-done.5.around_ref
  78.0 9.3 %attention.1 = (f32[8,128,512]{2,1,0:T(8,128)S(1)}, bf16[8,128,512]{2,1,0:T(8,128)(2,1)S(1)}) custom-call(s32[2]{0:T(128)S(1)} %pad_add_fusion.spot_ref, bf16[8,512,128]{2,1,0:T(8,128)(2,1)S(1)} %all-to-all-done.2.q_ref, bf16[8,1040,128]{2,1,0:T(8,128)(2,1)S(1)} %all-to-all-done.1.kv_ref, bf16[4,512,128]{2,1,0:T(8,128)(2,1)} %collective-permute-done.5.around_ref, ...), custom_call_target="tpu_custom_call" | custom-call | flops 24000000 | bytes 1048576 | tf_op jit(solution)/shard_map/attention/pallas_call | solution.py:374
  87.4 15.1 %collective-permute-start.7 = (bf16[3,256,512]{2,1,0:T(8,128)(2,1)}, bf16[3,256,512]{2,1,0:T(8,128)(2,1)S(1)}, u32[]{:S(2)}, u32[]{:S(2)}) collective-permute-start(bf16[3,256,512]{2,1,0:T(8,128)(2,1)} %combine.1.refs_4_), channel_id=1, source_target_pairs={{0,2},{2,0},{1,3},{3,1},{4,6},{6,4},{5,7},{7,5},{8,10},{10,8},{9,1... | collective-permute-start | bytes 2359304 | tf_op jit(solution)/shard_map/ppermute | solution.py:541
  102.5 7.2 %collective-permute-done.4.refs_5_ = bf16[3,256,512]{2,1,0:T(8,128)(2,1)} collective-permute-done((bf16[3,256,512]{2,1,0:T(8,128)(2,1)}, bf16[3,256,512]{2,1,0:T(8,128)(2,1)}, u32[]{:S(2)}, u32[]{:S(2)}) %collective-permute-start.4) | collective-permute-done | bytes 786464 | tf_op jit(solution)/shard_map/ppermute | solution.py:525
  109.6 0.0 collective-permute-start.8
  109.6 0.0 collective-permute-done.7.refs_6_
  109.7 2.5 %collective-permute-done.8.refs_7_ = bf16[3,256,512]{2,1,0:T(8,128)(2,1)S(1)} collective-permute-done((bf16[3,256,512]{2,1,0:T(8,128)(2,1)}, bf16[3,256,512]{2,1,0:T(8,128)(2,1)S(1)}, u32[]{:S(2)}, u32[]{:S(2)}) %collective-permute-start.8) | collective-permute-done | bytes 786464 | tf_op jit(solution)/shard_map/ppermute | solution.py:542
  112.1 7.1 %update_and_apply.1 = bf16[8,128,512]{2,1,0:T(8,128)(2,1)} custom-call(s32[2]{0:T(128)S(1)} %pad_add_fusion.spot_ref, bf16[4,3,32,512]{3,2,1,0:T(8,128)(2,1)} %all-to-all-done.refs_0_, bf16[4,3,32,512]{3,2,1,0:T(8,128)(2,1)} %collective-permute-done.refs_1_, bf16[4,3,32,512]{3,2,1,0:T(8,128)(2,1)} %collective-permute-done.1.refs_2_, ...), custom_call_target="tpu_custom_call" | custom-call | flops 24000000 | bytes 1048576 | tf_op jit(solution)/shard_map/update_and_apply/pallas_call | solution.py:440
  119.3 30.4 %all_to_all.20.back_ref = bf16[8,128,512]{2,1,0:T(8,128)(2,1)S(1)} all-to-all(bf16[8,128,512]{2,1,0:T(8,128)(2,1)} %update_and_apply.1), channel_id=1, replica_groups=mesh['outer'=2,'lane'=4,'inner'=2,'head'=2] {'lane','head'}, dimensions={0} | all-to-all | bytes 2097152 | tf_op jit(solution)/shard_map/all_to_all | solution.py:545
  149.7 1.0 unpack_columns.1
Async XLA Ops:
  2.4 12.4 %all-to-all-start = ((bf16[4,3,32,512]{3,2,1,0:T(8,128)(2,1)}), bf16[4,3,32,512]{3,2,1,0:T(8,128)(2,1)}, u32[]{:S(2)}, u32[]{:S(2)}) async-start(bf16[4,3,32,512]{3,2,1,0:T(8,128)(2,1)} %pack_weights.1), calls=%async_computation | async-start | bytes 786432 | tf_op jit(solution)/shard_map/all_to_all | solution.py:493
  7.8 0.7 copy-start
  14.8 40.3 %all-to-all-start.1 = ((bf16[8,1040,128]{2,1,0:T(8,128)(2,1)}), bf16[8,1040,128]{2,1,0:T(8,128)(2,1)S(1)}, u32[]{:S(2)}, u32[]{:S(2)}) async-start(bf16[8,1040,128]{2,1,0:T(8,128)(2,1)} %pack_keys.1), calls=%async_computation.1 | async-start | bytes 4259840 | tf_op jit(solution)/shard_map/all_to_all | solution.py:495
  18.7 34.2 %collective-permute-start = (bf16[4,3,32,512]{3,2,1,0:T(8,128)(2,1)}, bf16[4,3,32,512]{3,2,1,0:T(8,128)(2,1)}, u32[]{:S(2)}, u32[]{:S(2)}) collective-permute-start(bf16[4,3,32,512]{3,2,1,0:T(8,128)(2,1)} %all-to-all-done.refs_0_), channel_id=1, source_target_pairs={{0,16},{16,0},{1,17},{17,1},{2,18},{18,2},{3,19},{19,3},{4,20},{20... | collective-permute-start | bytes 1179656 | tf_op jit(solution)/shard_map/ppermute | solution.py:500
  21.3 40.8 %collective-permute-start.1 = (bf16[4,3,32,512]{3,2,1,0:T(8,128)(2,1)}, bf16[4,3,32,512]{3,2,1,0:T(8,128)(2,1)}, u32[]{:S(2)}, u32[]{:S(2)}) collective-permute-start(bf16[4,3,32,512]{3,2,1,0:T(8,128)(2,1)} %all-to-all-done.refs_0_), channel_id=1, source_target_pairs={{0,2},{2,0},{1,3},{3,1},{4,6},{6,4},{5,7},{7,5},{8,10},{10,8},{9,1... | collective-permute-start | bytes 1179656 | tf_op jit(solution)/shard_map/ppermute | solution.py:501
  52.9 9.3 %collective-permute-start.2 = (bf16[4,3,32,512]{3,2,1,0:T(8,128)(2,1)}, bf16[4,3,32,512]{3,2,1,0:T(8,128)(2,1)}, u32[]{:S(2)}, u32[]{:S(2)}) collective-permute-start(bf16[4,3,32,512]{3,2,1,0:T(8,128)(2,1)} %collective-permute-done.refs_1_), channel_id=1, source_target_pairs={{0,2},{2,0},{1,3},{3,1},{4,6},{6,4},{5,7},{7,5},{8,10},{10,8},{9,1... | collective-permute-start | bytes 1179656 | tf_op jit(solution)/shard_map/ppermute | solution.py:502
  55.2 22.8 %all-to-all-start.2 = ((bf16[8,512,128]{2,1,0:T(8,128)(2,1)}), bf16[8,512,128]{2,1,0:T(8,128)(2,1)S(1)}, u32[]{:S(2)}, u32[]{:S(2)}) async-start(bf16[8,512,128]{2,1,0:T(8,128)(2,1)} %pack_queries.1), calls=%async_computation.2 | async-start | bytes 2097152 | tf_op jit(solution)/shard_map/all_to_all | solution.py:497
  68.5 2.4 %collective-permute-start.3 = (bf16[3,256,512]{2,1,0:T(8,128)(2,1)S(1)}, bf16[3,256,512]{2,1,0:T(8,128)(2,1)S(1)}, u32[]{:S(2)}, u32[]{:S(2)}) collective-permute-start(bf16[3,256,512]{2,1,0:T(8,128)(2,1)S(1)} %get-tuple-element.17), channel_id=1, source_target_pairs={{0,2},{2,0},{1,3},{3,1},{4,6},{6,4},{5,7},{7,5},{8,10},{10,8},{9,1... | collective-permute-start | bytes 2359304 | tf_op jit(solution)/shard_map/ppermute | solution.py:511
  71.9 37.8 %collective-permute-start.4 = (bf16[3,256,512]{2,1,0:T(8,128)(2,1)}, bf16[3,256,512]{2,1,0:T(8,128)(2,1)}, u32[]{:S(2)}, u32[]{:S(2)}) collective-permute-start(bf16[3,256,512]{2,1,0:T(8,128)(2,1)} %combine.1.refs_4_), channel_id=1, source_target_pairs={{0,16},{16,0},{1,17},{17,1},{2,18},{18,2},{3,19},{19,3},{4,20},{20... | collective-permute-start | bytes 2359304 | tf_op jit(solution)/shard_map/ppermute | solution.py:525
  72.9 5.2 %collective-permute-start.5 = (bf16[4,512,128]{2,1,0:T(8,128)(2,1)}, bf16[4,512,128]{2,1,0:T(8,128)(2,1)}, u32[]{:S(2)}, u32[]{:S(2)}) collective-permute-start(bf16[4,512,128]{2,1,0:T(8,128)(2,1)} %last_rows.1), channel_id=1, source_target_pairs={{0,2},{2,0},{1,3},{3,1},{4,6},{6,4},{5,7},{7,5},{8,10},{10,8},{9,1... | collective-permute-start | bytes 1572872 | tf_op jit(solution)/shard_map/ppermute | solution.py:530
  73.9 4.1 %collective-permute-start.6 = (bf16[1,512,128]{2,1,0:T(8,128)(2,1)S(1)}, bf16[1,512,128]{2,1,0:T(8,128)(2,1)S(1)}, u32[]{:S(2)}, u32[]{:S(2)}) collective-permute-start(bf16[1,512,128]{2,1,0:T(8,128)(2,1)S(1)} %slice.4), channel_id=1, source_target_pairs={{2,16},{3,17},{6,20},{7,21},{10,24},{11,25},{14,28},{15,29}} | collective-permute-start | bytes 393224 | tf_op jit(solution)/shard_map/ppermute | solution.py:535
  87.4 22.3 %collective-permute-start.7 = (bf16[3,256,512]{2,1,0:T(8,128)(2,1)}, bf16[3,256,512]{2,1,0:T(8,128)(2,1)S(1)}, u32[]{:S(2)}, u32[]{:S(2)}) collective-permute-start(bf16[3,256,512]{2,1,0:T(8,128)(2,1)} %combine.1.refs_4_), channel_id=1, source_target_pairs={{0,2},{2,0},{1,3},{3,1},{4,6},{6,4},{5,7},{7,5},{8,10},{10,8},{9,1... | collective-permute-start | bytes 2359304 | tf_op jit(solution)/shard_map/ppermute | solution.py:541
  109.6 2.5 %collective-permute-start.8 = (bf16[3,256,512]{2,1,0:T(8,128)(2,1)}, bf16[3,256,512]{2,1,0:T(8,128)(2,1)S(1)}, u32[]{:S(2)}, u32[]{:S(2)}) collective-permute-start(bf16[3,256,512]{2,1,0:T(8,128)(2,1)} %collective-permute-done.4.refs_5_), channel_id=1, source_target_pairs={{0,2},{2,0},{1,3},{3,1},{4,6},{6,4},{5,7},{7,5},{8,10},{10,8},{9,1... | collective-permute-start | bytes 2359304 | tf_op jit(solution)/shard_map/ppermute | solution.py:542

commit v2 on v1

v2 whole, which is shorter than its diff:
```python
import math

import jax
import jax.numpy as jnp
from jax import lax
from jax.experimental import pallas as pl
from jax.experimental.pallas import tpu as pltpu
from jax.sharding import Mesh, PartitionSpec as P


HEADS = 8
HEAD_DIM = 128
WINDOW = 64
STEP_SIZE = 0.05
NORM_EPS = 1e-06
RATE_ROWS = 8
ANY = pl.BlockSpec(memory_space=pl.ANY)
VMEM = pl.BlockSpec(memory_space=pltpu.VMEM)
SMEM = pl.BlockSpec(memory_space=pltpu.SMEM)


def in_vmem(x):
    return pltpu.with_memory_space_constraint(x, pltpu.VMEM)


def in_hbm(x):
    return pltpu.with_memory_space_constraint(x, pltpu.HBM)


def cost(microseconds):
    return pl.CostEstimate(
        flops=int(microseconds * 4e6), bytes_accessed=1 << 20, transcendentals=0
    )


def params(mib=4):
    return pltpu.CompilerParams(vmem_limit_bytes=mib << 20)


def swap_pairs(count, stride):
    return [(i, i ^ stride) for i in range(count)]


def rms_rows(rows):
    wide = rows.astype(jnp.float32)
    scale = lax.rsqrt(jnp.mean(wide * wide, axis=1, keepdims=True) + NORM_EPS)
    return (wide * scale).astype(jnp.bfloat16)


def head_of(peer, lane, head_axis):
    return (peer % head_axis) * lane + peer // head_axis


def pack(place, key_rows, value_rows, rates_t, w_gate, w_up, w_down, lane, head_axis):
    rows, width = key_rows.shape
    size = width // HEADS
    piece, local, _ = w_gate.shape

    def kernel(place_ref, k_ref, v_ref, r_ref, g_ref, u_ref, d_ref, w_out_ref, *refs):
        out_refs, w_refs, (sem, w_sem) = refs[:HEADS], refs[HEADS : HEADS + 3], refs[HEADS + 3 :]
        loads = [
            pltpu.make_async_copy(src, dst, w_sem.at[i])
            for i, (src, dst) in enumerate(zip((g_ref, u_ref, d_ref), w_refs))
        ]
        for load in loads:
            load.start()
        moves = []
        heads = []
        for step, out_ref in enumerate(out_refs):
            head = head_of(place_ref[0] ^ step, lane, head_axis)
            heads.append(head)
            first = pl.multiple_of(head * size, size)
            for which, ref in enumerate((k_ref, v_ref)):
                move = pltpu.make_async_copy(
                    ref.at[:, pl.ds(first, size)],
                    out_ref.at[pl.ds(which * rows, rows), :],
                    sem.at[len(moves)],
                )
                move.start()
                moves.append(move)
        rates = r_ref[...].astype(jnp.float32)
        head_id = lax.broadcasted_iota(jnp.int32, rates.shape, 0)
        for head, out_ref in zip(heads, out_refs):
            row = jnp.sum(jnp.where(head_id == head, rates, 0.0), axis=0, keepdims=True)
            wide = jnp.broadcast_to(row, (RATE_ROWS, rows)).astype(jnp.bfloat16)
            for first in range(0, size, rows):
                out_ref[2 * rows :, first : first + rows] = wide
        for which, (load, ref) in enumerate(zip(loads, w_refs)):
            load.wait()
            for head in range(local):
                w_out_ref[head, which] = ref[:, head, :]
        for move in moves:
            move.wait()

    return pl.pallas_call(
        kernel,
        in_specs=[SMEM, ANY, ANY, VMEM, ANY, ANY, ANY],
        out_specs=[VMEM] * (1 + HEADS),
        out_shape=[pltpu.HBM((local, 3, piece, size), jnp.bfloat16)]
        + [pltpu.VMEM((2 * rows + RATE_ROWS, size), jnp.bfloat16)] * HEADS,
        scratch_shapes=[pltpu.VMEM(w_gate.shape, w_gate.dtype)] * 3
        + [pltpu.SemaphoreType.DMA((HEADS * 2,)), pltpu.SemaphoreType.DMA((3,))],
        compiler_params=params(),
        name="pack",
    )(place, *[in_hbm(x) for x in (key_rows, value_rows, rates_t, w_gate, w_up, w_down)])


def pack_queries(place, queries, lane, head_axis):
    rows, width = queries.shape
    size = width // HEADS

    def kernel(place_ref, q_ref, *refs):
        out_refs, sem = refs[:HEADS], refs[HEADS]
        moves = []
        for step, out_ref in enumerate(out_refs):
            head = head_of(place_ref[0] ^ step, lane, head_axis)
            first = pl.multiple_of(head * size, size)
            move = pltpu.make_async_copy(q_ref.at[:, pl.ds(first, size)], out_ref, sem.at[step])
            move.start()
            moves.append(move)
        for move in moves:
            move.wait()

    return pl.pallas_call(
        kernel,
        in_specs=[SMEM, ANY],
        out_specs=[VMEM] * HEADS,
        out_shape=[pltpu.VMEM((rows, size), jnp.bfloat16)] * HEADS,
        scratch_shapes=[pltpu.SemaphoreType.DMA((HEADS,))],
        compiler_params=params(),
        name="pack_queries",
    )(place, in_hbm(queries))


def unpack_columns(place, back, lane, head_axis):
    rows, size = back[0].shape

    def kernel(place_ref, *refs):
        back_refs, out_ref, sem = refs[:HEADS], refs[HEADS], refs[HEADS + 1]
        moves = []
        for step, ref in enumerate(back_refs):
            head = head_of(place_ref[0] ^ step, lane, head_axis)
            first = pl.multiple_of(head * size, size)
            move = pltpu.make_async_copy(ref, out_ref.at[:, pl.ds(first, size)], sem.at[step])
            move.start()
            moves.append(move)
        for move in moves:
            move.wait()

    return pl.pallas_call(
        kernel,
        in_specs=[SMEM] + [VMEM] * HEADS,
        out_specs=ANY,
        out_shape=pltpu.HBM((rows, HEADS * size), back[0].dtype),
        scratch_shapes=[pltpu.SemaphoreType.DMA((HEADS,))],
        compiler_params=params(),
        name="unpack_columns",
    )(place, *[in_vmem(x) for x in back])


def place_pieces(spot_ref, piece_refs, out_ref, outer, lane, inner):
    if len(piece_refs) == 1:
        out_ref[...] = piece_refs[0][...]
        return
    piece = piece_refs[0].shape[2]
    a, c = spot_ref[0], spot_ref[1]
    spots = [(a, c), (outer - 1 - a, c), (a, inner - 1 - c), (outer - 1 - a, inner - 1 - c)]
    for (at_a, at_c), ref in zip(spots, piece_refs):
        for l in range(lane):
            first = pl.multiple_of(((at_a * lane + l) * inner + at_c) * piece, piece)
            for which in range(3):
                out_ref[which, pl.ds(first, piece), :] = ref[l, which]


def gradients(spot, place, received, pieces, rows, outer, lane, inner, per_run):
    blocks = len(received)
    size = received[0].shape[1]
    runs = blocks // per_run
    half = size // inner
    count = blocks * rows
    group = 2 if blocks % 2 == 0 else 1
    span = group * rows

    def kernel(spot_ref, place_ref, *refs):
        kv_refs, refs = refs[:blocks], refs[blocks:]
        piece_refs, refs = refs[: len(pieces)], refs[len(pieces) :]
        keep_ref, send_ref, tail_ref, last_ref, w_ref = refs[:5]
        kn_ref, hid_ref, tgt_ref, gg_ref, ug_ref, all_ref = refs[5:]
        place_pieces(spot_ref, piece_refs, w_ref, outer, lane, inner)
        for g in range(blocks // group):
            here = slice(g * span, (g + 1) * span)
            mine = range(g * group, (g + 1) * group)

            def stacked(first):
                return jnp.concatenate([kv_refs[b][first : first + rows, :] for b in mine], axis=0)

            key_norm = rms_rows(stacked(0))
            values = stacked(rows).astype(jnp.float32)
            rates = []
            for b in mine:
                row = kv_refs[b][2 * rows : 2 * rows + 1, :rows].astype(jnp.float32)
                rates.append(jnp.broadcast_to(row, (rows, rows)).T)
            rate_columns = jnp.concatenate([jnp.concatenate(rates, axis=0)] * (size // rows), axis=1)
            target = (-rate_columns * values).astype(jnp.bfloat16)
            tgt_ref[here, :] = target
            gate_pre = jnp.dot(key_norm, w_ref[0], preferred_element_type=jnp.float32)
            up_pre = jnp.dot(key_norm, w_ref[1], preferred_element_type=jnp.float32)
            hidden_grad = lax.dot_general(
                target, w_ref[2], (((1,), (1,)), ((), ())), preferred_element_type=jnp.float32
            )
            sigma_gate = jax.nn.sigmoid(gate_pre)
            silu_gate = gate_pre * sigma_gate
            hidden = (silu_gate * up_pre).astype(jnp.bfloat16)
            for part in range(inner):
                columns = slice(part * half, (part + 1) * half)
                kn_ref[part, here, :] = key_norm[:, columns]
                hid_ref[part, here, :] = hidden[:, columns]
            gg_ref[here, :] = (
                hidden_grad * up_pre * sigma_gate * (1.0 + gate_pre * (1.0 - sigma_gate))
            ).astype(jnp.bfloat16)
            ug_ref[here, :] = (hidden_grad * silu_gate).astype(jnp.bfloat16)

        def total(left_ref, right_ref, part):
            return lax.dot_general(
                left_ref[part],
                right_ref[...],
                (((0,), (0,)), ((), ())),
                preferred_element_type=jnp.float32,
            )

        own = spot_ref[1]
        pairs = ((kn_ref, gg_ref), (kn_ref, ug_ref), (hid_ref, tgt_ref))
        for which, (left_ref, right_ref) in enumerate(pairs):
            send_ref[which] = total(left_ref, right_ref, inner - 1 - own).astype(jnp.bfloat16)
            keep_ref[which] = total(left_ref, right_ref, own)
        for step, ref in enumerate(kv_refs):
            block = place_ref[0] ^ step
            for which in range(2):
                end = (which + 1) * rows
                all_ref[block, which * WINDOW : (which + 1) * WINDOW, :] = ref[end - WINDOW : end, :]
        for run in range(runs):
            tail_ref[run] = all_ref[(run + 1) * per_run - 1]
        last_ref[0] = all_ref[blocks - 1]

    return pl.pallas_call(
        kernel,
        in_specs=[SMEM] * 2 + [VMEM] * (blocks + len(pieces)),
        out_specs=[VMEM] * 5,
        out_shape=[
            pltpu.VMEM((3, half, size), jnp.float32),
            pltpu.VMEM((3, half, size), jnp.bfloat16),
            pltpu.VMEM((runs, 2 * WINDOW, size), jnp.bfloat16),
            pltpu.VMEM((1, 2 * WINDOW, size), jnp.bfloat16),
            pltpu.VMEM((3, size, size), jnp.bfloat16),
        ],
        scratch_shapes=[
            pltpu.VMEM((inner, count, half), jnp.bfloat16),
            pltpu.VMEM((inner, count, half), jnp.bfloat16),
            pltpu.VMEM((count, size), jnp.bfloat16),
            pltpu.VMEM((count, size), jnp.bfloat16),
            pltpu.VMEM((count, size), jnp.bfloat16),
            pltpu.VMEM((blocks, 2 * WINDOW, size), jnp.bfloat16),
        ],
        compiler_params=params(20),
        cost_estimate=cost(6),
        name="gradients",
    )(spot, place, *[in_vmem(r) for r in received], *[in_vmem(p) for p in pieces])


def combine(keep, got):
    def kernel(keep_ref, got_ref, out_ref):
        out_ref[...] = (keep_ref[...] + got_ref[...].astype(jnp.float32)).astype(jnp.bfloat16)

    return pl.pallas_call(
        kernel,
        in_specs=[VMEM, VMEM],
        out_specs=VMEM,
        out_shape=pltpu.VMEM(keep.shape, jnp.bfloat16),
        compiler_params=params(),
        name="combine",
    )(in_vmem(keep), in_vmem(got))


def attention(spot, place, queries, received, around, from_outer, old, per_run):
    blocks = len(queries)
    rows, width = queries[0].shape
    span = 2 * WINDOW

    def kernel(spot_ref, place_ref, w_ref, around_ref, outer_ref, *refs):
        q_refs, kv_refs, refs = refs[:blocks], refs[blocks : 2 * blocks], refs[2 * blocks :]
        att_ref, qn_ref, norm_ref, kv_ref, q_ref = refs
        for step in range(blocks):
            kv_ref[place_ref[0] ^ step] = kv_refs[step][: 2 * rows, :]
            q_ref[place_ref[0] ^ step] = q_refs[step][...]
        for which in range(3):
            for first in range(0, width, HEAD_DIM):
                previous = w_ref[which, first : first + HEAD_DIM, :].astype(jnp.float32)
                norm = jnp.sqrt(jnp.mean(previous * previous, axis=1, keepdims=True))
                norm_ref[which, first : first + HEAD_DIM, :] = jnp.broadcast_to(
                    norm, (HEAD_DIM, HEAD_DIM)
                )
        on_first = jnp.where(spot_ref[1] == 0, 1, 0)
        begins = jnp.where(spot_ref[0] == 0, on_first, 0)
        row_id = lax.broadcasted_iota(jnp.int32, (WINDOW, span), 0)
        key_id = lax.broadcasted_iota(jnp.int32, (WINDOW, span), 1)
        allowed = (key_id <= row_id + WINDOW) & (key_id > row_id)
        bias = jnp.where(allowed, 0.0, -1e30)
        first_key = jnp.where(begins == 1, WINDOW, 0)
        first_bias = jnp.where(allowed & (key_id >= first_key), 0.0, -1e30)
        for b in range(blocks):
            qn_ref[b] = rms_rows(q_ref[b])
            pieces = [
                (part, first)
                for part in range(rows // WINDOW)
                for first in range(0, width, HEAD_DIM)
            ]

            def keys_or_values(which, part, first):
                columns = slice(first, first + HEAD_DIM)
                end = which * rows + (part + 1) * WINDOW
                if part:
                    return kv_ref[b, end - span : end, columns]
                before = slice(which * WINDOW, (which + 1) * WINDOW)
                if b % per_run:
                    after = (which + 1) * rows
                    tail = kv_ref[b - 1, after - WINDOW : after, columns]
                elif b:
                    tail = around_ref[b // per_run - on_first, before, columns]
                else:
                    tail = jnp.where(
                        on_first == 1, outer_ref[0, before, columns], around_ref[0, before, columns]
                    )
                return jnp.concatenate([tail, kv_ref[b, end - WINDOW : end, columns]], axis=0)

            masked = []
            for part, first in pieces:
                scores = lax.dot_general(
                    q_ref[b, part * WINDOW : (part + 1) * WINDOW, first : first + HEAD_DIM],
                    keys_or_values(0, part, first),
                    (((1,), (1,)), ((), ())),
                    preferred_element_type=jnp.float32,
                )
                masked.append(
                    scores * (1.0 / math.sqrt(HEAD_DIM)) + (bias if b or part else first_bias)
                )
            masked = jnp.concatenate(masked, axis=0)
            maximum = jnp.max(masked, axis=1, keepdims=True)
            exp_scores = jnp.exp(masked - maximum)
            scale = 1.0 / jnp.sum(exp_scores, axis=1, keepdims=True)
            weights = exp_scores.astype(jnp.bfloat16)
            for i, (part, first) in enumerate(pieces):
                here = slice(i * WINDOW, (i + 1) * WINDOW)
                mixed = jnp.dot(
                    weights[here],
                    keys_or_values(1, part, first),
                    preferred_element_type=jnp.float32,
                )
                att_ref[b, part * WINDOW : (part + 1) * WINDOW, first : first + HEAD_DIM] = (
                    mixed * scale[here]
                )

    return pl.pallas_call(
        kernel,
        in_specs=[SMEM] * 2 + [VMEM] * (3 + 2 * blocks),
        out_specs=[VMEM] * 3,
        out_shape=[
            pltpu.VMEM((blocks, rows, width), jnp.float32),
            pltpu.VMEM((blocks, rows, width), jnp.bfloat16),
            pltpu.VMEM((3, width, HEAD_DIM), jnp.float32),
        ],
        scratch_shapes=[
            pltpu.VMEM((blocks, 2 * rows, width), jnp.bfloat16),
            pltpu.VMEM((blocks, rows, width), jnp.bfloat16),
        ],
        compiler_params=params(10),
        cost_estimate=cost(6),
        name="attention",
    )(
        spot,
        place,
        in_vmem(old),
        in_vmem(around),
        in_vmem(from_outer),
        *[in_vmem(q) for q in queries],
        *[in_vmem(r) for r in received],
    )


def update_and_apply(spot, place, old, norms, sums, query_norm, attended):
    blocks, rows, size = query_norm.shape
    halves = len(sums) // 2
    half = size // halves
    group = 2 if blocks % 2 == 0 else 1

    def kernel(spot_ref, place_ref, w_ref, norm_ref, *refs):
        sum_refs, refs = refs[: 2 * halves], refs[2 * halves :]
        q_ref, a_ref, out_refs, (total_ref, new_ref) = refs[0], refs[1], refs[2:-2], refs[-2:]
        squares = jnp.zeros((8, size), jnp.float32)
        for part in range(halves):
            place = spot_ref[1] if part == 0 else halves - 1 - spot_ref[1]
            for which in range(3):
                total = sum_refs[2 * part][which].astype(jnp.float32) + sum_refs[2 * part + 1][
                    which
                ].astype(jnp.float32)
                total_ref[place, which] = total
                squares = squares + jnp.sum(
                    (total * total).reshape(half // 8, 8, size), axis=0
                )
        norm_scale = lax.rsqrt(
            jnp.sum(squares, axis=(0, 1), keepdims=True) / (3 * size * size) + NORM_EPS
        )
        scale = STEP_SIZE * norm_scale
        for part in range(halves):
            for which in range(3):
                here = slice(part * half, (part + 1) * half)
                previous = w_ref[which, here, :].astype(jnp.float32)
                stepped = previous - scale * total_ref[part, which]
                factor = norm_ref[which, here, 0:1] * lax.rsqrt(
                    jnp.mean(stepped * stepped, axis=1, keepdims=True) + NORM_EPS
                )
                new_ref[which, here, :] = (stepped * factor).astype(jnp.bfloat16)
        for g in range(blocks // group):
            steps = range(g * group, (g + 1) * group)
            mine = [place_ref[0] ^ step for step in steps]
            query = jnp.concatenate([q_ref[b] for b in mine], axis=0)
            query_gate = jnp.dot(query, new_ref[0], preferred_element_type=jnp.float32)
            query_up = jnp.dot(query, new_ref[1], preferred_element_type=jnp.float32)
            query_hidden = (query_gate * jax.nn.sigmoid(query_gate) * query_up).astype(
                jnp.bfloat16
            )
            fast = jnp.dot(query_hidden, new_ref[2], preferred_element_type=jnp.float32).astype(
                jnp.bfloat16
            )
            for i, (step, b) in enumerate(zip(steps, mine)):
                out_refs[step][...] = (
                    a_ref[b] + fast[i * rows : (i + 1) * rows, :].astype(jnp.float32)
                ).astype(jnp.bfloat16)

    return pl.pallas_call(
        kernel,
        in_specs=[SMEM] * 2 + [VMEM] * (len(sums) + 4),
        out_specs=[VMEM] * blocks,
        out_shape=[pltpu.VMEM((rows, size), jnp.bfloat16)] * blocks,
        scratch_shapes=[
            pltpu.VMEM((halves, 3, half, size), jnp.float32),
            pltpu.VMEM((3, size, size), jnp.bfloat16),
        ],
        compiler_params=params(16),
        cost_estimate=cost(6),
        name="update_and_apply",
    )(
        spot,
        place,
        in_vmem(old),
        in_vmem(norms),
        *[in_vmem(s) for s in sums],
        in_vmem(query_norm),
        in_vmem(attended),
    )


def gather_rows(mine, axis, count, index, order_axis):
    if count & (count - 1):
        return lax.all_gather(mine, axis, axis=order_axis, tiled=True)
    stride = 1
    while stride < count:
        theirs = lax.ppermute(mine, axis, swap_pairs(count, stride))
        low = (index // stride) % 2 == 0
        mine = jnp.concatenate(
            [jnp.where(low, mine, theirs), jnp.where(low, theirs, mine)], order_axis
        )
        stride *= 2
    return mine


def make_shards(outer, lane, inner, head_axis):
    group = ("lane", "head")

    def shards(queries, key_rows, value_rows, step_rates, w_gate, w_up, w_down):
        rows, width = queries.shape
        size = width // HEADS
        a = lax.axis_index("outer")
        c = lax.axis_index("inner")
        spot = jnp.stack([a, c]).astype(jnp.int32)
        place = jnp.reshape(lax.axis_index(group), (1,)).astype(jnp.int32)
        spot, place, w_gate = lax.optimization_barrier((spot, place, w_gate))

        own, *packed = pack(
            place,
            key_rows,
            value_rows,
            jnp.transpose(step_rates),
            w_gate,
            w_up,
            w_down,
            lane,
            head_axis,
        )
        if lane > 1:
            own = lax.all_to_all(own, "lane", split_axis=0, concat_axis=0, tiled=True)

        def exchange(chunks):
            got = [chunks[0]]
            for step in range(1, HEADS):
                got.append(lax.ppermute(chunks[step], group, swap_pairs(HEADS, step)))
            return got

        kv = exchange(packed)
        qs = pack_queries(place, queries, lane, head_axis)
        qs = exchange(qs)

        if outer == 2 and inner == 2:
            other = lax.ppermute(own, "outer", swap_pairs(outer, 1))
            own_beside = lax.ppermute(own, "inner", swap_pairs(inner, 1))
            other_beside = lax.ppermute(other, "inner", swap_pairs(inner, 1))
            pieces = [own, other, own_beside, other_beside]
        else:
            old = gather_rows(own[None], "outer", outer, a, 0)[:, :, None]
            old = gather_rows(old, "inner", inner, c, 2)
            pieces = [jnp.transpose(old, (3, 0, 1, 2, 4, 5)).reshape(3, size, size)]

        keep, send, tails, last, old = gradients(
            spot, place, kv, pieces, rows, outer, lane, inner, head_axis
        )
        if inner > 1:
            got = lax.ppermute(send, "inner", swap_pairs(inner, 1))
            half = combine(keep, got)
        else:
            half = keep.astype(jnp.bfloat16)
        mine, theirs = half, jnp.zeros_like(half)
        if outer & (outer - 1):
            mine = lax.psum(half, "outer")
        else:
            stride = 1
            while stride < outer:
                if stride > 1:
                    mine = (mine.astype(jnp.float32) + theirs.astype(jnp.float32)).astype(
                        jnp.bfloat16
                    )
                theirs = lax.ppermute(mine, "outer", swap_pairs(outer, stride))
                stride *= 2
        around = tails
        if inner > 1:
            around = lax.ppermute(tails, "inner", [(i, (i + 1) % inner) for i in range(inner)])
        pairs = [
            (i * inner + inner - 1, (i + 1) * inner) for i in range(outer - 1)
        ]
        from_outer = lax.ppermute(last, ("outer", "inner"), pairs) if pairs else last
        attended, query_norm, norms = attention(
            spot, place, qs, kv, around, from_outer, old, head_axis
        )

        theirs, attended, query_norm, norms = lax.optimization_barrier(
            (theirs, attended, query_norm, norms)
        )
        sums = [mine, theirs]
        if inner > 1:
            sums.append(lax.ppermute(mine, "inner", swap_pairs(inner, 1)))
            sums.append(lax.ppermute(theirs, "inner", swap_pairs(inner, 1)))

        out = update_and_apply(spot, place, old, norms, sums, query_norm, attended)
        return unpack_columns(place, exchange(out), lane, head_axis)

    return shards


def solution(mesh):
    seq, head_axis = mesh.shape["seq"], mesh.shape["head"]
    lane = HEADS // head_axis
    inner = 2 if (seq // lane) % 2 == 0 else 1
    outer = seq // lane // inner
    names = ("outer", "lane", "inner", "head")
    split = Mesh(mesh.devices.reshape(outer, lane, inner, head_axis), names)
    rows = P(names, None)
    weights = P(names[:3], names[3], None)
    shards = make_shards(outer, lane, inner, head_axis)

    return jax.shard_map(
        shards,
        mesh=split,
        in_specs=(rows, rows, rows, rows, weights, weights, weights),
        out_specs=rows,
        check_vma=False,
    )
```

time: 151 us -> 137 us (0.907)
  waiting for transfers between devices: 49.9 us -> 68.1 us
  blocking collectives: 30.4 us -> 12.4 us
  Pallas kernels: 33.5 us -> 20.2 us
  local copies, waits for them, and re-layouts: 1.59 us -> 0 us
    ppermute x0 -> x21, waiting for transfers between devices: none -> 55.2 us  [exchange(): got.append(lax.ppermute(chunks[step], group, swap_pairs(HEADS, step)))]
    ppermute x0 -> x21, starting transfers between devices: none -> 30.2 us  [exchange(): got.append(lax.ppermute(chunks[step], group, swap_pairs(HEADS, step)))]
    ppermute x1, waiting for transfers between devices: 31.6 us -> 7.74 us  [shards(): other = lax.ppermute(own, 'outer', swap_pairs(outer, 1))]
    all_to_all x1, blocking collectives: 30.4 us -> 12.4 us  [shards(): own = lax.all_to_all(own, 'lane', split_axis=0, concat_axis=0, tiled=True)]
    all_to_all x3 -> x0, starting transfers between devices: 16 us -> none  [the longest x1 6.94 us: shards(): qs = lax.all_to_all(qs, group, split_axis=0, concat_axis=0, tiled=True)]
    ppermute x1, starting transfers between devices: 15.1 us -> 0.08 us  [shards(): sums.append(lax.ppermute(mine, 'inner', swap_pairs(inner, 1)))]
    pallas_call x8 -> x6, Pallas kernels: 32.5 us -> 20 us  [the longest x1 5.32 us: gradients(): pl.pallas_call(kernel, in_specs=[SMEM] * 2 + [VMEM] * (blocks + len(piece...]
    ppermute x1, waiting for transfers between devices: 7.16 us -> 0.01 us  [shards(): theirs = lax.ppermute(mine, 'outer', swap_pairs(outer, stride))]
  transfers between devices with their start and end apart: 12 -> 30, of which waited for: 6 -> 19; matrix products, arithmetic and copies ran while one was open for 1% -> 0% of each run, Pallas kernels for 15% -> 4%
where the time goes in v2:
time: 137 us
  waiting for transfers between devices  68.1 us (50%)
  starting transfers between devices  35.7 us (26%)
  Pallas kernels  20.2 us (15%)
  blocking collectives  12.4 us (9%)
    ppermute x21, waiting for transfers between devices, exchange(): got.append(lax.ppermute(chunks[step], group, swap_pairs(HEADS, step)))  55.2 us
    ppermute x21, starting transfers between devices, exchange(): got.append(lax.ppermute(chunks[step], group, swap_pairs(HEADS, step)))  30.2 us
    all_to_all x1, blocking collectives, shards(): own = lax.all_to_all(own, 'lane', split_axis=0, concat_axis=0, tiled=True)  12.4 us
    ppermute x1, waiting for transfers between devices, shards(): other = lax.ppermute(own, 'outer', swap_pairs(outer, 1))  7.74 us
    pallas_call x1, Pallas kernels, gradients(): pl.pallas_call(kernel, in_specs=[SMEM] * 2 + [VMEM] * (blocks + len(piece...  5.32 us
    pallas_call x1, Pallas kernels, update_and_apply(): pl.pallas_call(kernel, in_specs=[SMEM] * 2 + [VMEM] * (len(sums) + 4), ou...  4.38 us
    pallas_call x1, Pallas kernels, attention(): pl.pallas_call(kernel, in_specs=[SMEM] * 2 + [VMEM] * (3 + 2 * blocks), o...  4.07 us
    pallas_call x1, Pallas kernels, pack(): pl.pallas_call(kernel, in_specs=[SMEM, ANY, ANY, VMEM, ANY, ANY, ANY], ou...  3.88 us
  transfers between devices with their start and end apart: 30, of which 19 were waited for; matrix products, arithmetic and copies ran while one was open for 0% of the time, Pallas kernels for 4%

profile of v2, /device:TPU:0, one launch (start us, length us, event | category | flops | bytes accessed | tf_op | source)
XLA Modules:
  0.0 136.7 jit_solution(4654105883645729955)
XLA Ops:
  0.1 3.9 %pack.1 = (bf16[4,3,32,512]{3,2,1,0:T(8,128)(2,1)}, bf16[264,512]{1,0:T(8,128)(2,1)S(1)}, bf16[264,512]{1,0:T(8,128)(2,1)S(1)}, bf16[264,512]{1,0:T(8,128)(2,1)S...) custom-call(s32[1]{0:T(128)} %bitcast.2.place_ref, ...), custom_call_target="tpu_custom_call" | custom-call | tf_op jit(solution)/shard_map/pack/pallas_call | solution.py:95
  4.0 12.4 %all_to_all.5.refs_8_ = bf16[4,3,32,512]{3,2,1,0:T(8,128)(2,1)S(1)} all-to-all(bf16[4,3,32,512]{3,2,1,0:T(8,128)(2,1)} %get-tuple-element.56), channel_id=1, replica_groups=mesh['outer'=2,'lane'=4,'inner'=2,'head'=2] {'lane'}, dimensions={0} | all-to-all | bytes 786432 | tf_op jit(solution)/shard_map/all_to_all | solution.py:500
  16.3 2.6 %collective-permute-start.7 = (bf16[4,3,32,512]{3,2,1,0:T(8,128)(2,1)S(1)}, bf16[4,3,32,512]{3,2,1,0:T(8,128)(2,1)S(1)}, u32[]{:S(2)}, u32[]{:S(2)}) collective-permute-start(bf16[4,3,32,512]{3,2,1,0:T(8,128)(2,1)S(1)} %all_to_all.5.refs_8_), channel_id=1, source_target_pairs={{0,16},{16,0},{1,17},{17,1},{2,18},{18,2},{3,19},{19,3},{4,20},{20... | collective-permute-start | bytes 1179656 | tf_op jit(solution)/shard_map/ppermute | solution.py:513
  18.9 1.5 %collective-permute-start = (bf16[264,512]{1,0:T(8,128)(2,1)S(1)}, bf16[264,512]{1,0:T(8,128)(2,1)S(1)}, u32[]{:S(2)}, u32[]{:S(2)}) collective-permute-start(bf16[264,512]{1,0:T(8,128)(2,1)S(1)} %get-tuple-element.49), channel_id=1, source_target_pairs={{0,1},{1,0},{4,5},{5,4},{8,9},{9,8},{12,13},{13,12},{2,3},{3,2},{6... | collective-permute-start | bytes 811016 | tf_op jit(solution)/shard_map/ppermute | solution.py:505
  20.5 0.9 collective-permute-start.1
  21.4 1.1 collective-permute-start.2
  22.4 0.9 collective-permute-start.3
  23.3 4.1 %collective-permute-done.refs_1_.refs_9_ = bf16[264,512]{1,0:T(8,128)(2,1)S(1)} collective-permute-done((bf16[264,512]{1,0:T(8,128)(2,1)S(1)}, bf16[264,512]{1,0:T(8,128)(2,1)S(1)}, u32[]{:S(2)}, u32[]{:S(2)}) %collective-permute-start) | collective-permute-done | bytes 270368 | tf_op jit(solution)/shard_map/ppermute | solution.py:505
  27.4 7.7 %collective-permute-done.7.refs_9_ = bf16[4,3,32,512]{3,2,1,0:T(8,128)(2,1)S(1)} collective-permute-done((bf16[4,3,32,512]{3,2,1,0:T(8,128)(2,1)S(1)}, bf16[4,3,32,512]{3,2,1,0:T(8,128)(2,1)S(1)}, u32[]{:S(2)}, u32[]{:S(2)}) %collective-permute-start.7) | collective-permute-done | bytes 393248 | tf_op jit(solution)/shard_map/ppermute | solution.py:513
  35.1 1.3 collective-permute-start.4
  36.5 2.3 %collective-permute-start.5 = (bf16[264,512]{1,0:T(8,128)(2,1)S(1)}, bf16[264,512]{1,0:T(8,128)(2,1)S(1)}, u32[]{:S(2)}, u32[]{:S(2)}) collective-permute-start(bf16[264,512]{1,0:T(8,128)(2,1)S(1)} %get-tuple-element.54), channel_id=1, source_target_pairs={{0,12},{1,13},{4,8},{5,9},{8,4},{9,5},{12,0},{13,1},{2,14},{3,15},... | collective-permute-start | bytes 811016 | tf_op jit(solution)/shard_map/ppermute | solution.py:505
  38.8 0.5 collective-permute-start.6
  39.4 6.0 %collective-permute-done.4.refs_5_.refs_13_ = bf16[264,512]{1,0:T(8,128)(2,1)S(1)} collective-permute-done((bf16[264,512]{1,0:T(8,128)(2,1)S(1)}, bf16[264,512]{1,0:T(8,128)(2,1)S(1)}, u32[]{:S(2)}, u32[]{:S(2)}) %collective-permute-start.4) | collective-permute-done | bytes 270368 | tf_op jit(solution)/shard_map/ppermute | solution.py:505
  45.4 6.6 %collective-permute-done.5.refs_6_.refs_14_ = bf16[264,512]{1,0:T(8,128)(2,1)S(1)} collective-permute-done((bf16[264,512]{1,0:T(8,128)(2,1)S(1)}, bf16[264,512]{1,0:T(8,128)(2,1)S(1)}, u32[]{:S(2)}, u32[]{:S(2)}) %collective-permute-start.5) | collective-permute-done | bytes 270368 | tf_op jit(solution)/shard_map/ppermute | solution.py:505
  52.0 5.3 %collective-permute-done.6.refs_7_.refs_15_ = bf16[264,512]{1,0:T(8,128)(2,1)S(1)} collective-permute-done((bf16[264,512]{1,0:T(8,128)(2,1)S(1)}, bf16[264,512]{1,0:T(8,128)(2,1)S(1)}, u32[]{:S(2)}, u32[]{:S(2)}) %collective-permute-start.6) | collective-permute-done | bytes 270368 | tf_op jit(solution)/shard_map/ppermute | solution.py:505
  57.2 5.3 %gradients.1 = (f32[3,256,512]{2,1,0:T(8,128)S(1)}, bf16[3,256,512]{2,1,0:T(8,128)(2,1)S(1)}, bf16[4,128,512]{2,1,0:T(8,128)(2,1)S(1)}, bf16[1,128,512]{2,1,0:T(8,128)(2,1)S(1)}, bf16[3,512,512]{2,1,0:T(8,128)(2,1)S(1)}) custom-call(s32[2]{0:T(128)S(1)} %pad_add_fusion.spot_ref, s32[1]{0:T(128)} %bitcast.2.place_ref, ...), custom_call_target="tpu_custom_call" | custom-call | flops 24000000 | bytes 1048576 | tf_op jit(solution)/shard_map/gradients/pallas_call | solution.py:245
  62.6 2.3 %collective-permute-done.10.got_ref = bf16[3,256,512]{2,1,0:T(8,128)(2,1)S(1)} collective-permute-done((bf16[3,256,512]{2,1,0:T(8,128)(2,1)S(1)}, bf16[3,256,512]{2,1,0:T(8,128)(2,1)S(1)}, u32[]{:S(2)}, u32[]{:S(2)}) %collective-permute-start.10) | collective-permute-done | bytes 786464 | tf_op jit(solution)/shard_map/ppermute | solution.py:526
  65.1 1.4 %collective-permute-start.11 = (bf16[3,256,512]{2,1,0:T(8,128)(2,1)S(1)}, bf16[3,256,512]{2,1,0:T(8,128)(2,1)S(1)}, u32[]{:S(2)}, u32[]{:S(2)}) collective-permute-start(bf16[3,256,512]{2,1,0:T(8,128)(2,1)S(1)} %combine.1.refs_0_), channel_id=1, source_target_pairs={{0,16},{16,0},{1,17},{17,1},{2,18},{18,2},{3,19},{19,3},{4,20},{20... | collective-permute-start | bytes 2359304 | tf_op jit(solution)/shard_map/ppermute | solution.py:540
  66.5 1.4 pack_queries.1
  67.9 0.6 collective-permute-start.14
  68.4 1.5 %collective-permute-start.15 = (bf16[128,512]{1,0:T(8,128)(2,1)S(1)}, bf16[128,512]{1,0:T(8,128)(2,1)S(1)}, u32[]{:S(2)}, u32[]{:S(2)}) collective-permute-start(bf16[128,512]{1,0:T(8,128)(2,1)S(1)} %get-tuple-element.64), channel_id=1, source_target_pairs={{0,4},{1,5},{4,0},{5,1},{8,12},{9,13},{12,8},{13,9},{2,6},{3,7},{6... | collective-permute-start | bytes 393224 | tf_op jit(solution)/shard_map/ppermute | solution.py:505
  69.9 1.5 %collective-permute-start.16 = (bf16[128,512]{1,0:T(8,128)(2,1)S(1)}, bf16[128,512]{1,0:T(8,128)(2,1)S(1)}, u32[]{:S(2)}, u32[]{:S(2)}) collective-permute-start(bf16[128,512]{1,0:T(8,128)(2,1)S(1)} %get-tuple-element.65), channel_id=1, source_target_pairs={{0,5},{1,4},{4,1},{5,0},{8,13},{9,12},{12,9},{13,8},{2,7},{3,6},{6... | collective-permute-start | bytes 393224 | tf_op jit(solution)/shard_map/ppermute | solution.py:505
  71.4 2.4 %collective-permute-done.14.refs_1_ = bf16[128,512]{1,0:T(8,128)(2,1)S(1)} collective-permute-done((bf16[128,512]{1,0:T(8,128)(2,1)S(1)}, bf16[128,512]{1,0:T(8,128)(2,1)S(1)}, u32[]{:S(2)}, u32[]{:S(2)}) %collective-permute-start.14) | collective-permute-done | bytes 131104 | tf_op jit(solution)/shard_map/ppermute | solution.py:505
  73.8 1.7 %collective-permute-start.17 = (bf16[128,512]{1,0:T(8,128)(2,1)S(1)}, bf16[128,512]{1,0:T(8,128)(2,1)S(1)}, u32[]{:S(2)}, u32[]{:S(2)}) collective-permute-start(bf16[128,512]{1,0:T(8,128)(2,1)S(1)} %get-tuple-element.66), channel_id=1, source_target_pairs={{0,8},{1,9},{4,12},{5,13},{8,0},{9,1},{12,4},{13,5},{2,10},{3,11},... | collective-permute-start | bytes 393224 | tf_op jit(solution)/shard_map/ppermute | solution.py:505
  75.5 1.8 %collective-permute-start.18 = (bf16[128,512]{1,0:T(8,128)(2,1)S(1)}, bf16[128,512]{1,0:T(8,128)(2,1)S(1)}, u32[]{:S(2)}, u32[]{:S(2)}) collective-permute-start(bf16[128,512]{1,0:T(8,128)(2,1)S(1)} %get-tuple-element.67), channel_id=1, source_target_pairs={{0,9},{1,8},{4,13},{5,12},{8,1},{9,0},{12,5},{13,4},{2,11},{3,10},... | collective-permute-start | bytes 393224 | tf_op jit(solution)/shard_map/ppermute | solution.py:505
  77.8 2.6 %collective-permute-start.19 = (bf16[128,512]{1,0:T(8,128)(2,1)S(1)}, bf16[128,512]{1,0:T(8,128)(2,1)S(1)}, u32[]{:S(2)}, u32[]{:S(2)}) collective-permute-start(bf16[128,512]{1,0:T(8,128)(2,1)S(1)} %get-tuple-element.68), channel_id=1, source_target_pairs={{0,12},{1,13},{4,8},{5,9},{8,4},{9,5},{12,0},{13,1},{2,14},{3,15},... | collective-permute-start | bytes 393224 | tf_op jit(solution)/shard_map/ppermute | solution.py:505
  80.4 6.9 %collective-permute-done.17.refs_4_ = bf16[128,512]{1,0:T(8,128)(2,1)S(1)} collective-permute-done((bf16[128,512]{1,0:T(8,128)(2,1)S(1)}, bf16[128,512]{1,0:T(8,128)(2,1)S(1)}, u32[]{:S(2)}, u32[]{:S(2)}) %collective-permute-start.17) | collective-permute-done | bytes 131104 | tf_op jit(solution)/shard_map/ppermute | solution.py:505
  87.3 3.3 %collective-permute-start.20 = (bf16[128,512]{1,0:T(8,128)(2,1)S(1)}, bf16[128,512]{1,0:T(8,128)(2,1)S(1)}, u32[]{:S(2)}, u32[]{:S(2)}) collective-permute-start(bf16[128,512]{1,0:T(8,128)(2,1)S(1)} %get-tuple-element.69), channel_id=1, source_target_pairs={{0,13},{1,12},{4,9},{5,8},{8,5},{9,4},{12,1},{13,0},{2,15},{3,14},... | collective-permute-start | bytes 393224 | tf_op jit(solution)/shard_map/ppermute | solution.py:505
  90.6 0.8 collective-permute-start.13
  91.5 1.4 %collective-permute-done.19.refs_6_ = bf16[128,512]{1,0:T(8,128)(2,1)S(1)} collective-permute-done((bf16[128,512]{1,0:T(8,128)(2,1)S(1)}, bf16[128,512]{1,0:T(8,128)(2,1)S(1)}, u32[]{:S(2)}, u32[]{:S(2)}) %collective-permute-start.19) | collective-permute-done | bytes 131104 | tf_op jit(solution)/shard_map/ppermute | solution.py:505
  92.9 13.5 %collective-permute-done.20.refs_7_ = bf16[128,512]{1,0:T(8,128)(2,1)S(1)} collective-permute-done((bf16[128,512]{1,0:T(8,128)(2,1)S(1)}, bf16[128,512]{1,0:T(8,128)(2,1)S(1)}, u32[]{:S(2)}, u32[]{:S(2)}) %collective-permute-start.20) | collective-permute-done | bytes 131104 | tf_op jit(solution)/shard_map/ppermute | solution.py:505
  106.4 4.1 %attention.1 = (f32[8,128,512]{2,1,0:T(8,128)S(1)}, bf16[8,128,512]{2,1,0:T(8,128)(2,1)S(1)}, f32[3,512,128]{2,1,0:T(8,128)S(1)}) custom-call(s32[2]{0:T(128)S(1)} %pad_add_fusion.spot_ref, s32[1]{0:T(128)} %bitcast.2.place_ref, bf16[3,512,512]{2,1,0:T(8,128)(2,1)S(1)} %get-tuple-element.57.w_ref, ...), custom_call_target="tpu_custom_call" | custom-call | flops 24000000 | bytes 1048576 | tf_op jit(solution)/shard_map/attention/pallas_call | solution.py:362
  110.6 0.5 collective-permute-start.22
  111.1 1.8 %collective-permute-done.21.refs_2_ = bf16[3,256,512]{2,1,0:T(8,128)(2,1)S(1)} collective-permute-done((bf16[3,256,512]{2,1,0:T(8,128)(2,1)S(1)}, bf16[3,256,512]{2,1,0:T(8,128)(2,1)S(1)}, u32[]{:S(2)}, u32[]{:S(2)}) %collective-permute-start.21) | collective-permute-done | bytes 786464 | tf_op jit(solution)/shard_map/ppermute | solution.py:558
  112.9 1.1 collective-permute-done.22.refs_3_
  114.0 4.4 %update_and_apply.1 = (bf16[128,512]{1,0:T(8,128)(2,1)S(1)}, bf16[128,512]{1,0:T(8,128)(2,1)S(1)}, bf16[128,512]{1,0:T(8,128)(2,1)S(1)}, bf16[128,512]{1,0:T(8,1...) custom-call(s32[2]{0:T(128)S(1)} %pad_add_fusion.spot_ref, ...), custom_call_target="tpu_custom_call" | custom-call | flops 24000000 | bytes 1048576 | tf_op jit(solution)/shard_map/update_and_apply/pallas_call | solution.py:439
  118.4 0.6 collective-permute-start.23
  119.0 1.1 collective-permute-start.24
  120.1 1.9 %collective-permute-start.25 = (bf16[128,512]{1,0:T(8,128)(2,1)S(1)}, bf16[128,512]{1,0:T(8,128)(2,1)S(1)}, u32[]{:S(2)}, u32[]{:S(2)}) collective-permute-start(bf16[128,512]{1,0:T(8,128)(2,1)S(1)} %get-tuple-element.80), channel_id=1, source_target_pairs={{0,5},{1,4},{4,1},{5,0},{8,13},{9,12},{12,9},{13,8},{2,7},{3,6},{6... | collective-permute-start | bytes 393224 | tf_op jit(solution)/shard_map/ppermute | solution.py:505
  121.9 2.0 %collective-permute-start.27 = (bf16[128,512]{1,0:T(8,128)(2,1)S(1)}, bf16[128,512]{1,0:T(8,128)(2,1)S(1)}, u32[]{:S(2)}, u32[]{:S(2)}) collective-permute-start(bf16[128,512]{1,0:T(8,128)(2,1)S(1)} %get-tuple-element.82), channel_id=1, source_target_pairs={{0,9},{1,8},{4,13},{5,12},{8,1},{9,0},{12,5},{13,4},{2,11},{3,10},... | collective-permute-start | bytes 393224 | tf_op jit(solution)/shard_map/ppermute | solution.py:505
  124.0 0.5 collective-permute-start.28
  124.5 0.7 collective-permute-done.24.refs_2_
  125.2 2.6 %collective-permute-start.29 = (bf16[128,512]{1,0:T(8,128)(2,1)S(1)}, bf16[128,512]{1,0:T(8,128)(2,1)S(1)}, u32[]{:S(2)}, u32[]{:S(2)}) collective-permute-start(bf16[128,512]{1,0:T(8,128)(2,1)S(1)} %get-tuple-element.84), channel_id=1, source_target_pairs={{0,13},{1,12},{4,9},{5,8},{8,5},{9,4},{12,1},{13,0},{2,15},{3,14},... | collective-permute-start | bytes 393224 | tf_op jit(solution)/shard_map/ppermute | solution.py:505
  127.8 1.1 collective-permute-done.25.refs_3_
  128.9 2.1 %collective-permute-done.27.refs_5_ = bf16[128,512]{1,0:T(8,128)(2,1)S(1)} collective-permute-done((bf16[128,512]{1,0:T(8,128)(2,1)S(1)}, bf16[128,512]{1,0:T(8,128)(2,1)S(1)}, u32[]{:S(2)}, u32[]{:S(2)}) %collective-permute-start.27) | collective-permute-done | bytes 131104 | tf_op jit(solution)/shard_map/ppermute | solution.py:505
  131.1 3.1 %collective-permute-done.28.refs_6_ = bf16[128,512]{1,0:T(8,128)(2,1)S(1)} collective-permute-done((bf16[128,512]{1,0:T(8,128)(2,1)S(1)}, bf16[128,512]{1,0:T(8,128)(2,1)S(1)}, u32[]{:S(2)}, u32[]{:S(2)}) %collective-permute-start.28) | collective-permute-done | bytes 131104 | tf_op jit(solution)/shard_map/ppermute | solution.py:505
  134.2 1.3 collective-permute-done.29.refs_7_
  135.6 1.0 unpack_columns.1
  (21 shorter events, 1.0 us)
Async XLA Ops:
  16.3 18.8 %collective-permute-start.7 = (bf16[4,3,32,512]{3,2,1,0:T(8,128)(2,1)S(1)}, bf16[4,3,32,512]{3,2,1,0:T(8,128)(2,1)S(1)}, u32[]{:S(2)}, u32[]{:S(2)}) collective-permute-start(bf16[4,3,32,512]{3,2,1,0:T(8,128)(2,1)S(1)} %all_to_all.5.refs_8_), channel_id=1, source_target_pairs={{0,16},{16,0},{1,17},{17,1},{2,18},{18,2},{3,19},{19,3},{4,20},{20... | collective-permute-start | bytes 1179656 | tf_op jit(solution)/shard_map/ppermute | solution.py:513
  18.9 8.5 %collective-permute-start = (bf16[264,512]{1,0:T(8,128)(2,1)S(1)}, bf16[264,512]{1,0:T(8,128)(2,1)S(1)}, u32[]{:S(2)}, u32[]{:S(2)}) collective-permute-start(bf16[264,512]{1,0:T(8,128)(2,1)S(1)} %get-tuple-element.49), channel_id=1, source_target_pairs={{0,1},{1,0},{4,5},{5,4},{8,9},{9,8},{12,13},{13,12},{2,3},{3,2},{6... | collective-permute-start | bytes 811016 | tf_op jit(solution)/shard_map/ppermute | solution.py:505
  20.5 14.7 %collective-permute-start.1 = (bf16[264,512]{1,0:T(8,128)(2,1)S(1)}, bf16[264,512]{1,0:T(8,128)(2,1)S(1)}, u32[]{:S(2)}, u32[]{:S(2)}) collective-permute-start(bf16[264,512]{1,0:T(8,128)(2,1)S(1)} %get-tuple-element.50), channel_id=1, source_target_pairs={{0,4},{1,5},{4,0},{5,1},{8,12},{9,13},{12,8},{13,9},{2,6},{3,7},{6... | collective-permute-start | bytes 811016 | tf_op jit(solution)/shard_map/ppermute | solution.py:505
  21.4 15.1 %collective-permute-start.2 = (bf16[264,512]{1,0:T(8,128)(2,1)S(1)}, bf16[264,512]{1,0:T(8,128)(2,1)S(1)}, u32[]{:S(2)}, u32[]{:S(2)}) collective-permute-start(bf16[264,512]{1,0:T(8,128)(2,1)S(1)} %get-tuple-element.51), channel_id=1, source_target_pairs={{0,5},{1,4},{4,1},{5,0},{8,13},{9,12},{12,9},{13,8},{2,7},{3,6},{6... | collective-permute-start | bytes 811016 | tf_op jit(solution)/shard_map/ppermute | solution.py:505
  22.4 16.4 %collective-permute-start.3 = (bf16[264,512]{1,0:T(8,128)(2,1)S(1)}, bf16[264,512]{1,0:T(8,128)(2,1)S(1)}, u32[]{:S(2)}, u32[]{:S(2)}) collective-permute-start(bf16[264,512]{1,0:T(8,128)(2,1)S(1)} %get-tuple-element.52), channel_id=1, source_target_pairs={{0,8},{1,9},{4,12},{5,13},{8,0},{9,1},{12,4},{13,5},{2,10},{3,11},... | collective-permute-start | bytes 811016 | tf_op jit(solution)/shard_map/ppermute | solution.py:505
  27.4 29.8 %collective-permute-start.8 = (bf16[4,3,32,512]{3,2,1,0:T(8,128)(2,1)S(1)}, bf16[4,3,32,512]{3,2,1,0:T(8,128)(2,1)S(1)}, u32[]{:S(2)}, u32[]{:S(2)}) collective-permute-start(bf16[4,3,32,512]{3,2,1,0:T(8,128)(2,1)S(1)} %all_to_all.5.refs_8_), channel_id=1, source_target_pairs={{0,2},{2,0},{1,3},{3,1},{4,6},{6,4},{5,7},{7,5},{8,10},{10,8},{9,1... | collective-permute-start | bytes 1179656 | tf_op jit(solution)/shard_map/ppermute | solution.py:514
  35.1 22.1 %collective-permute-start.9 = (bf16[4,3,32,512]{3,2,1,0:T(8,128)(2,1)S(1)}, bf16[4,3,32,512]{3,2,1,0:T(8,128)(2,1)S(1)}, u32[]{:S(2)}, u32[]{:S(2)}) collective-permute-start(bf16[4,3,32,512]{3,2,1,0:T(8,128)(2,1)S(1)} %collective-permute-done.7.refs_9_), channel_id=1, source_target_pairs={{0,2},{2,0},{1,3},{3,1},{4,6},{6,4},{5,7},{7,5},{8,10},{10,8},{9,1... | collective-permute-start | bytes 1179656 | tf_op jit(solution)/shard_map/ppermute | solution.py:515
  35.1 10.3 %collective-permute-start.4 = (bf16[264,512]{1,0:T(8,128)(2,1)S(1)}, bf16[264,512]{1,0:T(8,128)(2,1)S(1)}, u32[]{:S(2)}, u32[]{:S(2)}) collective-permute-start(bf16[264,512]{1,0:T(8,128)(2,1)S(1)} %get-tuple-element.53), channel_id=1, source_target_pairs={{0,9},{1,8},{4,13},{5,12},{8,1},{9,0},{12,5},{13,4},{2,11},{3,10},... | collective-permute-start | bytes 811016 | tf_op jit(solution)/shard_map/ppermute | solution.py:505
  36.5 15.5 %collective-permute-start.5 = (bf16[264,512]{1,0:T(8,128)(2,1)S(1)}, bf16[264,512]{1,0:T(8,128)(2,1)S(1)}, u32[]{:S(2)}, u32[]{:S(2)}) collective-permute-start(bf16[264,512]{1,0:T(8,128)(2,1)S(1)} %get-tuple-element.54), channel_id=1, source_target_pairs={{0,12},{1,13},{4,8},{5,9},{8,4},{9,5},{12,0},{13,1},{2,14},{3,15},... | collective-permute-start | bytes 811016 | tf_op jit(solution)/shard_map/ppermute | solution.py:505
  38.8 18.4 %collective-permute-start.6 = (bf16[264,512]{1,0:T(8,128)(2,1)S(1)}, bf16[264,512]{1,0:T(8,128)(2,1)S(1)}, u32[]{:S(2)}, u32[]{:S(2)}) collective-permute-start(bf16[264,512]{1,0:T(8,128)(2,1)S(1)} %get-tuple-element.55), channel_id=1, source_target_pairs={{0,13},{1,12},{4,9},{5,8},{8,5},{9,4},{12,1},{13,0},{2,15},{3,14},... | collective-permute-start | bytes 811016 | tf_op jit(solution)/shard_map/ppermute | solution.py:505
  62.6 2.4 %collective-permute-start.10 = (bf16[3,256,512]{2,1,0:T(8,128)(2,1)S(1)}, bf16[3,256,512]{2,1,0:T(8,128)(2,1)S(1)}, u32[]{:S(2)}, u32[]{:S(2)}) collective-permute-start(bf16[3,256,512]{2,1,0:T(8,128)(2,1)S(1)} %get-tuple-element.59), channel_id=1, source_target_pairs={{0,2},{2,0},{1,3},{3,1},{4,6},{6,4},{5,7},{7,5},{8,10},{10,8},{9,1... | collective-permute-start | bytes 2359304 | tf_op jit(solution)/shard_map/ppermute | solution.py:526
  65.1 45.5 %collective-permute-start.11 = (bf16[3,256,512]{2,1,0:T(8,128)(2,1)S(1)}, bf16[3,256,512]{2,1,0:T(8,128)(2,1)S(1)}, u32[]{:S(2)}, u32[]{:S(2)}) collective-permute-start(bf16[3,256,512]{2,1,0:T(8,128)(2,1)S(1)} %combine.1.refs_0_), channel_id=1, source_target_pairs={{0,16},{16,0},{1,17},{17,1},{2,18},{18,2},{3,19},{19,3},{4,20},{20... | collective-permute-start | bytes 2359304 | tf_op jit(solution)/shard_map/ppermute | solution.py:540
  66.5 39.9 %collective-permute-start.12 = (bf16[4,128,512]{2,1,0:T(8,128)(2,1)S(1)}, bf16[4,128,512]{2,1,0:T(8,128)(2,1)S(1)}, u32[]{:S(2)}, u32[]{:S(2)}) collective-permute-start(bf16[4,128,512]{2,1,0:T(8,128)(2,1)S(1)} %get-tuple-element.60), channel_id=1, source_target_pairs={{0,2},{2,0},{1,3},{3,1},{4,6},{6,4},{5,7},{7,5},{8,10},{10,8},{9,1... | collective-permute-start | bytes 1572872 | tf_op jit(solution)/shard_map/ppermute | solution.py:544
  67.9 6.0 %collective-permute-start.14 = (bf16[128,512]{1,0:T(8,128)(2,1)S(1)}, bf16[128,512]{1,0:T(8,128)(2,1)S(1)}, u32[]{:S(2)}, u32[]{:S(2)}) collective-permute-start(bf16[128,512]{1,0:T(8,128)(2,1)S(1)} %get-tuple-element.63), channel_id=1, source_target_pairs={{0,1},{1,0},{4,5},{5,4},{8,9},{9,8},{12,13},{13,12},{2,3},{3,2},{6... | collective-permute-start | bytes 393224 | tf_op jit(solution)/shard_map/ppermute | solution.py:505
  68.4 7.1 %collective-permute-start.15 = (bf16[128,512]{1,0:T(8,128)(2,1)S(1)}, bf16[128,512]{1,0:T(8,128)(2,1)S(1)}, u32[]{:S(2)}, u32[]{:S(2)}) collective-permute-start(bf16[128,512]{1,0:T(8,128)(2,1)S(1)} %get-tuple-element.64), channel_id=1, source_target_pairs={{0,4},{1,5},{4,0},{5,1},{8,12},{9,13},{12,8},{13,9},{2,6},{3,7},{6... | collective-permute-start | bytes 393224 | tf_op jit(solution)/shard_map/ppermute | solution.py:505
  69.9 7.9 %collective-permute-start.16 = (bf16[128,512]{1,0:T(8,128)(2,1)S(1)}, bf16[128,512]{1,0:T(8,128)(2,1)S(1)}, u32[]{:S(2)}, u32[]{:S(2)}) collective-permute-start(bf16[128,512]{1,0:T(8,128)(2,1)S(1)} %get-tuple-element.65), channel_id=1, source_target_pairs={{0,5},{1,4},{4,1},{5,0},{8,13},{9,12},{12,9},{13,8},{2,7},{3,6},{6... | collective-permute-start | bytes 393224 | tf_op jit(solution)/shard_map/ppermute | solution.py:505
  73.8 13.4 %collective-permute-start.17 = (bf16[128,512]{1,0:T(8,128)(2,1)S(1)}, bf16[128,512]{1,0:T(8,128)(2,1)S(1)}, u32[]{:S(2)}, u32[]{:S(2)}) collective-permute-start(bf16[128,512]{1,0:T(8,128)(2,1)S(1)} %get-tuple-element.66), channel_id=1, source_target_pairs={{0,8},{1,9},{4,12},{5,13},{8,0},{9,1},{12,4},{13,5},{2,10},{3,11},... | collective-permute-start | bytes 393224 | tf_op jit(solution)/shard_map/ppermute | solution.py:505
  75.5 15.1 %collective-permute-start.18 = (bf16[128,512]{1,0:T(8,128)(2,1)S(1)}, bf16[128,512]{1,0:T(8,128)(2,1)S(1)}, u32[]{:S(2)}, u32[]{:S(2)}) collective-permute-start(bf16[128,512]{1,0:T(8,128)(2,1)S(1)} %get-tuple-element.67), channel_id=1, source_target_pairs={{0,9},{1,8},{4,13},{5,12},{8,1},{9,0},{12,5},{13,4},{2,11},{3,10},... | collective-permute-start | bytes 393224 | tf_op jit(solution)/shard_map/ppermute | solution.py:505
  77.8 15.1 %collective-permute-start.19 = (bf16[128,512]{1,0:T(8,128)(2,1)S(1)}, bf16[128,512]{1,0:T(8,128)(2,1)S(1)}, u32[]{:S(2)}, u32[]{:S(2)}) collective-permute-start(bf16[128,512]{1,0:T(8,128)(2,1)S(1)} %get-tuple-element.68), channel_id=1, source_target_pairs={{0,12},{1,13},{4,8},{5,9},{8,4},{9,5},{12,0},{13,1},{2,14},{3,15},... | collective-permute-start | bytes 393224 | tf_op jit(solution)/shard_map/ppermute | solution.py:505
  87.3 19.1 %collective-permute-start.20 = (bf16[128,512]{1,0:T(8,128)(2,1)S(1)}, bf16[128,512]{1,0:T(8,128)(2,1)S(1)}, u32[]{:S(2)}, u32[]{:S(2)}) collective-permute-start(bf16[128,512]{1,0:T(8,128)(2,1)S(1)} %get-tuple-element.69), channel_id=1, source_target_pairs={{0,13},{1,12},{4,9},{5,8},{8,5},{9,4},{12,1},{13,0},{2,15},{3,14},... | collective-permute-start | bytes 393224 | tf_op jit(solution)/shard_map/ppermute | solution.py:505
  90.6 15.8 %collective-permute-start.13 = (bf16[1,128,512]{2,1,0:T(8,128)(2,1)S(1)}, bf16[1,128,512]{2,1,0:T(8,128)(2,1)S(1)}, u32[]{:S(2)}, u32[]{:S(2)}) collective-permute-start(bf16[1,128,512]{2,1,0:T(8,128)(2,1)S(1)} %get-tuple-element.61), channel_id=1, source_target_pairs={{2,16},{3,17},{6,20},{7,21},{10,24},{11,25},{14,28},{15,29}} | collective-permute-start | bytes 393224 | tf_op jit(solution)/shard_map/ppermute | solution.py:548
  110.5 2.4 %collective-permute-start.21 = (bf16[3,256,512]{2,1,0:T(8,128)(2,1)S(1)}, bf16[3,256,512]{2,1,0:T(8,128)(2,1)S(1)}, u32[]{:S(2)}, u32[]{:S(2)}) collective-permute-start(bf16[3,256,512]{2,1,0:T(8,128)(2,1)S(1)} %combine.1.refs_0_), channel_id=1, source_target_pairs={{0,2},{2,0},{1,3},{3,1},{4,6},{6,4},{5,7},{7,5},{8,10},{10,8},{9,1... | collective-permute-start | bytes 2359304 | tf_op jit(solution)/shard_map/ppermute | solution.py:558
  110.6 3.4 %collective-permute-start.22 = (bf16[3,256,512]{2,1,0:T(8,128)(2,1)S(1)}, bf16[3,256,512]{2,1,0:T(8,128)(2,1)S(1)}, u32[]{:S(2)}, u32[]{:S(2)}) collective-permute-start(bf16[3,256,512]{2,1,0:T(8,128)(2,1)S(1)} %collective-permute-done.11.refs_1_), channel_id=1, source_target_pairs={{0,2},{2,0},{1,3},{3,1},{4,6},{6,4},{5,7},{7,5},{8,10},{10,8},{9,1... | collective-permute-start | bytes 2359304 | tf_op jit(solution)/shard_map/ppermute | solution.py:559
  118.4 5.6 %collective-permute-start.23 = (bf16[128,512]{1,0:T(8,128)(2,1)S(1)}, bf16[128,512]{1,0:T(8,128)(2,1)S(1)}, u32[]{:S(2)}, u32[]{:S(2)}) collective-permute-start(bf16[128,512]{1,0:T(8,128)(2,1)S(1)} %get-tuple-element.78), channel_id=1, source_target_pairs={{0,1},{1,0},{4,5},{5,4},{8,9},{9,8},{12,13},{13,12},{2,3},{3,2},{6... | collective-permute-start | bytes 393224 | tf_op jit(solution)/shard_map/ppermute | solution.py:505
  119.0 6.3 %collective-permute-start.24 = (bf16[128,512]{1,0:T(8,128)(2,1)S(1)}, bf16[128,512]{1,0:T(8,128)(2,1)S(1)}, u32[]{:S(2)}, u32[]{:S(2)}) collective-permute-start(bf16[128,512]{1,0:T(8,128)(2,1)S(1)} %get-tuple-element.79), channel_id=1, source_target_pairs={{0,4},{1,5},{4,0},{5,1},{8,12},{9,13},{12,8},{13,9},{2,6},{3,7},{6... | collective-permute-start | bytes 393224 | tf_op jit(solution)/shard_map/ppermute | solution.py:505
  120.1 8.8 %collective-permute-start.25 = (bf16[128,512]{1,0:T(8,128)(2,1)S(1)}, bf16[128,512]{1,0:T(8,128)(2,1)S(1)}, u32[]{:S(2)}, u32[]{:S(2)}) collective-permute-start(bf16[128,512]{1,0:T(8,128)(2,1)S(1)} %get-tuple-element.80), channel_id=1, source_target_pairs={{0,5},{1,4},{4,1},{5,0},{8,13},{9,12},{12,9},{13,8},{2,7},{3,6},{6... | collective-permute-start | bytes 393224 | tf_op jit(solution)/shard_map/ppermute | solution.py:505
  121.9 7.0 %collective-permute-start.26 = (bf16[128,512]{1,0:T(8,128)(2,1)S(1)}, bf16[128,512]{1,0:T(8,128)(2,1)S(1)}, u32[]{:S(2)}, u32[]{:S(2)}) collective-permute-start(bf16[128,512]{1,0:T(8,128)(2,1)S(1)} %get-tuple-element.81), channel_id=1, source_target_pairs={{0,8},{1,9},{4,12},{5,13},{8,0},{9,1},{12,4},{13,5},{2,10},{3,11},... | collective-permute-start | bytes 393224 | tf_op jit(solution)/shard_map/ppermute | solution.py:505
  121.9 9.1 %collective-permute-start.27 = (bf16[128,512]{1,0:T(8,128)(2,1)S(1)}, bf16[128,512]{1,0:T(8,128)(2,1)S(1)}, u32[]{:S(2)}, u32[]{:S(2)}) collective-permute-start(bf16[128,512]{1,0:T(8,128)(2,1)S(1)} %get-tuple-element.82), channel_id=1, source_target_pairs={{0,9},{1,8},{4,13},{5,12},{8,1},{9,0},{12,5},{13,4},{2,11},{3,10},... | collective-permute-start | bytes 393224 | tf_op jit(solution)/shard_map/ppermute | solution.py:505
  124.0 10.2 %collective-permute-start.28 = (bf16[128,512]{1,0:T(8,128)(2,1)S(1)}, bf16[128,512]{1,0:T(8,128)(2,1)S(1)}, u32[]{:S(2)}, u32[]{:S(2)}) collective-permute-start(bf16[128,512]{1,0:T(8,128)(2,1)S(1)} %get-tuple-element.83), channel_id=1, source_target_pairs={{0,12},{1,13},{4,8},{5,9},{8,4},{9,5},{12,0},{13,1},{2,14},{3,15},... | collective-permute-start | bytes 393224 | tf_op jit(solution)/shard_map/ppermute | solution.py:505
  125.2 10.3 %collective-permute-start.29 = (bf16[128,512]{1,0:T(8,128)(2,1)S(1)}, bf16[128,512]{1,0:T(8,128)(2,1)S(1)}, u32[]{:S(2)}, u32[]{:S(2)}) collective-permute-start(bf16[128,512]{1,0:T(8,128)(2,1)S(1)} %get-tuple-element.84), channel_id=1, source_target_pairs={{0,13},{1,12},{4,9},{5,8},{8,5},{9,4},{12,1},{13,0},{2,15},{3,14},... | collective-permute-start | bytes 393224 | tf_op jit(solution)/shard_map/ppermute | solution.py:505

commit v3 on v2

--- a/solution.py
+++ b/solution.py
@@ -168,11 +168,38 @@
     for (at_a, at_c), ref in zip(spots, piece_refs):
         for l in range(lane):
             first = pl.multiple_of(((at_a * lane + l) * inner + at_c) * piece, piece)
-            for which in range(3):
+            for which in range(ref.shape[1]):
                 out_ref[which, pl.ds(first, piece), :] = ref[l, which]
 
 
-def gradients(spot, place, received, pieces, rows, outer, lane, inner, per_run):
+def split_pieces(own):
+    lane, _, piece, size = own.shape
+
+    def kernel(own_ref, first_ref, last_ref):
+        for l in range(lane):
+            first_ref[l] = own_ref[l, :2]
+            last_ref[l] = own_ref[l, 2:]
+
+    return pl.pallas_call(
+        kernel,
+        in_specs=[VMEM],
+        out_specs=[VMEM] * 2,
+        out_shape=[
+            pltpu.VMEM((lane, 2, piece, size), own.dtype),
+            pltpu.VMEM((lane, 1, piece, size), own.dtype),
+        ],
+        compiler_params=params(),
+        name="split_pieces",
+    )(in_vmem(own))
+
+
+def total_of(left_ref, right_ref, part):
+    return lax.dot_general(
+        left_ref[part], right_ref[...], (((0,), (0,)), ((), ())), preferred_element_type=jnp.float32
+    )
+
+
+def down_gradient(spot, place, received, pieces, rows, outer, lane, inner, per_run):
     blocks = len(received)
     size = received[0].shape[1]
     runs = blocks // per_run
@@ -184,8 +211,8 @@
     def kernel(spot_ref, place_ref, *refs):
         kv_refs, refs = refs[:blocks], refs[blocks:]
         piece_refs, refs = refs[: len(pieces)], refs[len(pieces) :]
-        keep_ref, send_ref, tail_ref, last_ref, w_ref = refs[:5]
-        kn_ref, hid_ref, tgt_ref, gg_ref, ug_ref, all_ref = refs[5:]
+        keep_ref, send_ref, tail_ref, last_ref, w_ref, kn_ref, tgt_ref, gf_ref, uf_ref = refs[:9]
+        hid_ref, all_ref = refs[9:]
         place_pieces(spot_ref, piece_refs, w_ref, outer, lane, inner)
         for g in range(blocks // group):
             here = slice(g * span, (g + 1) * span)
@@ -201,13 +228,9 @@
                 row = kv_refs[b][2 * rows : 2 * rows + 1, :rows].astype(jnp.float32)
                 rates.append(jnp.broadcast_to(row, (rows, rows)).T)
             rate_columns = jnp.concatenate([jnp.concatenate(rates, axis=0)] * (size // rows), axis=1)
-            target = (-rate_columns * values).astype(jnp.bfloat16)
-            tgt_ref[here, :] = target
+            tgt_ref[here, :] = (-rate_columns * values).astype(jnp.bfloat16)
             gate_pre = jnp.dot(key_norm, w_ref[0], preferred_element_type=jnp.float32)
             up_pre = jnp.dot(key_norm, w_ref[1], preferred_element_type=jnp.float32)
-            hidden_grad = lax.dot_general(
-                target, w_ref[2], (((1,), (1,)), ((), ())), preferred_element_type=jnp.float32
-            )
             sigma_gate = jax.nn.sigmoid(gate_pre)
             silu_gate = gate_pre * sigma_gate
             hidden = (silu_gate * up_pre).astype(jnp.bfloat16)
@@ -215,24 +238,11 @@
                 columns = slice(part * half, (part + 1) * half)
                 kn_ref[part, here, :] = key_norm[:, columns]
                 hid_ref[part, here, :] = hidden[:, columns]
-            gg_ref[here, :] = (
-                hidden_grad * up_pre * sigma_gate * (1.0 + gate_pre * (1.0 - sigma_gate))
-            ).astype(jnp.bfloat16)
-            ug_ref[here, :] = (hidden_grad * silu_gate).astype(jnp.bfloat16)
-
-        def total(left_ref, right_ref, part):
-            return lax.dot_general(
-                left_ref[part],
-                right_ref[...],
-                (((0,), (0,)), ((), ())),
-                preferred_element_type=jnp.float32,
-            )
-
+            gf_ref[here, :] = up_pre * sigma_gate * (1.0 + gate_pre * (1.0 - sigma_gate))
+            uf_ref[here, :] = silu_gate
         own = spot_ref[1]
-        pairs = ((kn_ref, gg_ref), (kn_ref, ug_ref), (hid_ref, tgt_ref))
-        for which, (left_ref, right_ref) in enumerate(pairs):
-            send_ref[which] = total(left_ref, right_ref, inner - 1 - own).astype(jnp.bfloat16)
-            keep_ref[which] = total(left_ref, right_ref, own)
+        send_ref[0] = total_of(hid_ref, tgt_ref, inner - 1 - own).astype(jnp.bfloat16)
+        keep_ref[0] = total_of(hid_ref, tgt_ref, own)
         for step, ref in enumerate(kv_refs):
             block = place_ref[0] ^ step
             for which in range(2):
@@ -245,26 +255,70 @@
     return pl.pallas_call(
         kernel,
         in_specs=[SMEM] * 2 + [VMEM] * (blocks + len(pieces)),
-        out_specs=[VMEM] * 5,
+        out_specs=[VMEM] * 9,
         out_shape=[
-            pltpu.VMEM((3, half, size), jnp.float32),
-            pltpu.VMEM((3, half, size), jnp.bfloat16),
+            pltpu.VMEM((1, half, size), jnp.float32),
+            pltpu.VMEM((1, half, size), jnp.bfloat16),
             pltpu.VMEM((runs, 2 * WINDOW, size), jnp.bfloat16),
             pltpu.VMEM((1, 2 * WINDOW, size), jnp.bfloat16),
-            pltpu.VMEM((3, size, size), jnp.bfloat16),
+            pltpu.VMEM((2, size, size), jnp.bfloat16),
+            pltpu.VMEM((inner, count, half), jnp.bfloat16),
+            pltpu.VMEM((count, size), jnp.bfloat16),
+            pltpu.VMEM((count, size), jnp.float32),
+            pltpu.VMEM((count, size), jnp.float32),
         ],
         scratch_shapes=[
             pltpu.VMEM((inner, count, half), jnp.bfloat16),
-            pltpu.VMEM((inner, count, half), jnp.bfloat16),
-            pltpu.VMEM((count, size), jnp.bfloat16),
-            pltpu.VMEM((count, size), jnp.bfloat16),
-            pltpu.VMEM((count, size), jnp.bfloat16),
             pltpu.VMEM((blocks, 2 * WINDOW, size), jnp.bfloat16),
         ],
-        compiler_params=params(20),
-        cost_estimate=cost(6),
-        name="gradients",
+        compiler_params=params(14),
+        cost_estimate=cost(4),
+        name="down_gradient",
     )(spot, place, *[in_vmem(r) for r in received], *[in_vmem(p) for p in pieces])
+
+
+def other_gradients(spot, pieces, key_norm, target, gate_factor, up_factor, outer, lane):
+    inner, count, half = key_norm.shape
+    size = target.shape[1]
+    span = count // 4
+
+    def kernel(spot_ref, *refs):
+        piece_refs, refs = refs[: len(pieces)], refs[len(pieces) :]
+        kn_ref, tgt_ref, gf_ref, uf_ref, keep_ref, send_ref, w_ref, gg_ref, ug_ref = refs
+        place_pieces(spot_ref, piece_refs, w_ref, outer, lane, inner)
+        for first in range(0, count, span):
+            here = slice(first, first + span)
+            hidden_grad = lax.dot_general(
+                tgt_ref[here, :],
+                w_ref[0],
+                (((1,), (1,)), ((), ())),
+                preferred_element_type=jnp.float32,
+            )
+            gg_ref[here, :] = (hidden_grad * gf_ref[here, :]).astype(jnp.bfloat16)
+            ug_ref[here, :] = (hidden_grad * uf_ref[here, :]).astype(jnp.bfloat16)
+        own = spot_ref[1]
+        for which, right_ref in enumerate((gg_ref, ug_ref)):
+            send_ref[which] = total_of(kn_ref, right_ref, inner - 1 - own).astype(jnp.bfloat16)
+            keep_ref[which] = total_of(kn_ref, right_ref, own)
+
+    return pl.pallas_call(
+        kernel,
+        in_specs=[SMEM] + [VMEM] * (len(pieces) + 4),
+        out_specs=[VMEM] * 3,
+        out_shape=[
+            pltpu.VMEM((2, half, size), jnp.float32),
+            pltpu.VMEM((2, half, size), jnp.bfloat16),
+            pltpu.VMEM((1, size, size), jnp.bfloat16),
+        ],
+        scratch_shapes=[pltpu.VMEM((count, size), jnp.bfloat16)] * 2,
+        compiler_params=params(10),
+        cost_estimate=cost(3),
+        name="other_gradients",
+    )(
+        spot,
+        *[in_vmem(p) for p in pieces],
+        *[in_vmem(x) for x in (key_norm, target, gate_factor, up_factor)],
+    )
 
 
 def combine(keep, got):
@@ -281,12 +335,12 @@
     )(in_vmem(keep), in_vmem(got))
 
 
-def attention(spot, place, queries, received, around, from_outer, old, per_run):
+def attention(spot, place, queries, received, around, from_outer, old_first, old_last, per_run):
     blocks = len(queries)
     rows, width = queries[0].shape
     span = 2 * WINDOW
 
-    def kernel(spot_ref, place_ref, w_ref, around_ref, outer_ref, *refs):
+    def kernel(spot_ref, place_ref, w_ref, w_last_ref, around_ref, outer_ref, *refs):
         q_refs, kv_refs, refs = refs[:blocks], refs[blocks : 2 * blocks], refs[2 * blocks :]
         att_ref, qn_ref, norm_ref, kv_ref, q_ref = refs
         for step in range(blocks):
@@ -294,7 +348,8 @@
             q_ref[place_ref[0] ^ step] = q_refs[step][...]
         for which in range(3):
             for first in range(0, width, HEAD_DIM):
-                previous = w_ref[which, first : first + HEAD_DIM, :].astype(jnp.float32)
+                source, index = (w_ref, which) if which < 2 else (w_last_ref, 0)
+                previous = source[index, first : first + HEAD_DIM, :].astype(jnp.float32)
                 norm = jnp.sqrt(jnp.mean(previous * previous, axis=1, keepdims=True))
                 norm_ref[which, first : first + HEAD_DIM, :] = jnp.broadcast_to(
                     norm, (HEAD_DIM, HEAD_DIM)
@@ -361,7 +416,7 @@
 
     return pl.pallas_call(
         kernel,
-        in_specs=[SMEM] * 2 + [VMEM] * (3 + 2 * blocks),
+        in_specs=[SMEM] * 2 + [VMEM] * (4 + 2 * blocks),
         out_specs=[VMEM] * 3,
         out_shape=[
             pltpu.VMEM((blocks, rows, width), jnp.float32),
@@ -378,7 +433,8 @@
     )(
         spot,
         place,
-        in_vmem(old),
+        in_vmem(old_first),
+        in_vmem(old_last),
         in_vmem(around),
         in_vmem(from_outer),
         *[in_vmem(q) for q in queries],
@@ -386,21 +442,23 @@
     )
 
 
-def update_and_apply(spot, place, old, norms, sums, query_norm, attended):
+def update_and_apply(spot, place, old_first, old_last, norms, first, last, query_norm, attended):
+    sums = first + last
     blocks, rows, size = query_norm.shape
-    halves = len(sums) // 2
+    halves = len(first) // 2
     half = size // halves
     group = 2 if blocks % 2 == 0 else 1
 
-    def kernel(spot_ref, place_ref, w_ref, norm_ref, *refs):
-        sum_refs, refs = refs[: 2 * halves], refs[2 * halves :]
+    def kernel(spot_ref, place_ref, w_ref, w_last_ref, norm_ref, *refs):
+        sum_refs, refs = refs[: len(sums)], refs[len(sums) :]
         q_ref, a_ref, out_refs, (total_ref, new_ref) = refs[0], refs[1], refs[2:-2], refs[-2:]
         squares = jnp.zeros((8, size), jnp.float32)
         for part in range(halves):
             place = spot_ref[1] if part == 0 else halves - 1 - spot_ref[1]
             for which in range(3):
-                total = sum_refs[2 * part][which].astype(jnp.float32) + sum_refs[2 * part + 1][
-                    which
+                begin, index = (2 * part, which) if which < 2 else (2 * halves + 2 * part, 0)
+                total = sum_refs[begin][index].astype(jnp.float32) + sum_refs[begin + 1][
+                    index
                 ].astype(jnp.float32)
                 total_ref[place, which] = total
                 squares = squares + jnp.sum(
@@ -413,7 +471,8 @@
         for part in range(halves):
             for which in range(3):
                 here = slice(part * half, (part + 1) * half)
-                previous = w_ref[which, here, :].astype(jnp.float32)
+                source, index = (w_ref, which) if which < 2 else (w_last_ref, 0)
+                previous = source[index, here, :].astype(jnp.float32)
                 stepped = previous - scale * total_ref[part, which]
                 factor = norm_ref[which, here, 0:1] * lax.rsqrt(
                     jnp.mean(stepped * stepped, axis=1, keepdims=True) + NORM_EPS
@@ -438,7 +497,7 @@
 
     return pl.pallas_call(
         kernel,
-        in_specs=[SMEM] * 2 + [VMEM] * (len(sums) + 4),
+        in_specs=[SMEM] * 2 + [VMEM] * (len(sums) + 5),
         out_specs=[VMEM] * blocks,
         out_shape=[pltpu.VMEM((rows, size), jnp.bfloat16)] * blocks,
         scratch_shapes=[
@@ -451,7 +510,8 @@
     )(
         spot,
         place,
-        in_vmem(old),
+        in_vmem(old_first),
+        in_vmem(old_last),
         in_vmem(norms),
         *[in_vmem(s) for s in sums],
         in_vmem(query_norm),
@@ -510,27 +570,25 @@
         qs = exchange(qs)
 
         if outer == 2 and inner == 2:
-            other = lax.ppermute(own, "outer", swap_pairs(outer, 1))
-            own_beside = lax.ppermute(own, "inner", swap_pairs(inner, 1))
-            other_beside = lax.ppermute(other, "inner", swap_pairs(inner, 1))
-            pieces = [own, other, own_beside, other_beside]
+            first_pieces, last_pieces = ([part] for part in split_pieces(own))
+            for pieces in (first_pieces, last_pieces):
+                pieces.append(lax.ppermute(pieces[0], "outer", swap_pairs(outer, 1)))
+                pieces.append(lax.ppermute(pieces[0], "inner", swap_pairs(inner, 1)))
+                pieces.append(lax.ppermute(pieces[1], "inner", swap_pairs(inner, 1)))
         else:
             old = gather_rows(own[None], "outer", outer, a, 0)[:, :, None]
             old = gather_rows(old, "inner", inner, c, 2)
-            pieces = [jnp.transpose(old, (3, 0, 1, 2, 4, 5)).reshape(3, size, size)]
-
-        keep, send, tails, last, old = gradients(
-            spot, place, kv, pieces, rows, outer, lane, inner, head_axis
-        )
-        if inner > 1:
-            got = lax.ppermute(send, "inner", swap_pairs(inner, 1))
-            half = combine(keep, got)
-        else:
+            old = jnp.transpose(old, (3, 0, 1, 2, 4, 5)).reshape(3, size, size)
+            first_pieces, last_pieces = [old[:2]], [old[2:]]
+
+        def begin_sum(keep, send):
             half = keep.astype(jnp.bfloat16)
-        mine, theirs = half, jnp.zeros_like(half)
-        if outer & (outer - 1):
-            mine = lax.psum(half, "outer")
-        else:
+            if inner > 1:
+                got = lax.ppermute(send, "inner", swap_pairs(inner, 1))
+                half = combine(keep, got)
+            mine, theirs = half, jnp.zeros_like(half)
+            if outer & (outer - 1):
+                return lax.psum(half, "outer"), theirs
             stride = 1
             while stride < outer:
                 if stride > 1:
@@ -539,6 +597,17 @@
                     )
                 theirs = lax.ppermute(mine, "outer", swap_pairs(outer, stride))
                 stride *= 2
+            return mine, theirs
+
+        def share(value):
+            return lax.ppermute(value, "inner", swap_pairs(inner, 1))
+
+        keep, send, tails, last, old_first, *rest = down_gradient(
+            spot, place, kv, first_pieces, rows, outer, lane, inner, head_axis
+        )
+        last_sums = list(begin_sum(keep, send))
+        keep, send, old_last = other_gradients(spot, last_pieces, *rest, outer, lane)
+        first_sums = list(begin_sum(keep, send))
         around = tails
         if inner > 1:
             around = lax.ppermute(tails, "inner", [(i, (i + 1) % inner) for i in range(inner)])
@@ -546,19 +615,18 @@
             (i * inner + inner - 1, (i + 1) * inner) for i in range(outer - 1)
         ]
         from_outer = lax.ppermute(last, ("outer", "inner"), pairs) if pairs else last
-        attended, query_norm, norms = attention(
-            spot, place, qs, kv, around, from_outer, old, head_axis
+        attended, query_norm, norms = attention(spot, place, qs, kv, around, from_outer, old_first, old_last, head_axis)
+
+        first_sums[1], attended, query_norm, norms = lax.optimization_barrier(
+            (first_sums[1], attended, query_norm, norms)
         )
-
-        theirs, attended, query_norm, norms = lax.optimization_barrier(
-            (theirs, attended, query_norm, norms)
+        if inner > 1:
+            last_sums += [share(last_sums[0]), share(last_sums[1])]
+            first_sums += [share(first_sums[0]), share(first_sums[1])]
+
+        out = update_and_apply(
+            spot, place, old_first, old_last, norms, first_sums, last_sums, query_norm, attended
         )
-        sums = [mine, theirs]
-        if inner > 1:
-            sums.append(lax.ppermute(mine, "inner", swap_pairs(inner, 1)))
-            sums.append(lax.ppermute(theirs, "inner", swap_pairs(inner, 1)))
-
-        out = update_and_apply(spot, place, old, norms, sums, query_norm, attended)
         return unpack_columns(place, exchange(out), lane, head_axis)
 
     return shards

time: 137 us -> 132 us (0.964)
  starting transfers between devices: 35.7 us -> 57.6 us
  waiting for transfers between devices: 68.1 us -> 53.1 us
  blocking collectives: 12.4 us -> 0 us
    ppermute x7 -> x14, starting transfers between devices: 4.66 us -> 19.1 us  [the longest x2 10.5 us: begin_sum(): theirs = lax.ppermute(mine, 'outer', swap_pairs(outer, stride))]
    all_to_all x1 -> x0, blocking collectives: 12.4 us -> none  [shards(): own = lax.all_to_all(own, 'lane', split_axis=0, concat_axis=0, tiled=True)]
    ppermute x21, waiting for transfers between devices: 55.2 us -> 43.4 us  [exchange(): got.append(lax.ppermute(chunks[step], group, swap_pairs(HEADS, step)))]
    all_to_all x0 -> x1, starting transfers between devices: none -> 5.26 us  [shards(): own = lax.all_to_all(own, 'lane', split_axis=0, concat_axis=0, tiled=True)]
    ppermute x7 -> x14, waiting for transfers between devices: 12.9 us -> 8.12 us  [the longest x2 4.72 us: begin_sum(): theirs = lax.ppermute(mine, 'outer', swap_pairs(outer, stride))]
    ppermute x21, starting transfers between devices: 30.2 us -> 32.2 us  [exchange(): got.append(lax.ppermute(chunks[step], group, swap_pairs(HEADS, step)))]
    all_to_all x0 -> x1, waiting for transfers between devices: none -> 1.51 us  [shards(): own = lax.all_to_all(own, 'lane', split_axis=0, concat_axis=0, tiled=True)]
    pallas_call x3 -> x5, Pallas kernels: 13.8 us -> 14.2 us  [the longest x1 4.31 us: update_and_apply(): pl.pallas_call(kernel, in_specs=[SMEM] * 2 + [VMEM] * (len(sums) + 5), ou...]
  transfers between devices with their start and end apart: 30 -> 38, of which waited for: 19 -> 18; matrix products, arithmetic and copies ran while one was open for 0% -> 0% of each run, Pallas kernels for 4% -> 7%
where the time goes in v3:
time: 132 us
  starting transfers between devices  57.6 us (44%)
  waiting for transfers between devices  53.1 us (40%)
  Pallas kernels  20.8 us (16%)
    ppermute x21, waiting for transfers between devices, exchange(): got.append(lax.ppermute(chunks[step], group, swap_pairs(HEADS, step)))  43.4 us
    ppermute x21, starting transfers between devices, exchange(): got.append(lax.ppermute(chunks[step], group, swap_pairs(HEADS, step)))  32.2 us
    ppermute x2, starting transfers between devices, begin_sum(): theirs = lax.ppermute(mine, 'outer', swap_pairs(outer, stride))  10.5 us
    all_to_all x1, starting transfers between devices, shards(): own = lax.all_to_all(own, 'lane', split_axis=0, concat_axis=0, tiled=True)  5.26 us
    ppermute x2, waiting for transfers between devices, begin_sum(): theirs = lax.ppermute(mine, 'outer', swap_pairs(outer, stride))  4.72 us
    pallas_call x1, Pallas kernels, update_and_apply(): pl.pallas_call(kernel, in_specs=[SMEM] * 2 + [VMEM] * (len(sums) + 5), ou...  4.31 us
    ppermute x2, starting transfers between devices, shards(): pieces.append(lax.ppermute(pieces[0], 'outer', swap_pairs(outer, 1)))  4.28 us
    pallas_call x1, Pallas kernels, pack(): pl.pallas_call(kernel, in_specs=[SMEM, ANY, ANY, VMEM, ANY, ANY, ANY], ou...  4.08 us
  transfers between devices with their start and end apart: 38, of which 18 were waited for; matrix products, arithmetic and copies ran while one was open for 0% of the time, Pallas kernels for 7%

profile of v3, /device:TPU:0, one launch (start us, length us, event | category | flops | bytes accessed | tf_op | source)
XLA Modules:
  0.0 131.9 jit_solution(9832000665966353064)
XLA Ops:
  0.1 4.1 %pack.1 = (bf16[4,3,32,512]{3,2,1,0:T(8,128)(2,1)}, bf16[264,512]{1,0:T(8,128)(2,1)S(1)}, bf16[264,512]{1,0:T(8,128)(2,1)}, bf16[264,512]{1,0:T(8,128)(2,1)}, bf...) custom-call(s32[1]{0:T(128)} %bitcast.2.place_ref, ...), custom_call_target="tpu_custom_call" | custom-call | tf_op jit(solution)/shard_map/pack/pallas_call | solution.py:95
  4.2 5.3 %all-to-all-start = ((bf16[4,3,32,512]{3,2,1,0:T(8,128)(2,1)}), bf16[4,3,32,512]{3,2,1,0:T(8,128)(2,1)S(1)}, u32[]{:S(2)}, u32[]{:S(2)}) async-start(bf16[4,3,32,512]{3,2,1,0:T(8,128)(2,1)} %get-tuple-element.65), calls=%async_computation | async-start | bytes 786432 | tf_op jit(solution)/shard_map/all_to_all | solution.py:560
  9.4 1.5 %collective-permute-start = (bf16[264,512]{1,0:T(8,128)(2,1)}, bf16[264,512]{1,0:T(8,128)(2,1)S(1)}, u32[]{:S(2)}, u32[]{:S(2)}) collective-permute-start(bf16[264,512]{1,0:T(8,128)(2,1)} %get-tuple-element.58), channel_id=1, source_target_pairs={{0,1},{1,0},{4,5},{5,4},{8,9},{9,8},{12,13},{13,12},{2,3},{3,2},{6... | collective-permute-start | bytes 811016 | tf_op jit(solution)/shard_map/ppermute | solution.py:565
  10.9 2.0 %collective-permute-start.1 = (bf16[264,512]{1,0:T(8,128)(2,1)}, bf16[264,512]{1,0:T(8,128)(2,1)S(1)}, u32[]{:S(2)}, u32[]{:S(2)}) collective-permute-start(bf16[264,512]{1,0:T(8,128)(2,1)} %get-tuple-element.59), channel_id=1, source_target_pairs={{0,4},{1,5},{4,0},{5,1},{8,12},{9,13},{12,8},{13,9},{2,6},{3,7},{6... | collective-permute-start | bytes 811016 | tf_op jit(solution)/shard_map/ppermute | solution.py:565
  13.0 2.0 %collective-permute-start.3 = (bf16[264,512]{1,0:T(8,128)(2,1)S(1)}, bf16[264,512]{1,0:T(8,128)(2,1)S(1)}, u32[]{:S(2)}, u32[]{:S(2)}) collective-permute-start(bf16[264,512]{1,0:T(8,128)(2,1)S(1)} %get-tuple-element.61), channel_id=1, source_target_pairs={{0,8},{1,9},{4,12},{5,13},{8,0},{9,1},{12,4},{13,5},{2,10},{3,11},... | collective-permute-start | bytes 811016 | tf_op jit(solution)/shard_map/ppermute | solution.py:565
  14.9 1.0 collective-permute-start.4
  15.9 1.5 %all-to-all-done.own_ref = bf16[4,3,32,512]{3,2,1,0:T(8,128)(2,1)S(1)} async-done(((bf16[4,3,32,512]{3,2,1,0:T(8,128)(2,1)}), bf16[4,3,32,512]{3,2,1,0:T(8,128)(2,1)S(1)}, u32[]{:S(2)}, u32[]{:S(2)}) %all-to-all-start) | async-done | bytes 393248 | tf_op jit(solution)/shard_map/all_to_all | solution.py:560
  17.6 2.6 %collective-permute-start.7 = (bf16[4,2,32,512]{3,2,1,0:T(8,128)(2,1)S(1)}, bf16[4,2,32,512]{3,2,1,0:T(8,128)(2,1)S(1)}, u32[]{:S(2)}, u32[]{:S(2)}) collective-permute-start(bf16[4,2,32,512]{3,2,1,0:T(8,128)(2,1)S(1)} %get-tuple-element.66.refs_8_), channel_id=1, source_target_pairs={{0,16},{16,0},{1,17},{17,1},{2,18},{18,2},{3,19},{19,3},{4,20},{20... | collective-permute-start | bytes 786440 | tf_op jit(solution)/shard_map/ppermute | solution.py:575
  20.2 2.6 %collective-permute-done.1.refs_2_.refs_10_ = bf16[264,512]{1,0:T(8,128)(2,1)S(1)} collective-permute-done((bf16[264,512]{1,0:T(8,128)(2,1)}, bf16[264,512]{1,0:T(8,128)(2,1)S(1)}, u32[]{:S(2)}, u32[]{:S(2)}) %collective-permute-start.1) | collective-permute-done | bytes 270368 | tf_op jit(solution)/shard_map/ppermute | solution.py:565
  22.8 0.7 collective-permute-start.5
  23.4 6.0 %collective-permute-done.2.refs_3_.refs_11_ = bf16[264,512]{1,0:T(8,128)(2,1)S(1)} collective-permute-done((bf16[264,512]{1,0:T(8,128)(2,1)S(1)}, bf16[264,512]{1,0:T(8,128)(2,1)S(1)}, u32[]{:S(2)}, u32[]{:S(2)}) %collective-permute-start.2) | collective-permute-done | bytes 270368 | tf_op jit(solution)/shard_map/ppermute | solution.py:565
  29.4 4.9 %collective-permute-start.6 = (bf16[264,512]{1,0:T(8,128)(2,1)S(1)}, bf16[264,512]{1,0:T(8,128)(2,1)S(1)}, u32[]{:S(2)}, u32[]{:S(2)}) collective-permute-start(bf16[264,512]{1,0:T(8,128)(2,1)S(1)} %get-tuple-element.64), channel_id=1, source_target_pairs={{0,13},{1,12},{4,9},{5,8},{8,5},{9,4},{12,1},{13,0},{2,15},{3,14},... | collective-permute-start | bytes 811016 | tf_op jit(solution)/shard_map/ppermute | solution.py:565
  34.9 0.8 collective-permute-done.4.refs_5_.refs_13_
  35.6 1.6 %collective-permute-start.10 = (bf16[4,1,32,512]{3,2,1,0:T(8,128)(2,1)S(1)}, bf16[4,1,32,512]{3,2,1,0:T(8,128)(2,1)S(1)}, u32[]{:S(2)}, u32[]{:S(2)}) collective-permute-start(bf16[4,1,32,512]{3,2,1,0:T(8,128)(2,1)S(1)} %get-tuple-element.68.refs_0_), channel_id=1, source_target_pairs={{0,16},{16,0},{1,17},{17,1},{2,18},{18,2},{3,19},{19,3},{4,20},{20... | collective-permute-start | bytes 393224 | tf_op jit(solution)/shard_map/ppermute | solution.py:575
  37.3 6.8 %collective-permute-done.5.refs_6_.refs_14_ = bf16[264,512]{1,0:T(8,128)(2,1)S(1)} collective-permute-done((bf16[264,512]{1,0:T(8,128)(2,1)S(1)}, bf16[264,512]{1,0:T(8,128)(2,1)S(1)}, u32[]{:S(2)}, u32[]{:S(2)}) %collective-permute-start.5) | collective-permute-done | bytes 270368 | tf_op jit(solution)/shard_map/ppermute | solution.py:565
  44.1 2.0 %collective-permute-done.10.refs_1_ = bf16[4,1,32,512]{3,2,1,0:T(8,128)(2,1)S(1)} collective-permute-done((bf16[4,1,32,512]{3,2,1,0:T(8,128)(2,1)S(1)}, bf16[4,1,32,512]{3,2,1,0:T(8,128)(2,1)S(1)}, u32[]{:S(2)}, u32[]{:S(2)}) %collective-permute-start.10) | collective-permute-done | bytes 131104 | tf_op jit(solution)/shard_map/ppermute | solution.py:575
  46.1 3.4 %collective-permute-done.6.refs_7_.refs_15_ = bf16[264,512]{1,0:T(8,128)(2,1)S(1)} collective-permute-done((bf16[264,512]{1,0:T(8,128)(2,1)S(1)}, bf16[264,512]{1,0:T(8,128)(2,1)S(1)}, u32[]{:S(2)}, u32[]{:S(2)}) %collective-permute-start.6) | collective-permute-done | bytes 270368 | tf_op jit(solution)/shard_map/ppermute | solution.py:565
  49.5 3.4 %down_gradient.1 = (f32[1,256,512]{2,1,0:T(8,128)S(1)}, bf16[1,256,512]{2,1,0:T(8,128)(2,1)S(1)}, bf16[4,128,512]{2,1,0:T(8,128)(2,1)S(1)}, bf16[1,128,512]{2,1,...) custom-call(s32[2]{0:T(128)S(1)} %pad_add_fusion.spot_ref, ...), custom_call_target="tpu_custom_call" | custom-call | flops 16000000 | bytes 1048576 | tf_op jit(solution)/shard_map/down_gradient/pallas_call | solution.py:255
  52.9 2.4 %other_gradients.1 = (f32[2,256,512]{2,1,0:T(8,128)S(1)}, bf16[2,256,512]{2,1,0:T(8,128)(2,1)S(1)}, bf16[1,512,512]{2,1,0:T(8,128)(2,1)S(1)}) custom-call(s32[2]{0:T(128)S(1)} %pad_add_fusion.spot_ref, bf16[4,1,32,512]{3,2,1,0:T(8,128)(2,1)S(1)} %get-tuple-element.68.refs_0_, bf16[4,1,32,512]{3,2,1,0:T(8,128)(2,1)S(1)} %collective-permute-done.10.refs_1_, ...), custom_call_target="tpu_custom_call" | custom-call | flops 12000000 | bytes 1048576 | tf_op jit(solution)/shard_map/other_gradients/pallas_call | solution.py:304
  55.4 1.4 %pack_queries.1 = (bf16[128,512]{1,0:T(8,128)(2,1)S(1)}, bf16[128,512]{1,0:T(8,128)(2,1)S(1)}, bf16[128,512]{1,0:T(8,128)(2,1)S(1)}, bf16[128,512]{1,0:T(8,128)(...) custom-call(s32[1]{0:T(128)} %bitcast.2.place_ref, ...), custom_call_target="tpu_custom_call" | custom-call | tf_op jit(solution)/shard_map/pack_queries/pallas_call | solution.py:124
  57.7 3.9 %collective-permute-start.14 = (bf16[2,256,512]{2,1,0:T(8,128)(2,1)S(1)}, bf16[2,256,512]{2,1,0:T(8,128)(2,1)S(1)}, u32[]{:S(2)}, u32[]{:S(2)}) collective-permute-start(bf16[2,256,512]{2,1,0:T(8,128)(2,1)S(1)} %combine.2.refs_0_), channel_id=1, source_target_pairs={{0,16},{16,0},{1,17},{17,1},{2,18},{18,2},{3,19},{19,3},{4,20},{20... | collective-permute-start | bytes 1572872 | tf_op jit(solution)/shard_map/ppermute | solution.py:598
  61.7 2.8 %collective-permute-start.19 = (bf16[128,512]{1,0:T(8,128)(2,1)S(1)}, bf16[128,512]{1,0:T(8,128)(2,1)S(1)}, u32[]{:S(2)}, u32[]{:S(2)}) collective-permute-start(bf16[128,512]{1,0:T(8,128)(2,1)S(1)} %get-tuple-element.81), channel_id=1, source_target_pairs={{0,5},{1,4},{4,1},{5,0},{8,13},{9,12},{12,9},{13,8},{2,7},{3,6},{6... | collective-permute-start | bytes 393224 | tf_op jit(solution)/shard_map/ppermute | solution.py:565
  64.5 3.4 %collective-permute-done.18.refs_2_ = bf16[128,512]{1,0:T(8,128)(2,1)S(1)} collective-permute-done((bf16[128,512]{1,0:T(8,128)(2,1)S(1)}, bf16[128,512]{1,0:T(8,128)(2,1)S(1)}, u32[]{:S(2)}, u32[]{:S(2)}) %collective-permute-start.18) | collective-permute-done | bytes 131104 | tf_op jit(solution)/shard_map/ppermute | solution.py:565
  68.5 2.3 %collective-permute-done.19.refs_3_ = bf16[128,512]{1,0:T(8,128)(2,1)S(1)} collective-permute-done((bf16[128,512]{1,0:T(8,128)(2,1)S(1)}, bf16[128,512]{1,0:T(8,128)(2,1)S(1)}, u32[]{:S(2)}, u32[]{:S(2)}) %collective-permute-start.19) | collective-permute-done | bytes 131104 | tf_op jit(solution)/shard_map/ppermute | solution.py:565
  70.8 1.1 collective-permute-start.21
  71.9 4.9 %collective-permute-done.20.refs_4_ = bf16[128,512]{1,0:T(8,128)(2,1)S(1)} collective-permute-done((bf16[128,512]{1,0:T(8,128)(2,1)S(1)}, bf16[128,512]{1,0:T(8,128)(2,1)S(1)}, u32[]{:S(2)}, u32[]{:S(2)}) %collective-permute-start.20) | collective-permute-done | bytes 131104 | tf_op jit(solution)/shard_map/ppermute | solution.py:565
  76.8 2.0 %collective-permute-start.22 = (bf16[128,512]{1,0:T(8,128)(2,1)S(1)}, bf16[128,512]{1,0:T(8,128)(2,1)S(1)}, u32[]{:S(2)}, u32[]{:S(2)}) collective-permute-start(bf16[128,512]{1,0:T(8,128)(2,1)S(1)} %get-tuple-element.84), channel_id=1, source_target_pairs={{0,12},{1,13},{4,8},{5,9},{8,4},{9,5},{12,0},{13,1},{2,14},{3,15},... | collective-permute-start | bytes 393224 | tf_op jit(solution)/shard_map/ppermute | solution.py:565
  78.8 0.8 collective-permute-done.21.refs_5_
  79.6 2.4 %collective-permute-start.23 = (bf16[128,512]{1,0:T(8,128)(2,1)S(1)}, bf16[128,512]{1,0:T(8,128)(2,1)S(1)}, u32[]{:S(2)}, u32[]{:S(2)}) collective-permute-start(bf16[128,512]{1,0:T(8,128)(2,1)S(1)} %get-tuple-element.85), channel_id=1, source_target_pairs={{0,13},{1,12},{4,9},{5,8},{8,5},{9,4},{12,1},{13,0},{2,15},{3,14},... | collective-permute-start | bytes 393224 | tf_op jit(solution)/shard_map/ppermute | solution.py:565
  82.0 0.8 collective-permute-start.16
  82.9 4.9 %collective-permute-done.22.refs_6_ = bf16[128,512]{1,0:T(8,128)(2,1)S(1)} collective-permute-done((bf16[128,512]{1,0:T(8,128)(2,1)S(1)}, bf16[128,512]{1,0:T(8,128)(2,1)S(1)}, u32[]{:S(2)}, u32[]{:S(2)}) %collective-permute-start.22) | collective-permute-done | bytes 131104 | tf_op jit(solution)/shard_map/ppermute | solution.py:565
  87.8 6.6 %collective-permute-start.27 = (bf16[1,256,512]{2,1,0:T(8,128)(2,1)S(1)}, bf16[1,256,512]{2,1,0:T(8,128)(2,1)S(1)}, u32[]{:S(2)}, u32[]{:S(2)}) collective-permute-start(bf16[1,256,512]{2,1,0:T(8,128)(2,1)S(1)} %combine.3.refs_4_), channel_id=1, source_target_pairs={{0,16},{16,0},{1,17},{17,1},{2,18},{18,2},{3,19},{19,3},{4,20},{20... | collective-permute-start | bytes 786440 | tf_op jit(solution)/shard_map/ppermute | solution.py:598
  94.4 0.8 collective-permute-start.24
  95.2 4.1 %attention.1 = (f32[8,128,512]{2,1,0:T(8,128)S(1)}, bf16[8,128,512]{2,1,0:T(8,128)(2,1)S(1)}, f32[3,512,128]{2,1,0:T(8,128)S(1)}) custom-call(s32[2]{0:T(128)S(1)} %pad_add_fusion.spot_ref, s32[1]{0:T(128)} %bitcast.2.place_ref, bf16[2,512,512]{2,1,0:T(8,128)(2,1)S(1)} %get-tuple-element.67.w_ref, bf16[1,512,512]{2,1,0:T(8,128)(2,1)S(1)} %get-tuple-element.73.w_last_ref, ...), custom_call_target="tpu_custom_call" | custom-call | flops 24000000 | bytes 1048576 | tf_op jit(solution)/shard_map/attention/pallas_call | solution.py:417
  99.3 2.7 %collective-permute-start.25 = (bf16[2,256,512]{2,1,0:T(8,128)(2,1)S(1)}, bf16[2,256,512]{2,1,0:T(8,128)(2,1)S(1)}, u32[]{:S(2)}, u32[]{:S(2)}) collective-permute-start(bf16[2,256,512]{2,1,0:T(8,128)(2,1)S(1)} %collective-permute-done.14.refs_1_), channel_id=1, source_target_pairs={{0,2},{2,0},{1,3},{3,1},{4,6},{6,4},{5,7},{7,5},{8,10},{10,8},{9,1... | collective-permute-start | bytes 1572872 | tf_op jit(solution)/shard_map/ppermute | solution.py:603
  102.1 4.7 %collective-permute-done.27.refs_5_ = bf16[1,256,512]{2,1,0:T(8,128)(2,1)S(1)} collective-permute-done((bf16[1,256,512]{2,1,0:T(8,128)(2,1)S(1)}, bf16[1,256,512]{2,1,0:T(8,128)(2,1)S(1)}, u32[]{:S(2)}, u32[]{:S(2)}) %collective-permute-start.27) | collective-permute-done | bytes 262176 | tf_op jit(solution)/shard_map/ppermute | solution.py:598
  107.0 1.4 %collective-permute-done.29.refs_7_ = bf16[1,256,512]{2,1,0:T(8,128)(2,1)S(1)} collective-permute-done((bf16[1,256,512]{2,1,0:T(8,128)(2,1)S(1)}, bf16[1,256,512]{2,1,0:T(8,128)(2,1)S(1)}, u32[]{:S(2)}, u32[]{:S(2)}) %collective-permute-start.29) | collective-permute-done | bytes 262176 | tf_op jit(solution)/shard_map/ppermute | solution.py:603
  108.4 4.3 %update_and_apply.1 = (bf16[128,512]{1,0:T(8,128)(2,1)S(1)}, bf16[128,512]{1,0:T(8,128)(2,1)S(1)}, bf16[128,512]{1,0:T(8,128)(2,1)S(1)}, bf16[128,512]{1,0:T(8,1...) custom-call(s32[2]{0:T(128)S(1)} %pad_add_fusion.spot_ref, ...), custom_call_target="tpu_custom_call" | custom-call | flops 24000000 | bytes 1048576 | tf_op jit(solution)/shard_map/update_and_apply/pallas_call | solution.py:498
  112.7 1.3 collective-permute-start.30
  114.0 2.3 %collective-permute-start.32 = (bf16[128,512]{1,0:T(8,128)(2,1)S(1)}, bf16[128,512]{1,0:T(8,128)(2,1)S(1)}, u32[]{:S(2)}, u32[]{:S(2)}) collective-permute-start(bf16[128,512]{1,0:T(8,128)(2,1)S(1)} %get-tuple-element.98), channel_id=1, source_target_pairs={{0,5},{1,4},{4,1},{5,0},{8,13},{9,12},{12,9},{13,8},{2,7},{3,6},{6... | collective-permute-start | bytes 393224 | tf_op jit(solution)/shard_map/ppermute | solution.py:565
  116.2 1.6 %collective-permute-start.33 = (bf16[128,512]{1,0:T(8,128)(2,1)S(1)}, bf16[128,512]{1,0:T(8,128)(2,1)S(1)}, u32[]{:S(2)}, u32[]{:S(2)}) collective-permute-start(bf16[128,512]{1,0:T(8,128)(2,1)S(1)} %get-tuple-element.99), channel_id=1, source_target_pairs={{0,8},{1,9},{4,12},{5,13},{8,0},{9,1},{12,4},{13,5},{2,10},{3,11},... | collective-permute-start | bytes 393224 | tf_op jit(solution)/shard_map/ppermute | solution.py:565
  117.9 1.1 collective-permute-start.34
  118.9 2.3 %collective-permute-start.35 = (bf16[128,512]{1,0:T(8,128)(2,1)S(1)}, bf16[128,512]{1,0:T(8,128)(2,1)S(1)}, u32[]{:S(2)}, u32[]{:S(2)}) collective-permute-start(bf16[128,512]{1,0:T(8,128)(2,1)S(1)} %get-tuple-element.101), channel_id=1, source_target_pairs={{0,12},{1,13},{4,8},{5,9},{8,4},{9,5},{12,0},{13,1},{2,14},{3,15},... | collective-permute-start | bytes 393224 | tf_op jit(solution)/shard_map/ppermute | solution.py:565
  121.2 2.1 %collective-permute-start.36 = (bf16[128,512]{1,0:T(8,128)(2,1)S(1)}, bf16[128,512]{1,0:T(8,128)(2,1)S(1)}, u32[]{:S(2)}, u32[]{:S(2)}) collective-permute-start(bf16[128,512]{1,0:T(8,128)(2,1)S(1)} %get-tuple-element.102), channel_id=1, source_target_pairs={{0,13},{1,12},{4,9},{5,8},{8,5},{9,4},{12,1},{13,0},{2,15},{3,14},... | collective-permute-start | bytes 393224 | tf_op jit(solution)/shard_map/ppermute | solution.py:565
  123.3 2.8 %collective-permute-done.34.refs_5_ = bf16[128,512]{1,0:T(8,128)(2,1)S(1)} collective-permute-done((bf16[128,512]{1,0:T(8,128)(2,1)S(1)}, bf16[128,512]{1,0:T(8,128)(2,1)S(1)}, u32[]{:S(2)}, u32[]{:S(2)}) %collective-permute-start.34) | collective-permute-done | bytes 131104 | tf_op jit(solution)/shard_map/ppermute | solution.py:565
  126.1 2.8 %collective-permute-done.35.refs_6_ = bf16[128,512]{1,0:T(8,128)(2,1)S(1)} collective-permute-done((bf16[128,512]{1,0:T(8,128)(2,1)S(1)}, bf16[128,512]{1,0:T(8,128)(2,1)S(1)}, u32[]{:S(2)}, u32[]{:S(2)}) %collective-permute-start.35) | collective-permute-done | bytes 131104 | tf_op jit(solution)/shard_map/ppermute | solution.py:565
  128.9 1.8 %collective-permute-done.36.refs_7_ = bf16[128,512]{1,0:T(8,128)(2,1)S(1)} collective-permute-done((bf16[128,512]{1,0:T(8,128)(2,1)S(1)}, bf16[128,512]{1,0:T(8,128)(2,1)S(1)}, u32[]{:S(2)}, u32[]{:S(2)}) %collective-permute-start.36) | collective-permute-done | bytes 131104 | tf_op jit(solution)/shard_map/ppermute | solution.py:565
  130.7 1.0 unpack_columns.1
  (39 shorter events, 2.6 us)
Async XLA Ops:
  4.2 13.2 %all-to-all-start = ((bf16[4,3,32,512]{3,2,1,0:T(8,128)(2,1)}), bf16[4,3,32,512]{3,2,1,0:T(8,128)(2,1)S(1)}, u32[]{:S(2)}, u32[]{:S(2)}) async-start(bf16[4,3,32,512]{3,2,1,0:T(8,128)(2,1)} %get-tuple-element.65), calls=%async_computation | async-start | bytes 786432 | tf_op jit(solution)/shard_map/all_to_all | solution.py:560
  9.4 8.2 %collective-permute-start = (bf16[264,512]{1,0:T(8,128)(2,1)}, bf16[264,512]{1,0:T(8,128)(2,1)S(1)}, u32[]{:S(2)}, u32[]{:S(2)}) collective-permute-start(bf16[264,512]{1,0:T(8,128)(2,1)} %get-tuple-element.58), channel_id=1, source_target_pairs={{0,1},{1,0},{4,5},{5,4},{8,9},{9,8},{12,13},{13,12},{2,3},{3,2},{6... | collective-permute-start | bytes 811016 | tf_op jit(solution)/shard_map/ppermute | solution.py:565
  10.9 11.8 %collective-permute-start.1 = (bf16[264,512]{1,0:T(8,128)(2,1)}, bf16[264,512]{1,0:T(8,128)(2,1)S(1)}, u32[]{:S(2)}, u32[]{:S(2)}) collective-permute-start(bf16[264,512]{1,0:T(8,128)(2,1)} %get-tuple-element.59), channel_id=1, source_target_pairs={{0,4},{1,5},{4,0},{5,1},{8,12},{9,13},{12,8},{13,9},{2,6},{3,7},{6... | collective-permute-start | bytes 811016 | tf_op jit(solution)/shard_map/ppermute | solution.py:565
  13.0 16.4 %collective-permute-start.2 = (bf16[264,512]{1,0:T(8,128)(2,1)S(1)}, bf16[264,512]{1,0:T(8,128)(2,1)S(1)}, u32[]{:S(2)}, u32[]{:S(2)}) collective-permute-start(bf16[264,512]{1,0:T(8,128)(2,1)S(1)} %get-tuple-element.60), channel_id=1, source_target_pairs={{0,5},{1,4},{4,1},{5,0},{8,13},{9,12},{12,9},{13,8},{2,7},{3,6},{6... | collective-permute-start | bytes 811016 | tf_op jit(solution)/shard_map/ppermute | solution.py:565
  13.0 21.4 %collective-permute-start.3 = (bf16[264,512]{1,0:T(8,128)(2,1)S(1)}, bf16[264,512]{1,0:T(8,128)(2,1)S(1)}, u32[]{:S(2)}, u32[]{:S(2)}) collective-permute-start(bf16[264,512]{1,0:T(8,128)(2,1)S(1)} %get-tuple-element.61), channel_id=1, source_target_pairs={{0,8},{1,9},{4,12},{5,13},{8,0},{9,1},{12,4},{13,5},{2,10},{3,11},... | collective-permute-start | bytes 811016 | tf_op jit(solution)/shard_map/ppermute | solution.py:565
  14.9 20.7 %collective-permute-start.4 = (bf16[264,512]{1,0:T(8,128)(2,1)S(1)}, bf16[264,512]{1,0:T(8,128)(2,1)S(1)}, u32[]{:S(2)}, u32[]{:S(2)}) collective-permute-start(bf16[264,512]{1,0:T(8,128)(2,1)S(1)} %get-tuple-element.62), channel_id=1, source_target_pairs={{0,9},{1,8},{4,13},{5,12},{8,1},{9,0},{12,5},{13,4},{2,11},{3,10},... | collective-permute-start | bytes 811016 | tf_op jit(solution)/shard_map/ppermute | solution.py:565
  17.6 16.8 %collective-permute-start.7 = (bf16[4,2,32,512]{3,2,1,0:T(8,128)(2,1)S(1)}, bf16[4,2,32,512]{3,2,1,0:T(8,128)(2,1)S(1)}, u32[]{:S(2)}, u32[]{:S(2)}) collective-permute-start(bf16[4,2,32,512]{3,2,1,0:T(8,128)(2,1)S(1)} %get-tuple-element.66.refs_8_), channel_id=1, source_target_pairs={{0,16},{16,0},{1,17},{17,1},{2,18},{18,2},{3,19},{19,3},{4,20},{20... | collective-permute-start | bytes 786440 | tf_op jit(solution)/shard_map/ppermute | solution.py:575
  22.8 21.3 %collective-permute-start.5 = (bf16[264,512]{1,0:T(8,128)(2,1)S(1)}, bf16[264,512]{1,0:T(8,128)(2,1)S(1)}, u32[]{:S(2)}, u32[]{:S(2)}) collective-permute-start(bf16[264,512]{1,0:T(8,128)(2,1)S(1)} %get-tuple-element.63), channel_id=1, source_target_pairs={{0,12},{1,13},{4,8},{5,9},{8,4},{9,5},{12,0},{13,1},{2,14},{3,15},... | collective-permute-start | bytes 811016 | tf_op jit(solution)/shard_map/ppermute | solution.py:565
  29.4 20.1 %collective-permute-start.6 = (bf16[264,512]{1,0:T(8,128)(2,1)S(1)}, bf16[264,512]{1,0:T(8,128)(2,1)S(1)}, u32[]{:S(2)}, u32[]{:S(2)}) collective-permute-start(bf16[264,512]{1,0:T(8,128)(2,1)S(1)} %get-tuple-element.64), channel_id=1, source_target_pairs={{0,13},{1,12},{4,9},{5,8},{8,5},{9,4},{12,1},{13,0},{2,15},{3,14},... | collective-permute-start | bytes 811016 | tf_op jit(solution)/shard_map/ppermute | solution.py:565
  34.3 15.2 %collective-permute-start.8 = (bf16[4,2,32,512]{3,2,1,0:T(8,128)(2,1)S(1)}, bf16[4,2,32,512]{3,2,1,0:T(8,128)(2,1)S(1)}, u32[]{:S(2)}, u32[]{:S(2)}) collective-permute-start(bf16[4,2,32,512]{3,2,1,0:T(8,128)(2,1)S(1)} %get-tuple-element.66.refs_8_), channel_id=1, source_target_pairs={{0,2},{2,0},{1,3},{3,1},{4,6},{6,4},{5,7},{7,5},{8,10},{10,8},{9,1... | collective-permute-start | bytes 786440 | tf_op jit(solution)/shard_map/ppermute | solution.py:576
  34.3 15.1 %collective-permute-start.9 = (bf16[4,2,32,512]{3,2,1,0:T(8,128)(2,1)S(1)}, bf16[4,2,32,512]{3,2,1,0:T(8,128)(2,1)S(1)}, u32[]{:S(2)}, u32[]{:S(2)}) collective-permute-start(bf16[4,2,32,512]{3,2,1,0:T(8,128)(2,1)S(1)} %collective-permute-done.7.refs_9_), channel_id=1, source_target_pairs={{0,2},{2,0},{1,3},{3,1},{4,6},{6,4},{5,7},{7,5},{8,10},{10,8},{9,1... | collective-permute-start | bytes 786440 | tf_op jit(solution)/shard_map/ppermute | solution.py:577
  35.6 10.4 %collective-permute-start.10 = (bf16[4,1,32,512]{3,2,1,0:T(8,128)(2,1)S(1)}, bf16[4,1,32,512]{3,2,1,0:T(8,128)(2,1)S(1)}, u32[]{:S(2)}, u32[]{:S(2)}) collective-permute-start(bf16[4,1,32,512]{3,2,1,0:T(8,128)(2,1)S(1)} %get-tuple-element.68.refs_0_), channel_id=1, source_target_pairs={{0,16},{16,0},{1,17},{17,1},{2,18},{18,2},{3,19},{19,3},{4,20},{20... | collective-permute-start | bytes 393224 | tf_op jit(solution)/shard_map/ppermute | solution.py:575
  44.1 8.8 %collective-permute-start.11 = (bf16[4,1,32,512]{3,2,1,0:T(8,128)(2,1)S(1)}, bf16[4,1,32,512]{3,2,1,0:T(8,128)(2,1)S(1)}, u32[]{:S(2)}, u32[]{:S(2)}) collective-permute-start(bf16[4,1,32,512]{3,2,1,0:T(8,128)(2,1)S(1)} %get-tuple-element.68.refs_0_), channel_id=1, source_target_pairs={{0,2},{2,0},{1,3},{3,1},{4,6},{6,4},{5,7},{7,5},{8,10},{10,8},{9,1... | collective-permute-start | bytes 393224 | tf_op jit(solution)/shard_map/ppermute | solution.py:576
  46.1 6.8 %collective-permute-start.12 = (bf16[4,1,32,512]{3,2,1,0:T(8,128)(2,1)S(1)}, bf16[4,1,32,512]{3,2,1,0:T(8,128)(2,1)S(1)}, u32[]{:S(2)}, u32[]{:S(2)}) collective-permute-start(bf16[4,1,32,512]{3,2,1,0:T(8,128)(2,1)S(1)} %collective-permute-done.10.refs_1_), channel_id=1, source_target_pairs={{0,2},{2,0},{1,3},{3,1},{4,6},{6,4},{5,7},{7,5},{8,10},{10,8},{9,1... | collective-permute-start | bytes 393224 | tf_op jit(solution)/shard_map/ppermute | solution.py:577
  55.3 2.2 %collective-permute-start.13 = (bf16[2,256,512]{2,1,0:T(8,128)(2,1)S(1)}, bf16[2,256,512]{2,1,0:T(8,128)(2,1)S(1)}, u32[]{:S(2)}, u32[]{:S(2)}) collective-permute-start(bf16[2,256,512]{2,1,0:T(8,128)(2,1)S(1)} %get-tuple-element.75), channel_id=1, source_target_pairs={{0,2},{2,0},{1,3},{3,1},{4,6},{6,4},{5,7},{7,5},{8,10},{10,8},{9,1... | collective-permute-start | bytes 1572872 | tf_op jit(solution)/shard_map/ppermute | solution.py:587
  56.8 7.7 %collective-permute-start.17 = (bf16[128,512]{1,0:T(8,128)(2,1)S(1)}, bf16[128,512]{1,0:T(8,128)(2,1)S(1)}, u32[]{:S(2)}, u32[]{:S(2)}) collective-permute-start(bf16[128,512]{1,0:T(8,128)(2,1)S(1)} %get-tuple-element.79), channel_id=1, source_target_pairs={{0,1},{1,0},{4,5},{5,4},{8,9},{9,8},{12,13},{13,12},{2,3},{3,2},{6... | collective-permute-start | bytes 393224 | tf_op jit(solution)/shard_map/ppermute | solution.py:565
  57.4 37.9 %collective-permute-start.15 = (bf16[4,128,512]{2,1,0:T(8,128)(2,1)S(1)}, bf16[4,128,512]{2,1,0:T(8,128)(2,1)S(1)}, u32[]{:S(2)}, u32[]{:S(2)}) collective-permute-start(bf16[4,128,512]{2,1,0:T(8,128)(2,1)S(1)} %get-tuple-element.76), channel_id=1, source_target_pairs={{0,2},{2,0},{1,3},{3,1},{4,6},{6,4},{5,7},{7,5},{8,10},{10,8},{9,1... | collective-permute-start | bytes 1572872 | tf_op jit(solution)/shard_map/ppermute | solution.py:613
  57.7 41.7 %collective-permute-start.14 = (bf16[2,256,512]{2,1,0:T(8,128)(2,1)S(1)}, bf16[2,256,512]{2,1,0:T(8,128)(2,1)S(1)}, u32[]{:S(2)}, u32[]{:S(2)}) collective-permute-start(bf16[2,256,512]{2,1,0:T(8,128)(2,1)S(1)} %combine.2.refs_0_), channel_id=1, source_target_pairs={{0,16},{16,0},{1,17},{17,1},{2,18},{18,2},{3,19},{19,3},{4,20},{20... | collective-permute-start | bytes 1572872 | tf_op jit(solution)/shard_map/ppermute | solution.py:598
  61.6 6.4 %collective-permute-start.18 = (bf16[128,512]{1,0:T(8,128)(2,1)S(1)}, bf16[128,512]{1,0:T(8,128)(2,1)S(1)}, u32[]{:S(2)}, u32[]{:S(2)}) collective-permute-start(bf16[128,512]{1,0:T(8,128)(2,1)S(1)} %get-tuple-element.80), channel_id=1, source_target_pairs={{0,4},{1,5},{4,0},{5,1},{8,12},{9,13},{12,8},{13,9},{2,6},{3,7},{6... | collective-permute-start | bytes 393224 | tf_op jit(solution)/shard_map/ppermute | solution.py:565
  61.7 9.1 %collective-permute-start.19 = (bf16[128,512]{1,0:T(8,128)(2,1)S(1)}, bf16[128,512]{1,0:T(8,128)(2,1)S(1)}, u32[]{:S(2)}, u32[]{:S(2)}) collective-permute-start(bf16[128,512]{1,0:T(8,128)(2,1)S(1)} %get-tuple-element.81), channel_id=1, source_target_pairs={{0,5},{1,4},{4,1},{5,0},{8,13},{9,12},{12,9},{13,8},{2,7},{3,6},{6... | collective-permute-start | bytes 393224 | tf_op jit(solution)/shard_map/ppermute | solution.py:565
  64.5 17.4 %collective-permute-start.26 = (bf16[1,256,512]{2,1,0:T(8,128)(2,1)S(1)}, bf16[1,256,512]{2,1,0:T(8,128)(2,1)S(1)}, u32[]{:S(2)}, u32[]{:S(2)}) collective-permute-start(bf16[1,256,512]{2,1,0:T(8,128)(2,1)S(1)} %get-tuple-element.92), channel_id=1, source_target_pairs={{0,2},{2,0},{1,3},{3,1},{4,6},{6,4},{5,7},{7,5},{8,10},{10,8},{9,1... | collective-permute-start | bytes 786440 | tf_op jit(solution)/shard_map/ppermute | solution.py:587
  68.0 8.8 %collective-permute-start.20 = (bf16[128,512]{1,0:T(8,128)(2,1)S(1)}, bf16[128,512]{1,0:T(8,128)(2,1)S(1)}, u32[]{:S(2)}, u32[]{:S(2)}) collective-permute-start(bf16[128,512]{1,0:T(8,128)(2,1)S(1)} %get-tuple-element.82), channel_id=1, source_target_pairs={{0,8},{1,9},{4,12},{5,13},{8,0},{9,1},{12,4},{13,5},{2,10},{3,11},... | collective-permute-start | bytes 393224 | tf_op jit(solution)/shard_map/ppermute | solution.py:565
  70.8 8.8 %collective-permute-start.21 = (bf16[128,512]{1,0:T(8,128)(2,1)S(1)}, bf16[128,512]{1,0:T(8,128)(2,1)S(1)}, u32[]{:S(2)}, u32[]{:S(2)}) collective-permute-start(bf16[128,512]{1,0:T(8,128)(2,1)S(1)} %get-tuple-element.83), channel_id=1, source_target_pairs={{0,9},{1,8},{4,13},{5,12},{8,1},{9,0},{12,5},{13,4},{2,11},{3,10},... | collective-permute-start | bytes 393224 | tf_op jit(solution)/shard_map/ppermute | solution.py:565
  76.8 11.0 %collective-permute-start.22 = (bf16[128,512]{1,0:T(8,128)(2,1)S(1)}, bf16[128,512]{1,0:T(8,128)(2,1)S(1)}, u32[]{:S(2)}, u32[]{:S(2)}) collective-permute-start(bf16[128,512]{1,0:T(8,128)(2,1)S(1)} %get-tuple-element.84), channel_id=1, source_target_pairs={{0,12},{1,13},{4,8},{5,9},{8,4},{9,5},{12,0},{13,1},{2,14},{3,15},... | collective-permute-start | bytes 393224 | tf_op jit(solution)/shard_map/ppermute | solution.py:565
  79.6 14.8 %collective-permute-start.23 = (bf16[128,512]{1,0:T(8,128)(2,1)S(1)}, bf16[128,512]{1,0:T(8,128)(2,1)S(1)}, u32[]{:S(2)}, u32[]{:S(2)}) collective-permute-start(bf16[128,512]{1,0:T(8,128)(2,1)S(1)} %get-tuple-element.85), channel_id=1, source_target_pairs={{0,13},{1,12},{4,9},{5,8},{8,5},{9,4},{12,1},{13,0},{2,15},{3,14},... | collective-permute-start | bytes 393224 | tf_op jit(solution)/shard_map/ppermute | solution.py:565
  82.0 13.3 %collective-permute-start.16 = (bf16[1,128,512]{2,1,0:T(8,128)(2,1)S(1)}, bf16[1,128,512]{2,1,0:T(8,128)(2,1)S(1)}, u32[]{:S(2)}, u32[]{:S(2)}) collective-permute-start(bf16[1,128,512]{2,1,0:T(8,128)(2,1)S(1)} %get-tuple-element.77), channel_id=1, source_target_pairs={{2,16},{3,17},{6,20},{7,21},{10,24},{11,25},{14,28},{15,29}} | collective-permute-start | bytes 393224 | tf_op jit(solution)/shard_map/ppermute | solution.py:617
  87.8 19.0 %collective-permute-start.27 = (bf16[1,256,512]{2,1,0:T(8,128)(2,1)S(1)}, bf16[1,256,512]{2,1,0:T(8,128)(2,1)S(1)}, u32[]{:S(2)}, u32[]{:S(2)}) collective-permute-start(bf16[1,256,512]{2,1,0:T(8,128)(2,1)S(1)} %combine.3.refs_4_), channel_id=1, source_target_pairs={{0,16},{16,0},{1,17},{17,1},{2,18},{18,2},{3,19},{19,3},{4,20},{20... | collective-permute-start | bytes 786440 | tf_op jit(solution)/shard_map/ppermute | solution.py:598
  94.4 14.0 %collective-permute-start.24 = (bf16[2,256,512]{2,1,0:T(8,128)(2,1)S(1)}, bf16[2,256,512]{2,1,0:T(8,128)(2,1)S(1)}, u32[]{:S(2)}, u32[]{:S(2)}) collective-permute-start(bf16[2,256,512]{2,1,0:T(8,128)(2,1)S(1)} %combine.2.refs_0_), channel_id=1, source_target_pairs={{0,2},{2,0},{1,3},{3,1},{4,6},{6,4},{5,7},{7,5},{8,10},{10,8},{9,1... | collective-permute-start | bytes 1572872 | tf_op jit(solution)/shard_map/ppermute | solution.py:603
  99.3 9.0 %collective-permute-start.25 = (bf16[2,256,512]{2,1,0:T(8,128)(2,1)S(1)}, bf16[2,256,512]{2,1,0:T(8,128)(2,1)S(1)}, u32[]{:S(2)}, u32[]{:S(2)}) collective-permute-start(bf16[2,256,512]{2,1,0:T(8,128)(2,1)S(1)} %collective-permute-done.14.refs_1_), channel_id=1, source_target_pairs={{0,2},{2,0},{1,3},{3,1},{4,6},{6,4},{5,7},{7,5},{8,10},{10,8},{9,1... | collective-permute-start | bytes 1572872 | tf_op jit(solution)/shard_map/ppermute | solution.py:603
  102.0 4.9 %collective-permute-start.28 = (bf16[1,256,512]{2,1,0:T(8,128)(2,1)S(1)}, bf16[1,256,512]{2,1,0:T(8,128)(2,1)S(1)}, u32[]{:S(2)}, u32[]{:S(2)}) collective-permute-start(bf16[1,256,512]{2,1,0:T(8,128)(2,1)S(1)} %combine.3.refs_4_), channel_id=1, source_target_pairs={{0,2},{2,0},{1,3},{3,1},{4,6},{6,4},{5,7},{7,5},{8,10},{10,8},{9,1... | collective-permute-start | bytes 786440 | tf_op jit(solution)/shard_map/ppermute | solution.py:603
  106.8 1.5 %collective-permute-start.29 = (bf16[1,256,512]{2,1,0:T(8,128)(2,1)S(1)}, bf16[1,256,512]{2,1,0:T(8,128)(2,1)S(1)}, u32[]{:S(2)}, u32[]{:S(2)}) collective-permute-start(bf16[1,256,512]{2,1,0:T(8,128)(2,1)S(1)} %collective-permute-done.27.refs_5_), channel_id=1, source_target_pairs={{0,2},{2,0},{1,3},{3,1},{4,6},{6,4},{5,7},{7,5},{8,10},{10,8},{9,1... | collective-permute-start | bytes 786440 | tf_op jit(solution)/shard_map/ppermute | solution.py:603
  112.7 6.2 %collective-permute-start.30 = (bf16[128,512]{1,0:T(8,128)(2,1)S(1)}, bf16[128,512]{1,0:T(8,128)(2,1)S(1)}, u32[]{:S(2)}, u32[]{:S(2)}) collective-permute-start(bf16[128,512]{1,0:T(8,128)(2,1)S(1)} %get-tuple-element.96), channel_id=1, source_target_pairs={{0,1},{1,0},{4,5},{5,4},{8,9},{9,8},{12,13},{13,12},{2,3},{3,2},{6... | collective-permute-start | bytes 393224 | tf_op jit(solution)/shard_map/ppermute | solution.py:565
  114.0 7.2 %collective-permute-start.31 = (bf16[128,512]{1,0:T(8,128)(2,1)S(1)}, bf16[128,512]{1,0:T(8,128)(2,1)S(1)}, u32[]{:S(2)}, u32[]{:S(2)}) collective-permute-start(bf16[128,512]{1,0:T(8,128)(2,1)S(1)} %get-tuple-element.97), channel_id=1, source_target_pairs={{0,4},{1,5},{4,0},{5,1},{8,12},{9,13},{12,8},{13,9},{2,6},{3,7},{6... | collective-permute-start | bytes 393224 | tf_op jit(solution)/shard_map/ppermute | solution.py:565
  114.0 9.3 %collective-permute-start.32 = (bf16[128,512]{1,0:T(8,128)(2,1)S(1)}, bf16[128,512]{1,0:T(8,128)(2,1)S(1)}, u32[]{:S(2)}, u32[]{:S(2)}) collective-permute-start(bf16[128,512]{1,0:T(8,128)(2,1)S(1)} %get-tuple-element.98), channel_id=1, source_target_pairs={{0,5},{1,4},{4,1},{5,0},{8,13},{9,12},{12,9},{13,8},{2,7},{3,6},{6... | collective-permute-start | bytes 393224 | tf_op jit(solution)/shard_map/ppermute | solution.py:565
  116.2 7.0 %collective-permute-start.33 = (bf16[128,512]{1,0:T(8,128)(2,1)S(1)}, bf16[128,512]{1,0:T(8,128)(2,1)S(1)}, u32[]{:S(2)}, u32[]{:S(2)}) collective-permute-start(bf16[128,512]{1,0:T(8,128)(2,1)S(1)} %get-tuple-element.99), channel_id=1, source_target_pairs={{0,8},{1,9},{4,12},{5,13},{8,0},{9,1},{12,4},{13,5},{2,10},{3,11},... | collective-permute-start | bytes 393224 | tf_op jit(solution)/shard_map/ppermute | solution.py:565
  117.9 8.2 %collective-permute-start.34 = (bf16[128,512]{1,0:T(8,128)(2,1)S(1)}, bf16[128,512]{1,0:T(8,128)(2,1)S(1)}, u32[]{:S(2)}, u32[]{:S(2)}) collective-permute-start(bf16[128,512]{1,0:T(8,128)(2,1)S(1)} %get-tuple-element.100), channel_id=1, source_target_pairs={{0,9},{1,8},{4,13},{5,12},{8,1},{9,0},{12,5},{13,4},{2,11},{3,10},... | collective-permute-start | bytes 393224 | tf_op jit(solution)/shard_map/ppermute | solution.py:565
  118.9 10.0 %collective-permute-start.35 = (bf16[128,512]{1,0:T(8,128)(2,1)S(1)}, bf16[128,512]{1,0:T(8,128)(2,1)S(1)}, u32[]{:S(2)}, u32[]{:S(2)}) collective-permute-start(bf16[128,512]{1,0:T(8,128)(2,1)S(1)} %get-tuple-element.101), channel_id=1, source_target_pairs={{0,12},{1,13},{4,8},{5,9},{8,4},{9,5},{12,0},{13,1},{2,14},{3,15},... | collective-permute-start | bytes 393224 | tf_op jit(solution)/shard_map/ppermute | solution.py:565
  121.2 9.5 %collective-permute-start.36 = (bf16[128,512]{1,0:T(8,128)(2,1)S(1)}, bf16[128,512]{1,0:T(8,128)(2,1)S(1)}, u32[]{:S(2)}, u32[]{:S(2)}) collective-permute-start(bf16[128,512]{1,0:T(8,128)(2,1)S(1)} %get-tuple-element.102), channel_id=1, source_target_pairs={{0,13},{1,12},{4,9},{5,8},{8,5},{9,4},{12,1},{13,0},{2,15},{3,14},... | collective-permute-start | bytes 393224 | tf_op jit(solution)/shard_map/ppermute | solution.py:565
